TPU v7x, 32 devices: a whole 2x2x4 slice. The times are simulated.
32 devices in a mesh: groups: 2 (over x), seq: 16 (over z, y, core).
Axes of the slice: x: 2, y: 2, z: 4, core: 2. Of those that a mesh axis runs over, the one named last changes fastest.
Arguments:
- query_block: bfloat16 [512, 4096], P(('groups', 'seq')), parts along dimension 0, may hold values from -112 to 112
- cache_keys: bfloat16 [8192, 2048], P(('groups', 'seq')), parts along dimension 0, may hold values from -4 to 4
- stored_values: bfloat16 [8192, 2048], P(('groups', 'seq')), parts along dimension 0, may hold values from -6 to 6
- live_counts: int32 [32], P(('groups', 'seq')), parts along dimension 0, may hold values from 128 to 256
- first_position: int32 [2], P('groups'), parts along dimension 0, may hold values from 0 to 3840
- out_weight: bfloat16 [4096, 5376], P('seq'), may hold values from -0.09375 to 0.09375
Outputs:
- attended: bfloat16 [512, 5376], P(('groups', 'seq')), parts along dimension 0
There are 2 independent parts, one for each index of `groups`. A program takes and returns all parts, laid end to end along the dimension named above; an argument that names none is the same for every part. Nothing has to cross between parts.
Inputs may be any that keep to these rules, and one draw needn't show every extreme that they name: `live_counts`: the live slots of a block are its first ones.
All inputs are finite; a program needn't handle non-finite values.
Results may differ from a plain program's by a relative error of at most 0.0058.
Values may be sent and summed in bfloat16 or wider, within the bound.
No kernel may reach another device: no remote copies, remote signals or barrier semaphores. Data moves between devices by JAX's collectives and lax.ppermute only.
A program may use at most 64 MiB of HBM per device.

v0:
```python
import functools

import jax
import jax.numpy as jnp
from jax import lax
from jax.experimental import pallas as pl
from jax.experimental.pallas import tpu as pltpu
from jax.sharding import PartitionSpec as P


QUERY_HEADS = 32
KEY_VALUE_HEADS = 16
HEAD_SIZE = 128
INNER = 4
CHUNKS = 3

score_scale = 168.0 ** (-0.5)
masked_value = -1e30
log2e = 1.4426950408889634
ln2 = 0.6931471805599453


bf16 = jnp.bfloat16
f32 = jnp.float32
VM = pltpu.MemorySpace.VMEM
SM = pltpu.MemorySpace.SMEM


def vspec():
    return pl.BlockSpec(memory_space=VM)


def sspec():
    return pl.BlockSpec(memory_space=SM)


def place():
    me = lax.axis_index("seq")
    return me, lax.shift_right_logical(me, 2), lax.bitwise_and(me, 3)


def call(kernel, ins, outs, scratch=(), scalars=0, flops=0):
    in_specs = [sspec()] * scalars + [vspec()] * (len(ins) - scalars)
    moved = sum(a.size * a.dtype.itemsize for a in list(ins) + list(outs))
    return pl.pallas_call(
        kernel,
        out_shape=tuple(outs),
        in_specs=in_specs,
        out_specs=tuple(vspec() for _ in outs),
        scratch_shapes=list(scratch),
        cost_estimate=pl.CostEstimate(flops=flops, transcendentals=0, bytes_accessed=moved),
    )(*ins)


def split_kernel(live_ref, q_ref, k_ref, v_ref, *refs, outer, width, groups, copies):
    _, z, r = place()
    q_outs = refs[:INNER]
    kv_outs = refs[INNER:INNER + len(groups)]
    live_rows, sems = refs[INNER + len(groups):]
    keys = k_ref.shape[0]
    started = []

    def copy(source, target):
        one = pltpu.make_async_copy(source, target, sems.at[len(started)])
        one.start()
        started.append(one)

    live_rows[...] = jnp.full(live_rows.shape, live_ref[0], jnp.int32).astype(f32).astype(bf16)
    for k, out in enumerate(q_outs):
        for zz in range(outer):
            col = pl.multiple_of((zz * INNER + lax.bitwise_xor(r, k)) * width, width)
            copy(q_ref.at[:, pl.ds(col, width)], out.at[zz])
    for (k, offsets), out in zip(groups, kv_outs):
        for i, kk in enumerate(offsets):
            head = lax.bitwise_xor(z, kk) * INNER + lax.bitwise_xor(r, k)
            col = pl.multiple_of((head // copies) * HEAD_SIZE, HEAD_SIZE)
            copy(k_ref.at[:, pl.ds(col, HEAD_SIZE)], out.at[i, pl.ds(0, keys), :])
            copy(v_ref.at[:, pl.ds(col, HEAD_SIZE)], out.at[i, pl.ds(keys, keys), :])
            copy(live_rows, out.at[i, pl.ds(2 * keys, 16), :])
    for one in started:
        one.wait()


def split_weight_kernel(w_ref, out_ref, sem):
    _, _, r = place()
    half = out_ref.shape[1]
    col = pl.multiple_of((1 - lax.bitwise_and(r, 1)) * half, 128)
    one = pltpu.make_async_copy(w_ref.at[:, pl.ds(col, half)], out_ref, sem)
    one.start()
    one.wait()


def attention_kernel(first_ref, *refs, outer, offsets, rows_all, keys, heads, width):
    ys = refs[:outer]
    kvs = refs[outer:outer + INNER]
    outs = refs[outer + INNER:outer + INNER + len(offsets)]
    bias_ref, q_ref = refs[outer + INNER + len(offsets):]
    _, z, r = place()
    rows = rows_all // (outer * INNER)
    q_pos = first_ref[0] + lax.broadcasted_iota(jnp.int32, (rows_all, keys), 0)
    lane = lax.broadcasted_iota(jnp.int32, (rows_all, keys), 1)
    lane_f = lane.astype(f32)
    for k in range(INNER):
        start = (z * INNER + lax.bitwise_xor(r, k)) * keys
        live = kvs[k][0, 2 * keys:2 * keys + 1, :].astype(f32)
        live = jnp.concatenate([live] * (keys // HEAD_SIZE), axis=1)
        allowed = (lane_f < live) & (start + lane <= q_pos)
        bias_ref[:, k * keys:(k + 1) * keys] = jnp.where(allowed, 0.0, masked_value)
    column = lax.broadcasted_iota(jnp.int32, (rows_all, 128), 1)
    for i, kk in enumerate(offsets):
        zz = lax.bitwise_xor(z, kk)
        for k2 in range(outer):
            for k in range(INNER):
                src = lax.bitwise_xor(z, k2) * INNER + lax.bitwise_xor(r, k)
                at = pl.multiple_of(src * rows, rows)
                q_ref[pl.ds(at, rows), :] = ys[k2][k, zz].astype(f32)
        stats = jnp.zeros((rows_all, 128), f32)
        for h in range(heads):
            cols = slice(h * HEAD_SIZE, (h + 1) * HEAD_SIZE)
            query = q_ref[:, cols].astype(bf16)
            scores = []
            for k in range(INNER):
                part = lax.dot_general(
                    query, kvs[k][i, 0:keys, :], (((1,), (1,)), ((), ())),
                    preferred_element_type=f32,
                )
                scores.append(part * (score_scale * log2e) + bias_ref[:, k * keys:(k + 1) * keys])
            top = functools.reduce(jnp.maximum, scores)
            best = jnp.maximum(jnp.max(top, axis=1, keepdims=True), -1e29)
            acc = jnp.zeros((rows_all, HEAD_SIZE), f32)
            sums = jnp.zeros((rows_all, keys), f32)
            for k in range(INNER):
                weights = jnp.exp2(scores[k] - best)
                sums = sums + weights
                acc = acc + jnp.dot(
                    weights.astype(bf16), kvs[k][i, keys:2 * keys, :], preferred_element_type=f32
                )
            total = jnp.sum(sums, axis=1, keepdims=True)
            safe = jnp.where(total > 0, total, 1.0)
            outs[i][0:rows_all, cols] = (acc / safe).astype(bf16)
            logsum = jnp.where(total > 0, best * ln2 + jnp.log(safe), masked_value)
            high = logsum.astype(bf16).astype(f32)
            rest = logsum - high
            mid = rest.astype(bf16).astype(f32)
            low = rest - mid
            for p, piece in enumerate((high, mid, low)):
                stats = jnp.where(column == p * heads + h, piece, stats)
        turned = stats.T
        pieces = rows_all // width
        per = 16 // pieces
        block = [turned[0:per, j * width:(j + 1) * width] for j in range(pieces)]
        block = block[0] if pieces == 1 else jnp.concatenate(block, axis=0)
        outs[i][rows_all:rows_all + 16, :] = block.astype(bf16)


def merge_kernel(*refs, sources, rows_all, heads, width):
    parts = refs[:sources]
    out, turn_ref = refs[sources:]
    pieces = rows_all // width
    per = 16 // pieces
    logs = []
    for part in parts:
        block = part[rows_all:rows_all + 16, :].astype(f32)
        block = [block[j * per:(j + 1) * per] for j in range(pieces)]
        block = block[0] if pieces == 1 else jnp.concatenate(block, axis=1)
        logs.append(block[0:heads] + (block[heads:2 * heads] + block[2 * heads:3 * heads]))
    top = functools.reduce(jnp.maximum, logs)
    scales = [jnp.exp(l - top) for l in logs]
    total = functools.reduce(jnp.add, scales)
    turn_ref[...] = jnp.zeros_like(turn_ref)
    for i, scale in enumerate(scales):
        turn_ref[i * heads:(i + 1) * heads, :] = scale / total
    turned = turn_ref[...].T
    for h in range(heads):
        cols = slice(h * HEAD_SIZE, (h + 1) * HEAD_SIZE)
        acc = jnp.zeros((rows_all, HEAD_SIZE), f32)
        for i, part in enumerate(parts):
            at = i * heads + h
            acc = acc + turned[:, at:at + 1] * part[0:rows_all, cols].astype(f32)
        out[:, cols] = acc.astype(bf16)


def project_kernel(side_ref, mine_ref, other_ref, w_mine_ref, w_other_ref, *out_refs, groups, rows):
    _, z, r = place()
    y = lax.shift_right_logical(r, 1)

    def gather(ref, side):
        found = []
        for group in groups:
            for kk in group:
                at = (lax.bitwise_xor(z, kk) * INNER + side * 2) * rows
                found.append(ref[pl.ds(pl.multiple_of(at, 2 * rows), 2 * rows), :])
        return jnp.concatenate(found, axis=0)

    for side, outs in ((1 - y, out_refs[:len(groups)]), (y, out_refs[len(groups):])):
        term = jnp.dot(gather(mine_ref, side), w_mine_ref[...], preferred_element_type=f32)
        term = term + jnp.dot(gather(other_ref, side), w_other_ref[...], preferred_element_type=f32)
        at = 0
        for group, out in zip(groups, outs):
            size = 2 * rows * len(group)
            out[...] = term[at:at + size].astype(out.dtype)
            at += size


def first_sum_kernel(keep_ref, got_ref, *out_refs, span):
    for i, out in enumerate(out_refs):
        at = slice(i * span, (i + 1) * span)
        out[...] = (keep_ref[at, :] + got_ref[at, :].astype(f32)).astype(out.dtype)


def last_sum_kernel(keep_ref, got_ref, *refs, rows):
    *parts, mine_ref, other_ref, total_ref = refs
    _, _, r = place()
    c = lax.bitwise_and(r, 1)
    total = keep_ref[...] + got_ref[...].astype(f32)
    for part in parts:
        total = total + part[...].astype(f32)
    total_ref[...] = total
    mine_ref[...] = total_ref[pl.ds(pl.multiple_of(c * rows, rows), rows), :].astype(bf16)
    other_ref[...] = total_ref[pl.ds(pl.multiple_of((1 - c) * rows, rows), rows), :].astype(bf16)


def join_kernel(mine_ref, other_ref, out_ref):
    _, _, r = place()
    c = lax.bitwise_and(r, 1)
    half = mine_ref.shape[1]
    out_ref[:, pl.ds(pl.multiple_of(c * half, 128), half)] = mine_ref[...]
    out_ref[:, pl.ds(pl.multiple_of((1 - c) * half, 128), half)] = other_ref[...]


def layer(query_block, cache_keys, stored_values, live_counts, first_position, out_weight):
    devices = lax.axis_size("seq")
    outer = devices // INNER
    rows = query_block.shape[0]
    rows_all = rows * devices
    keys = cache_keys.shape[0]
    heads = QUERY_HEADS // devices
    width = heads * HEAD_SIZE
    copies = devices // KEY_VALUE_HEADS
    model = out_weight.shape[1]
    half = model // 2
    assert heads * copies == QUERY_HEADS // KEY_VALUE_HEADS and keys <= 256
    blocks = CHUNKS if half % (CHUNKS * 128) == 0 else 1
    cols = half // blocks
    shape = jax.ShapeDtypeStruct
    anywhere = pl.BlockSpec(memory_space=pl.ANY)

    def swap(x, k):
        return lax.ppermute(x, "seq", [(i, i ^ k) for i in range(devices)])

    order = list(range(outer - 1, -1, -1))
    phases = [order[:outer // 2], order[outer // 2:3 * outer // 4], order[3 * outer // 4:]]
    groups = [(0, order), (1, order)] + [(k, p) for p in phases for k in range(2, INNER)]
    outs = [shape((outer, rows, width), bf16)] * INNER + [
        shape((len(p), 2 * keys + 16, HEAD_SIZE), bf16) for k, p in groups
    ]
    copies_started = INNER * outer + sum(3 * len(p) for k, p in groups)
    split = pl.pallas_call(
        functools.partial(
            split_kernel, outer=outer, width=width, groups=groups, copies=copies
        ),
        out_shape=tuple(outs),
        in_specs=[sspec(), anywhere, anywhere, anywhere],
        out_specs=tuple(anywhere for _ in outs),
        scratch_shapes=[
            pltpu.VMEM((16, HEAD_SIZE), bf16), pltpu.SemaphoreType.DMA((copies_started,)),
        ],
        name="split",
    )(live_counts, query_block, cache_keys, stored_values)
    q_out, kv_out = split[:INNER], split[INNER:]
    q_got = {k: swap(q_out[k], k) for k in (2, 3, 1)}
    kv_pair = swap(kv_out[1], 1)
    kv_far = [
        {k: swap(kv_out[2 + 2 * i + k - 2], k) for k in range(2, INNER)}
        for i in range(len(phases))
    ]
    inner_q = jnp.stack([q_out[0], q_got[1], q_got[2], q_got[3]])
    ys = [inner_q] + [swap(inner_q, k * INNER) for k in range(1, outer)]

    w_send = pl.pallas_call(
        split_weight_kernel,
        out_shape=shape((out_weight.shape[0], half), bf16),
        in_specs=[anywhere],
        out_specs=anywhere,
        scratch_shapes=[pltpu.SemaphoreType.DMA],
        name="split_weight",
    )(out_weight)
    w_other = swap(w_send, 1)

    partial_of = {}
    at = 0
    for i, offsets in enumerate(phases):
        size = len(offsets)
        near = pl.BlockSpec(
            (size, 2 * keys + 16, HEAD_SIZE), functools.partial(lambda b, g: (b, 0, 0), at // size)
        )
        outs = pl.pallas_call(
            functools.partial(
                attention_kernel, outer=outer, offsets=offsets, rows_all=rows_all, keys=keys,
                heads=heads, width=width,
            ),
            out_shape=tuple([shape((rows_all + 16, width), bf16)] * size),
            grid=(1,),
            in_specs=[sspec()] + [vspec()] * outer + [near, near] + [vspec()] * (INNER - 2),
            out_specs=tuple(vspec() for _ in offsets),
            scratch_shapes=[
                pltpu.VMEM((rows_all, INNER * keys), f32), pltpu.VMEM((rows_all, width), f32),
            ],
            name="attention",
            cost_estimate=pl.CostEstimate(
                flops=4 * rows_all * INNER * keys * width * size, transcendentals=0,
                bytes_accessed=2 * INNER * keys * HEAD_SIZE * 2 * size,
            ),
        )(first_position, *ys, kv_out[0], kv_pair, kv_far[i][2], kv_far[i][3])
        at += size
        for kk, out in zip(offsets, outs):
            partial_of[kk] = swap(out, kk * INNER) if kk else out

    (merged,) = call(
        functools.partial(merge_kernel, sources=outer, rows_all=rows_all, heads=heads, width=width),
        [partial_of[k] for k in range(outer)], [shape((rows_all, width), bf16)],
        scratch=[pltpu.VMEM((128, rows_all), f32)],
    )
    other = swap(merged, 1)

    span = 2 * rows
    term_groups = [[kk] for kk in order[:-2]] + [order[-2:]]
    side = lax.bitwise_and(lax.axis_index("seq"), 1).reshape(1)
    out_shapes = [shape((span * len(g), half), bf16) for g in term_groups]
    out_shapes += [shape((span * len(g), half), f32) for g in term_groups]
    terms = pl.pallas_call(
        functools.partial(project_kernel, groups=term_groups, rows=rows),
        out_shape=tuple(out_shapes),
        grid_spec=pltpu.PrefetchScalarGridSpec(
            num_scalar_prefetch=1,
            grid=(blocks,),
            in_specs=[
                pl.BlockSpec((rows_all, width), lambda j, side: (0, 0)),
                pl.BlockSpec((rows_all, width), lambda j, side: (0, 0)),
                pl.BlockSpec((width, cols), lambda j, side: (0, side[0] * blocks + j)),
                pl.BlockSpec((width, cols), lambda j, side: (0, j)),
            ],
            out_specs=tuple(
                pl.BlockSpec((o.shape[0], cols), lambda j, side: (0, j)) for o in out_shapes
            ),
        ),
        name="project",
        cost_estimate=pl.CostEstimate(
            flops=4 * rows_all * width * half, transcendentals=0,
            bytes_accessed=4 * width * half,
        ),
    )(side, merged, other, out_weight, w_other)
    sends, keeps = terms[:len(term_groups)], terms[len(term_groups):]
    gots = [swap(x, 2) for x in sends]
    parts = []
    for i, group in enumerate(term_groups):
        moved = [kk for kk in group if kk]
        keep, got = keeps[i], gots[i]
        sums = pl.pallas_call(
            functools.partial(first_sum_kernel, span=span),
            out_shape=tuple([shape((span, half), bf16)] * len(moved)),
            grid=(1,),
            in_specs=[pl.BlockSpec((span * len(moved), half), lambda g: (0, 0))] * 2,
            out_specs=tuple(vspec() for _ in moved),
            name="first_sum",
        )(keep, got)
        parts += [swap(x, kk * INNER) for kk, x in zip(moved, sums)]
    last = len(term_groups[-1]) - 1
    mine, theirs = pl.pallas_call(
        functools.partial(last_sum_kernel, rows=rows),
        out_shape=tuple([shape((rows, half), bf16)] * 2),
        grid=(1,),
        in_specs=[pl.BlockSpec((span, half), lambda g: (last, 0))] * 2 + [vspec()] * len(parts),
        out_specs=(vspec(), vspec()),
        scratch_shapes=[pltpu.VMEM((span, half), f32)],
        name="last_sum",
    )(keeps[-1], gots[-1], *parts)
    (joined,) = call(join_kernel, [mine, swap(theirs, 1)], [shape((rows, model), bf16)])
    return joined


def solution(mesh):
    in_specs = (
        P(("groups", "seq"), None),
        P(("groups", "seq"), None),
        P(("groups", "seq"), None),
        P(("groups", "seq")),
        P("groups"),
        P("seq", None),
    )
    out_specs = P(("groups", "seq"), None)
    return jax.shard_map(layer, mesh=mesh, in_specs=in_specs, out_specs=out_specs, check_vma=False)
```

profile of v0, /device:TPU:0, one launch (start us, length us, event | category | flops | bytes accessed | tf_op | source)
XLA Modules:
  0.0 213.8 jit_solution(10568778639613552414)
XLA Ops:
  0.0 42.8 %split_weight.1 = bf16[256,2688]{1,0:T(8,128)(2,1)} custom-call(bf16[256,5376]{1,0:T(8,128)(2,1)} %w_mine_ref.1), custom_call_target="tpu_custom_call" | custom-call | tf_op jit(solution)/shard_map/split_weight/pallas_call | solution.py:280
  44.0 69.2 %split.1 = (bf16[4,16,256]{2,1,0:T(8,128)(2,1)}, bf16[4,16,256]{2,1,0:T(8,128)(2,1)}, bf16[4,16,256]{2,1,0:T(8,128)(2,1)}, bf16[4,16,256]{2,1,0:T(8,128)(2,1)}, ...) custom-call(s32[1]{0:T(128)S(6)} %copy.7.live_ref, ...), custom_call_target="tpu_custom_call" | custom-call | tf_op jit(solution)/shard_map/split/pallas_call | solution.py:258
  113.3 3.0 %collective-permute-start.1 = (bf16[4,16,256]{2,1,0:T(8,128)(2,1)}, bf16[4,16,256]{2,1,0:T(8,128)(2,1)S(1)}, u32[]{:S(2)}, u32[]{:S(2)}) collective-permute-start(bf16[4,16,256]{2,1,0:T(8,128)(2,1)} %get-tuple-element.29), channel_id=1, source_target_pairs={{0,2},{1,3},{2,0},{3,1},{4,6},{5,7},{6,4},{7,5},{8,10},{9,11},{10,... | collective-permute-start | bytes 98312 | tf_op jit(solution)/shard_map/ppermute | solution.py:249
  116.4 2.0 collective-permute-done.1
  118.4 1.8 collective-permute-done.2
  123.1 2.6 %collective-permute-start.4 = (bf16[4,4,16,256]{3,2,1,0:T(8,128)(2,1)S(1)}, bf16[4,4,16,256]{3,2,1,0:T(8,128)(2,1)S(1)}, u32[]{:S(2)}, u32[]{:S(2)}) collective-permute-start(bf16[4,4,16,256]{3,2,1,0:T(8,128)(2,1)S(1)} %pad_maximum_fusion.refs_0_), channel_id=1, source_target_pairs={{0,8},{1,9},{2,10},{3,11},{4,12},{5,13},{6,14},{7,15},{8,0},{9,1},... | collective-permute-start | bytes 393224 | tf_op jit(solution)/shard_map/ppermute | solution.py:249
  125.7 2.4 %collective-permute-done.3.refs_1_ = bf16[4,4,16,256]{3,2,1,0:T(8,128)(2,1)S(1)} collective-permute-done((bf16[4,4,16,256]{3,2,1,0:T(8,128)(2,1)S(1)}, bf16[4,4,16,256]{3,2,1,0:T(8,128)(2,1)S(1)}, u32[]{:S(2)}, u32[]{:S(2)}) %collective-permute-start.3) | collective-permute-done | bytes 131104 | tf_op jit(solution)/shard_map/ppermute | solution.py:249
  128.1 3.8 %collective-permute-done.4.refs_2_ = bf16[4,4,16,256]{3,2,1,0:T(8,128)(2,1)S(1)} collective-permute-done((bf16[4,4,16,256]{3,2,1,0:T(8,128)(2,1)S(1)}, bf16[4,4,16,256]{3,2,1,0:T(8,128)(2,1)S(1)}, u32[]{:S(2)}, u32[]{:S(2)}) %collective-permute-start.4) | collective-permute-done | bytes 131104 | tf_op jit(solution)/shard_map/ppermute | solution.py:249
  131.9 2.5 %collective-permute-start.5 = (bf16[4,4,16,256]{3,2,1,0:T(8,128)(2,1)S(1)}, bf16[4,4,16,256]{3,2,1,0:T(8,128)(2,1)S(1)}, u32[]{:S(2)}, u32[]{:S(2)}) collective-permute-start(bf16[4,4,16,256]{3,2,1,0:T(8,128)(2,1)S(1)} %pad_maximum_fusion.refs_0_), channel_id=1, source_target_pairs={{0,12},{1,13},{2,14},{3,15},{4,8},{5,9},{6,10},{7,11},{8,4},{9,5},... | collective-permute-start | bytes 393224 | tf_op jit(solution)/shard_map/ppermute | solution.py:249
  134.4 4.4 %collective-permute-done.5.refs_3_ = bf16[4,4,16,256]{3,2,1,0:T(8,128)(2,1)S(1)} collective-permute-done((bf16[4,4,16,256]{3,2,1,0:T(8,128)(2,1)S(1)}, bf16[4,4,16,256]{3,2,1,0:T(8,128)(2,1)S(1)}, u32[]{:S(2)}, u32[]{:S(2)}) %collective-permute-start.5) | collective-permute-done | bytes 131104 | tf_op jit(solution)/shard_map/ppermute | solution.py:249
  142.8 4.4 %attention.5 = (bf16[272,256]{1,0:T(8,128)(2,1)}, bf16[272,256]{1,0:T(8,128)(2,1)}) custom-call(s32[1]{0:T(128)S(6)} %copy.8.first_ref, bf16[4,4,16,256]{3,2,1,0:T(8,128)(2,1)} %copy-done.1, bf16[4,4,16,256]{3,2,1,0:T(8,128)(2,1)} %copy-done.4, bf16[4,4,16,256]{3,2,1,0:T(8,128)(2,1)} %copy-done.5, bf16[4,4,16,256]{3,2,1,0:T(8,128)(2,1)} %copy-done.6, ...), custom_call_target="tpu_custom_call" | custom-call | flops 536870912 | bytes 1048576 | tf_op jit(solution)/shard_map/attention/pallas_call | solution.py:297
  147.4 2.8 %collective-permute-start.15 = (bf16[272,256]{1,0:T(8,128)(2,1)}, bf16[272,256]{1,0:T(8,128)(2,1)S(1)}, u32[]{:S(2)}, u32[]{:S(2)}) collective-permute-start(bf16[272,256]{1,0:T(8,128)(2,1)} %get-tuple-element.40), channel_id=1, source_target_pairs={{0,12},{1,13},{2,14},{3,15},{4,8},{5,9},{6,10},{7,11},{8,4},{9,5},... | collective-permute-start | bytes 417800 | tf_op jit(solution)/shard_map/ppermute | solution.py:249
  150.3 3.2 %attention.4 = bf16[272,256]{1,0:T(8,128)(2,1)} custom-call(s32[1]{0:T(128)S(6)} %copy.8.first_ref, bf16[4,4,16,256]{3,2,1,0:T(8,128)(2,1)} %copy-done.1, bf16[4,4,16,256]{3,2,1,0:T(8,128)(2,1)} %copy-done.4, bf16[4,4,16,256]{3,2,1,0:T(8,128)(2,1)} %copy-done.5, bf16[4,4,16,256]{3,2,1,0:T(8,128)(2,1)} %copy-done.6, ...), custom_call_target="tpu_custom_call" | custom-call | flops 268435456 | bytes 524288 | tf_op jit(solution)/shard_map/attention/pallas_call | solution.py:297
  154.7 3.2 %attention.3.refs_0_ = bf16[272,256]{1,0:T(8,128)(2,1)} custom-call(s32[1]{0:T(128)S(6)} %copy.8.first_ref, bf16[4,4,16,256]{3,2,1,0:T(8,128)(2,1)} %copy-done.1, bf16[4,4,16,256]{3,2,1,0:T(8,128)(2,1)} %copy-done.4, bf16[4,4,16,256]{3,2,1,0:T(8,128)(2,1)} %copy-done.5, bf16[4,4,16,256]{3,2,1,0:T(8,128)(2,1)} %copy-done.6, ...), custom_call_target="tpu_custom_call" | custom-call | flops 268435456 | bytes 524288 | tf_op jit(solution)/shard_map/attention/pallas_call | solution.py:297
  157.9 2.8 %collective-permute-done.14.refs_2_ = bf16[272,256]{1,0:T(8,128)(2,1)S(1)} collective-permute-done((bf16[272,256]{1,0:T(8,128)(2,1)}, bf16[272,256]{1,0:T(8,128)(2,1)S(1)}, u32[]{:S(2)}, u32[]{:S(2)}) %collective-permute-start.14) | collective-permute-done | bytes 139296 | tf_op jit(solution)/shard_map/ppermute | solution.py:249
  160.7 2.5 %collective-permute-done.11.refs_1_ = bf16[272,256]{1,0:T(8,128)(2,1)S(1)} collective-permute-done((bf16[272,256]{1,0:T(8,128)(2,1)}, bf16[272,256]{1,0:T(8,128)(2,1)S(1)}, u32[]{:S(2)}, u32[]{:S(2)}) %collective-permute-start.11) | collective-permute-done | bytes 139296 | tf_op jit(solution)/shard_map/ppermute | solution.py:249
  163.9 2.2 %shard_map.64.mine_ref = bf16[256,256]{1,0:T(8,128)(2,1)} custom-call(bf16[272,256]{1,0:T(8,128)(2,1)} %attention.3.refs_0_, bf16[272,256]{1,0:T(8,128)(2,1)} %copy-done.16, bf16[272,256]{1,0:T(8,128)(2,1)} %copy-done.14, bf16[272,256]{1,0:T(8,128)(2,1)} %copy-done.15), custom_call_target="tpu_custom_call" | custom-call | bytes 688128 | tf_op jit(solution)/shard_map/pallas_call | solution.py:45
  168.8 4.4 %project.1 = (bf16[32,2688]{1,0:T(8,128)(2,1)}, bf16[32,2688]{1,0:T(8,128)(2,1)}, bf16[64,2688]{1,0:T(8,128)(2,1)}, f32[32,2688]{1,0:T(8,128)}, f32[32,2688]{1,0:T(8,128)}, /*index=5*/f32[64,2688]{1,0:T(8,128)}) custom-call(s32[1]{0:T(128)} %bitcast.side_ref, bf16[256,256]{1,0:T(8,128)(2,1)} %shard_map.64.mine_ref, bf16[256,256]{1,0:T(8,128)(2,1)} %copy-done.21, ...), custom_call_target="tpu_custom_call" | custom-call | flops 704643072 | bytes 2752512 | tf_op jit(solution)/shard_map/project/pallas_call | solution.py:331
  176.0 12.0 %collective-permute-done.21.got_ref = bf16[32,2688]{1,0:T(8,128)(2,1)S(1)} collective-permute-done((bf16[32,2688]{1,0:T(8,128)(2,1)}, bf16[32,2688]{1,0:T(8,128)(2,1)S(1)}, u32[]{:S(2)}, u32[]{:S(2)}) %collective-permute-start.21) | collective-permute-done | bytes 172064 | tf_op jit(solution)/shard_map/ppermute | solution.py:249
  188.7 1.7 first_sum.4
  193.8 2.6 %collective-permute-start.20 = (bf16[32,2688]{1,0:T(8,128)(2,1)}, bf16[32,2688]{1,0:T(8,128)(2,1)S(1)}, u32[]{:S(2)}, u32[]{:S(2)}) collective-permute-start(bf16[32,2688]{1,0:T(8,128)(2,1)} %first_sum.3), channel_id=1, source_target_pairs={{0,12},{1,13},{2,14},{3,15},{4,8},{5,9},{6,10},{7,11},{8,4},{9,5},... | collective-permute-start | bytes 516104 | tf_op jit(solution)/shard_map/ppermute | solution.py:249
  198.9 5.6 %collective-permute-done.22.refs_1_ = bf16[32,2688]{1,0:T(8,128)(2,1)S(1)} collective-permute-done((bf16[32,2688]{1,0:T(8,128)(2,1)}, bf16[32,2688]{1,0:T(8,128)(2,1)S(1)}, u32[]{:S(2)}, u32[]{:S(2)}) %collective-permute-start.22) | collective-permute-done | bytes 172064 | tf_op jit(solution)/shard_map/ppermute | solution.py:249
  204.5 2.8 %collective-permute-done.23.refs_2_ = bf16[32,2688]{1,0:T(8,128)(2,1)S(1)} collective-permute-done((bf16[32,2688]{1,0:T(8,128)(2,1)}, bf16[32,2688]{1,0:T(8,128)(2,1)S(1)}, u32[]{:S(2)}, u32[]{:S(2)}) %collective-permute-start.23) | collective-permute-done | bytes 172064 | tf_op jit(solution)/shard_map/ppermute | solution.py:249
  208.0 2.1 last_sum.1
  (85 shorter events, 25.6 us)
Async XLA Ops:
  42.8 124.8 %collective-permute-start.17 = (bf16[256,2688]{1,0:T(8,128)(2,1)}, bf16[256,2688]{1,0:T(8,128)(2,1)S(1)}, u32[]{:S(2)}, u32[]{:S(2)}) collective-permute-start(bf16[256,2688]{1,0:T(8,128)(2,1)} %split_weight.1), channel_id=1, source_target_pairs={{0,1},{1,0},{2,3},{3,2},{4,5},{5,4},{6,7},{7,6},{8,9},{9,8},{10,11... | collective-permute-start | bytes 4128776 | tf_op jit(solution)/shard_map/ppermute | solution.py:249
  113.2 3.2 %collective-permute-start = (bf16[4,16,256]{2,1,0:T(8,128)(2,1)}, bf16[4,16,256]{2,1,0:T(8,128)(2,1)S(1)}, u32[]{:S(2)}, u32[]{:S(2)}) collective-permute-start(bf16[4,16,256]{2,1,0:T(8,128)(2,1)} %get-tuple-element.28), channel_id=1, source_target_pairs={{0,1},{1,0},{2,3},{3,2},{4,5},{5,4},{6,7},{7,6},{8,9},{9,8},{10,11... | collective-permute-start | bytes 98312 | tf_op jit(solution)/shard_map/ppermute | solution.py:249
  113.3 5.1 %collective-permute-start.1 = (bf16[4,16,256]{2,1,0:T(8,128)(2,1)}, bf16[4,16,256]{2,1,0:T(8,128)(2,1)S(1)}, u32[]{:S(2)}, u32[]{:S(2)}) collective-permute-start(bf16[4,16,256]{2,1,0:T(8,128)(2,1)} %get-tuple-element.29), channel_id=1, source_target_pairs={{0,2},{1,3},{2,0},{3,1},{4,6},{5,7},{6,4},{7,5},{8,10},{9,11},{10,... | collective-permute-start | bytes 98312 | tf_op jit(solution)/shard_map/ppermute | solution.py:249
  116.3 3.9 %collective-permute-start.2 = (bf16[4,16,256]{2,1,0:T(8,128)(2,1)}, bf16[4,16,256]{2,1,0:T(8,128)(2,1)S(1)}, u32[]{:S(2)}, u32[]{:S(2)}) collective-permute-start(bf16[4,16,256]{2,1,0:T(8,128)(2,1)} %get-tuple-element.30), channel_id=1, source_target_pairs={{0,3},{1,2},{2,1},{3,0},{4,7},{5,6},{6,5},{7,4},{8,11},{9,10},{10,... | collective-permute-start | bytes 98312 | tf_op jit(solution)/shard_map/ppermute | solution.py:249
  116.3 25.2 %collective-permute-start.6 = (bf16[4,528,128]{2,1,0:T(8,128)(2,1)}, bf16[4,528,128]{2,1,0:T(8,128)(2,1)S(1)}, u32[]{:S(2)}, u32[]{:S(2)}) collective-permute-start(bf16[4,528,128]{2,1,0:T(8,128)(2,1)} %get-tuple-element.32), channel_id=1, source_target_pairs={{0,1},{1,0},{2,3},{3,2},{4,5},{5,4},{6,7},{7,6},{8,9},{9,8},{10,11... | collective-permute-start | bytes 1622024 | tf_op jit(solution)/shard_map/ppermute | solution.py:249
  121.0 7.2 %collective-permute-start.3 = (bf16[4,4,16,256]{3,2,1,0:T(8,128)(2,1)S(1)}, bf16[4,4,16,256]{3,2,1,0:T(8,128)(2,1)S(1)}, u32[]{:S(2)}, u32[]{:S(2)}) collective-permute-start(bf16[4,4,16,256]{3,2,1,0:T(8,128)(2,1)S(1)} %pad_maximum_fusion.refs_0_), channel_id=1, source_target_pairs={{0,4},{1,5},{2,6},{3,7},{4,0},{5,1},{6,2},{7,3},{8,12},{9,13},{10,... | collective-permute-start | bytes 393224 | tf_op jit(solution)/shard_map/ppermute | solution.py:249
  122.6 16.2 %collective-permute-start.12 = (bf16[2,528,128]{2,1,0:T(8,128)(2,1)}, bf16[2,528,128]{2,1,0:T(8,128)(2,1)S(1)}, u32[]{:S(2)}, u32[]{:S(2)}) collective-permute-start(bf16[2,528,128]{2,1,0:T(8,128)(2,1)} %get-tuple-element.37), channel_id=1, source_target_pairs={{0,2},{1,3},{2,0},{3,1},{4,6},{5,7},{6,4},{7,5},{8,10},{9,11},{10,... | collective-permute-start | bytes 811016 | tf_op jit(solution)/shard_map/ppermute | solution.py:249
  123.1 8.8 %collective-permute-start.4 = (bf16[4,4,16,256]{3,2,1,0:T(8,128)(2,1)S(1)}, bf16[4,4,16,256]{3,2,1,0:T(8,128)(2,1)S(1)}, u32[]{:S(2)}, u32[]{:S(2)}) collective-permute-start(bf16[4,4,16,256]{3,2,1,0:T(8,128)(2,1)S(1)} %pad_maximum_fusion.refs_0_), channel_id=1, source_target_pairs={{0,8},{1,9},{2,10},{3,11},{4,12},{5,13},{6,14},{7,15},{8,0},{9,1},... | collective-permute-start | bytes 393224 | tf_op jit(solution)/shard_map/ppermute | solution.py:249
  128.1 12.0 %collective-permute-start.13 = (bf16[2,528,128]{2,1,0:T(8,128)(2,1)}, bf16[2,528,128]{2,1,0:T(8,128)(2,1)S(1)}, u32[]{:S(2)}, u32[]{:S(2)}) collective-permute-start(bf16[2,528,128]{2,1,0:T(8,128)(2,1)} %get-tuple-element.38), channel_id=1, source_target_pairs={{0,3},{1,2},{2,1},{3,0},{4,7},{5,6},{6,5},{7,4},{8,11},{9,10},{10,... | collective-permute-start | bytes 811016 | tf_op jit(solution)/shard_map/ppermute | solution.py:249
  131.9 6.9 %collective-permute-start.5 = (bf16[4,4,16,256]{3,2,1,0:T(8,128)(2,1)S(1)}, bf16[4,4,16,256]{3,2,1,0:T(8,128)(2,1)S(1)}, u32[]{:S(2)}, u32[]{:S(2)}) collective-permute-start(bf16[4,4,16,256]{3,2,1,0:T(8,128)(2,1)S(1)} %pad_maximum_fusion.refs_0_), channel_id=1, source_target_pairs={{0,12},{1,13},{2,14},{3,15},{4,8},{5,9},{6,10},{7,11},{8,4},{9,5},... | collective-permute-start | bytes 393224 | tf_op jit(solution)/shard_map/ppermute | solution.py:249
  138.8 8.4 %collective-permute-start.10 = (bf16[1,528,128]{2,1,0:T(8,128)(2,1)}, bf16[1,528,128]{2,1,0:T(8,128)(2,1)S(1)}, u32[]{:S(2)}, u32[]{:S(2)}) collective-permute-start(bf16[1,528,128]{2,1,0:T(8,128)(2,1)} %get-tuple-element.36), channel_id=1, source_target_pairs={{0,3},{1,2},{2,1},{3,0},{4,7},{5,6},{6,5},{7,4},{8,11},{9,10},{10,... | collective-permute-start | bytes 405512 | tf_op jit(solution)/shard_map/ppermute | solution.py:249
  138.8 8.6 %collective-permute-start.9 = (bf16[1,528,128]{2,1,0:T(8,128)(2,1)}, bf16[1,528,128]{2,1,0:T(8,128)(2,1)S(1)}, u32[]{:S(2)}, u32[]{:S(2)}) collective-permute-start(bf16[1,528,128]{2,1,0:T(8,128)(2,1)} %get-tuple-element.35), channel_id=1, source_target_pairs={{0,2},{1,3},{2,0},{3,1},{4,6},{5,7},{6,4},{7,5},{8,10},{9,11},{10,... | collective-permute-start | bytes 405512 | tf_op jit(solution)/shard_map/ppermute | solution.py:249
  140.1 13.3 %collective-permute-start.7 = (bf16[1,528,128]{2,1,0:T(8,128)(2,1)}, bf16[1,528,128]{2,1,0:T(8,128)(2,1)S(1)}, u32[]{:S(2)}, u32[]{:S(2)}) collective-permute-start(bf16[1,528,128]{2,1,0:T(8,128)(2,1)} %get-tuple-element.33), channel_id=1, source_target_pairs={{0,2},{1,3},{2,0},{3,1},{4,6},{5,7},{6,4},{7,5},{8,10},{9,11},{10,... | collective-permute-start | bytes 405512 | tf_op jit(solution)/shard_map/ppermute | solution.py:249
  141.6 12.5 %collective-permute-start.8 = (bf16[1,528,128]{2,1,0:T(8,128)(2,1)}, bf16[1,528,128]{2,1,0:T(8,128)(2,1)S(1)}, u32[]{:S(2)}, u32[]{:S(2)}) collective-permute-start(bf16[1,528,128]{2,1,0:T(8,128)(2,1)} %get-tuple-element.34), channel_id=1, source_target_pairs={{0,3},{1,2},{2,1},{3,0},{4,7},{5,6},{6,5},{7,4},{8,11},{9,10},{10,... | collective-permute-start | bytes 405512 | tf_op jit(solution)/shard_map/ppermute | solution.py:249
  147.2 13.5 %collective-permute-start.14 = (bf16[272,256]{1,0:T(8,128)(2,1)}, bf16[272,256]{1,0:T(8,128)(2,1)S(1)}, u32[]{:S(2)}, u32[]{:S(2)}) collective-permute-start(bf16[272,256]{1,0:T(8,128)(2,1)} %get-tuple-element.39), channel_id=1, source_target_pairs={{0,8},{1,9},{2,10},{3,11},{4,12},{5,13},{6,14},{7,15},{8,0},{9,1},... | collective-permute-start | bytes 417800 | tf_op jit(solution)/shard_map/ppermute | solution.py:249
  147.4 13.3 %collective-permute-start.15 = (bf16[272,256]{1,0:T(8,128)(2,1)}, bf16[272,256]{1,0:T(8,128)(2,1)S(1)}, u32[]{:S(2)}, u32[]{:S(2)}) collective-permute-start(bf16[272,256]{1,0:T(8,128)(2,1)} %get-tuple-element.40), channel_id=1, source_target_pairs={{0,12},{1,13},{2,14},{3,15},{4,8},{5,9},{6,10},{7,11},{8,4},{9,5},... | collective-permute-start | bytes 417800 | tf_op jit(solution)/shard_map/ppermute | solution.py:249
  153.4 9.8 %collective-permute-start.11 = (bf16[272,256]{1,0:T(8,128)(2,1)}, bf16[272,256]{1,0:T(8,128)(2,1)S(1)}, u32[]{:S(2)}, u32[]{:S(2)}) collective-permute-start(bf16[272,256]{1,0:T(8,128)(2,1)} %attention.4), channel_id=1, source_target_pairs={{0,4},{1,5},{2,6},{3,7},{4,0},{5,1},{6,2},{7,3},{8,12},{9,13},{10,... | collective-permute-start | bytes 417800 | tf_op jit(solution)/shard_map/ppermute | solution.py:249
  166.1 1.6 collective-permute-start.16
  173.2 23.2 %collective-permute-start.18 = (bf16[64,2688]{1,0:T(8,128)(2,1)}, bf16[64,2688]{1,0:T(8,128)(2,1)S(1)}, u32[]{:S(2)}, u32[]{:S(2)}) collective-permute-start(bf16[64,2688]{1,0:T(8,128)(2,1)} %get-tuple-element.42), channel_id=1, source_target_pairs={{0,2},{1,3},{2,0},{3,1},{4,6},{5,7},{6,4},{7,5},{8,10},{9,11},{10,... | collective-permute-start | bytes 1032200 | tf_op jit(solution)/shard_map/ppermute | solution.py:249
  174.0 14.1 %collective-permute-start.21 = (bf16[32,2688]{1,0:T(8,128)(2,1)}, bf16[32,2688]{1,0:T(8,128)(2,1)S(1)}, u32[]{:S(2)}, u32[]{:S(2)}) collective-permute-start(bf16[32,2688]{1,0:T(8,128)(2,1)} %get-tuple-element.46), channel_id=1, source_target_pairs={{0,2},{1,3},{2,0},{3,1},{4,6},{5,7},{6,4},{7,5},{8,10},{9,11},{10,... | collective-permute-start | bytes 516104 | tf_op jit(solution)/shard_map/ppermute | solution.py:249
  175.2 16.2 %collective-permute-start.19 = (bf16[32,2688]{1,0:T(8,128)(2,1)}, bf16[32,2688]{1,0:T(8,128)(2,1)S(1)}, u32[]{:S(2)}, u32[]{:S(2)}) collective-permute-start(bf16[32,2688]{1,0:T(8,128)(2,1)} %get-tuple-element.44), channel_id=1, source_target_pairs={{0,2},{1,3},{2,0},{3,1},{4,6},{5,7},{6,4},{7,5},{8,10},{9,11},{10,... | collective-permute-start | bytes 516104 | tf_op jit(solution)/shard_map/ppermute | solution.py:249
  190.4 14.1 %collective-permute-start.22 = (bf16[32,2688]{1,0:T(8,128)(2,1)}, bf16[32,2688]{1,0:T(8,128)(2,1)S(1)}, u32[]{:S(2)}, u32[]{:S(2)}) collective-permute-start(bf16[32,2688]{1,0:T(8,128)(2,1)} %first_sum.4), channel_id=1, source_target_pairs={{0,8},{1,9},{2,10},{3,11},{4,12},{5,13},{6,14},{7,15},{8,0},{9,1},... | collective-permute-start | bytes 516104 | tf_op jit(solution)/shard_map/ppermute | solution.py:249
  193.8 10.7 %collective-permute-start.20 = (bf16[32,2688]{1,0:T(8,128)(2,1)}, bf16[32,2688]{1,0:T(8,128)(2,1)S(1)}, u32[]{:S(2)}, u32[]{:S(2)}) collective-permute-start(bf16[32,2688]{1,0:T(8,128)(2,1)} %first_sum.3), channel_id=1, source_target_pairs={{0,12},{1,13},{2,14},{3,15},{4,8},{5,9},{6,10},{7,11},{8,4},{9,5},... | collective-permute-start | bytes 516104 | tf_op jit(solution)/shard_map/ppermute | solution.py:249
  198.9 8.5 %collective-permute-start.23 = (bf16[32,2688]{1,0:T(8,128)(2,1)}, bf16[32,2688]{1,0:T(8,128)(2,1)S(1)}, u32[]{:S(2)}, u32[]{:S(2)}) collective-permute-start(bf16[32,2688]{1,0:T(8,128)(2,1)} %first_sum.5), channel_id=1, source_target_pairs={{0,4},{1,5},{2,6},{3,7},{4,0},{5,1},{6,2},{7,3},{8,12},{9,13},{10,... | collective-permute-start | bytes 516104 | tf_op jit(solution)/shard_map/ppermute | solution.py:249
  (24 other events, 84.3 us)
where the time goes:
time: 214 us
  Pallas kernels  138 us (64%)
  waiting for transfers between devices  43.3 us (20%)
  starting transfers between devices  24.3 us (11%)
  local copies, waits for them, and re-layouts  5.84 us (3%)
    pallas_call x1, Pallas kernels, layer(): pl.pallas_call(functools.partial(split_kernel, outer=outer, width=width,...  69.2 us
    ppermute x25, waiting for transfers between devices, swap(): return lax.ppermute(x, 'seq', [(i, i ^ k) for i in range(devices)])  43.3 us
    pallas_call x1, Pallas kernels, layer(): pl.pallas_call(split_weight_kernel, out_shape=shape((out_weight.shape[0],...  42.8 us
    ppermute x25, starting transfers between devices, swap(): return lax.ppermute(x, 'seq', [(i, i ^ k) for i in range(devices)])  24.3 us
    pallas_call x3, Pallas kernels, layer(): pl.pallas_call(functools.partial(attention_kernel, outer=outer, offsets=o...  10.7 us
    unnamed x46, local copies, waits for them, and re-layouts  5.84 us
    pallas_call x3, Pallas kernels, layer(): pl.pallas_call(functools.partial(first_sum_kernel, span=span), out_shape=...  5.16 us
    pallas_call x1, Pallas kernels, layer(): pl.pallas_call(functools.partial(project_kernel, groups=term_groups, rows...  4.43 us
  transfers between devices with their start and end apart: 25, of which 13 were waited for; matrix products, arithmetic and copies ran while one was open for 0% of the time, Pallas kernels for 41%

commit v1 on v0

v1 whole, which is shorter than its diff:
```python
import functools

import jax
import jax.numpy as jnp
from jax import lax
from jax.experimental import pallas as pl
from jax.experimental.pallas import tpu as pltpu
from jax.sharding import PartitionSpec as P


QUERY_HEADS = 32
KEY_VALUE_HEADS = 16
HEAD_SIZE = 128
INNER = 4
CHUNKS = 3

score_scale = 168.0 ** (-0.5)
masked_value = -1e30
log2e = 1.4426950408889634
ln2 = 0.6931471805599453


bf16 = jnp.bfloat16
f32 = jnp.float32
VM = pltpu.MemorySpace.VMEM
SM = pltpu.MemorySpace.SMEM


def vspec():
    return pl.BlockSpec(memory_space=VM)


def sspec():
    return pl.BlockSpec(memory_space=SM)


def place():
    me = lax.axis_index("seq")
    return me, lax.shift_right_logical(me, 2), lax.bitwise_and(me, 3)


def call(kernel, ins, outs, scratch=(), scalars=0, flops=0, limit=8):
    in_specs = [sspec()] * scalars + [vspec()] * (len(ins) - scalars)
    moved = sum(a.size * a.dtype.itemsize for a in list(ins) + list(outs))
    return pl.pallas_call(
        kernel,
        out_shape=tuple(outs),
        in_specs=in_specs,
        out_specs=tuple(vspec() for _ in outs),
        scratch_shapes=list(scratch),
        cost_estimate=pl.CostEstimate(flops=flops, transcendentals=0, bytes_accessed=moved),
        compiler_params=pltpu.CompilerParams(vmem_limit_bytes=limit << 20),
    )(*ins)


def split_kernel(live_ref, q_ref, k_ref, v_ref, *refs, outer, width, groups, copies):
    _, z, r = place()
    q_outs = refs[:INNER]
    kv_outs = refs[INNER:]
    keys = k_ref.shape[0]
    live = jnp.full((16, HEAD_SIZE), live_ref[0], jnp.int32).astype(f32).astype(bf16)
    for k, out in enumerate(q_outs):
        for zz in range(outer):
            col = pl.multiple_of((zz * INNER + lax.bitwise_xor(r, k)) * width, width)
            out[zz] = q_ref[:, pl.ds(col, width)]
    for (k, offsets), out in zip(groups, kv_outs):
        for i, kk in enumerate(offsets):
            head = lax.bitwise_xor(z, kk) * INNER + lax.bitwise_xor(r, k)
            col = pl.multiple_of((head // copies) * HEAD_SIZE, HEAD_SIZE)
            out[i, 0:keys, :] = k_ref[:, pl.ds(col, HEAD_SIZE)]
            out[i, keys:2 * keys, :] = v_ref[:, pl.ds(col, HEAD_SIZE)]
            out[i, 2 * keys:2 * keys + 16, :] = live


def split_weight_kernel(w_ref, out_ref):
    _, _, r = place()
    half = out_ref.shape[1]
    col = pl.multiple_of((1 - lax.bitwise_and(r, 1)) * half, 128)
    out_ref[...] = w_ref[:, pl.ds(col, half)]


def attention_kernel(first_ref, *refs, outer, first, offsets, rows_all, keys, heads, width):
    ys = refs[:outer]
    kvs = refs[outer:outer + INNER]
    begin = [first, first] + [0] * (INNER - 2)
    outs = refs[outer + INNER:outer + INNER + len(offsets)]
    bias_ref, q_ref = refs[outer + INNER + len(offsets):]
    _, z, r = place()
    rows = rows_all // (outer * INNER)
    q_pos = first_ref[0] + lax.broadcasted_iota(jnp.int32, (rows_all, keys), 0)
    lane = lax.broadcasted_iota(jnp.int32, (rows_all, keys), 1)
    lane_f = lane.astype(f32)
    for k in range(INNER):
        start = (z * INNER + lax.bitwise_xor(r, k)) * keys
        live = kvs[k][0, 2 * keys:2 * keys + 1, :].astype(f32)
        live = jnp.concatenate([live] * (keys // HEAD_SIZE), axis=1)
        allowed = (lane_f < live) & (start + lane <= q_pos)
        bias_ref[:, k * keys:(k + 1) * keys] = jnp.where(allowed, 0.0, masked_value)
    column = lax.broadcasted_iota(jnp.int32, (rows_all, 128), 1)
    for i, kk in enumerate(offsets):
        zz = lax.bitwise_xor(z, kk)
        for k2 in range(outer):
            for k in range(INNER):
                src = lax.bitwise_xor(z, k2) * INNER + lax.bitwise_xor(r, k)
                at = pl.multiple_of(src * rows, rows)
                q_ref[pl.ds(at, rows), :] = ys[k2][k, zz].astype(f32)
        stats = jnp.zeros((rows_all, 128), f32)
        for h in range(heads):
            cols = slice(h * HEAD_SIZE, (h + 1) * HEAD_SIZE)
            query = q_ref[:, cols].astype(bf16)
            scores = []
            for k in range(INNER):
                part = lax.dot_general(
                    query, kvs[k][begin[k] + i, 0:keys, :], (((1,), (1,)), ((), ())),
                    preferred_element_type=f32,
                )
                scores.append(part * (score_scale * log2e) + bias_ref[:, k * keys:(k + 1) * keys])
            top = functools.reduce(jnp.maximum, scores)
            best = jnp.maximum(jnp.max(top, axis=1, keepdims=True), -1e29)
            acc = jnp.zeros((rows_all, HEAD_SIZE), f32)
            sums = jnp.zeros((rows_all, keys), f32)
            for k in range(INNER):
                weights = jnp.exp2(scores[k] - best)
                sums = sums + weights
                acc = acc + jnp.dot(
                    weights.astype(bf16), kvs[k][begin[k] + i, keys:2 * keys, :], preferred_element_type=f32
                )
            total = jnp.sum(sums, axis=1, keepdims=True)
            safe = jnp.where(total > 0, total, 1.0)
            outs[i][0:rows_all, cols] = (acc / safe).astype(bf16)
            logsum = jnp.where(total > 0, best * ln2 + jnp.log(safe), masked_value)
            high = logsum.astype(bf16).astype(f32)
            rest = logsum - high
            mid = rest.astype(bf16).astype(f32)
            low = rest - mid
            for p, piece in enumerate((high, mid, low)):
                stats = jnp.where(column == p * heads + h, piece, stats)
        turned = stats.T
        pieces = rows_all // width
        per = 16 // pieces
        block = [turned[0:per, j * width:(j + 1) * width] for j in range(pieces)]
        block = block[0] if pieces == 1 else jnp.concatenate(block, axis=0)
        outs[i][rows_all:rows_all + 16, :] = block.astype(bf16)


def merge_kernel(*refs, sources, rows_all, heads, width):
    parts = refs[:sources]
    out, turn_ref = refs[sources:]
    pieces = rows_all // width
    per = 16 // pieces
    logs = []
    for part in parts:
        block = part[rows_all:rows_all + 16, :].astype(f32)
        block = [block[j * per:(j + 1) * per] for j in range(pieces)]
        block = block[0] if pieces == 1 else jnp.concatenate(block, axis=1)
        logs.append(block[0:heads] + (block[heads:2 * heads] + block[2 * heads:3 * heads]))
    top = functools.reduce(jnp.maximum, logs)
    scales = [jnp.exp(l - top) for l in logs]
    total = functools.reduce(jnp.add, scales)
    turn_ref[...] = jnp.zeros_like(turn_ref)
    for i, scale in enumerate(scales):
        turn_ref[i * heads:(i + 1) * heads, :] = scale / total
    turned = turn_ref[...].T
    for h in range(heads):
        cols = slice(h * HEAD_SIZE, (h + 1) * HEAD_SIZE)
        acc = jnp.zeros((rows_all, HEAD_SIZE), f32)
        for i, part in enumerate(parts):
            at = i * heads + h
            acc = acc + turned[:, at:at + 1] * part[0:rows_all, cols].astype(f32)
        out[:, cols] = acc.astype(bf16)


def project_kernel(mine_ref, other_ref, w_mine_ref, w_other_ref, *out_refs, groups, rows, blocks):
    _, z, r = place()
    y = lax.shift_right_logical(r, 1)
    half = w_other_ref.shape[1]
    cols = half // blocks

    def gather(ref, side):
        found = []
        for group in groups:
            for kk in group:
                at = (lax.bitwise_xor(z, kk) * INNER + side * 2) * rows
                found.append(ref[pl.ds(pl.multiple_of(at, 2 * rows), 2 * rows), :])
        return jnp.concatenate(found, axis=0)

    mine = jnp.concatenate([gather(mine_ref, 1 - y), gather(mine_ref, y)], axis=0)
    other = jnp.concatenate([gather(other_ref, 1 - y), gather(other_ref, y)], axis=0)
    for j in range(blocks):
        here = slice(j * cols, (j + 1) * cols)
        col = pl.multiple_of(lax.bitwise_and(r, 1) * half + j * cols, 128)
        term = jnp.dot(mine, w_mine_ref[:, pl.ds(col, cols)], preferred_element_type=f32)
        term = term + jnp.dot(other, w_other_ref[:, here], preferred_element_type=f32)
        at = 0
        for group, out in zip(groups + groups, out_refs):
            size = 2 * rows * len(group)
            out[:, here] = term[at:at + size].astype(out.dtype)
            at += size


def first_sum_kernel(keep_ref, got_ref, out_ref):
    out_ref[...] = (keep_ref[...] + got_ref[...].astype(f32)).astype(out_ref.dtype)


def last_sum_kernel(keep_ref, got_ref, *refs, rows):
    *parts, mine_ref, other_ref, total_ref = refs
    _, _, r = place()
    c = lax.bitwise_and(r, 1)
    total = keep_ref[...] + got_ref[...].astype(f32)
    for part in parts:
        total = total + part[...].astype(f32)
    total_ref[...] = total
    mine_ref[...] = total_ref[pl.ds(pl.multiple_of(c * rows, rows), rows), :].astype(bf16)
    other_ref[...] = total_ref[pl.ds(pl.multiple_of((1 - c) * rows, rows), rows), :].astype(bf16)


def join_kernel(mine_ref, other_ref, out_ref):
    _, _, r = place()
    c = lax.bitwise_and(r, 1)
    half = mine_ref.shape[1]
    out_ref[:, pl.ds(pl.multiple_of(c * half, 128), half)] = mine_ref[...]
    out_ref[:, pl.ds(pl.multiple_of((1 - c) * half, 128), half)] = other_ref[...]


def layer(query_block, cache_keys, stored_values, live_counts, first_position, out_weight):
    devices = lax.axis_size("seq")
    outer = devices // INNER
    rows = query_block.shape[0]
    rows_all = rows * devices
    keys = cache_keys.shape[0]
    heads = QUERY_HEADS // devices
    width = heads * HEAD_SIZE
    copies = devices // KEY_VALUE_HEADS
    model = out_weight.shape[1]
    half = model // 2
    assert heads * copies == QUERY_HEADS // KEY_VALUE_HEADS and keys <= 256
    blocks = CHUNKS if half % (CHUNKS * 128) == 0 else 1
    shape = jax.ShapeDtypeStruct

    def swap(x, k):
        return lax.ppermute(x, "seq", [(i, i ^ k) for i in range(devices)])

    order = list(range(outer - 1, -1, -1))
    phases = [order[:outer // 2], order[outer // 2:3 * outer // 4], order[3 * outer // 4:]]
    groups = [(0, order), (1, order)] + [(k, p) for p in phases for k in range(2, INNER)]
    outs = [shape((outer, rows, width), bf16)] * INNER + [
        shape((len(p), 2 * keys + 16, HEAD_SIZE), bf16) for k, p in groups
    ]
    split = call(
        functools.partial(split_kernel, outer=outer, width=width, groups=groups, copies=copies),
        [live_counts, query_block, cache_keys, stored_values], outs, scalars=1,
    )
    q_out, kv_out = split[:INNER], split[INNER:]
    q_got = {k: swap(q_out[k], k) for k in (2, 3, 1)}
    kv_pair = swap(kv_out[1], 1)
    kv_far = [
        {k: swap(kv_out[2 + 2 * i + k - 2], k) for k in range(2, INNER)}
        for i in range(len(phases))
    ]
    inner_q = jnp.stack([q_out[0], q_got[1], q_got[2], q_got[3]])
    ys = [inner_q] + [swap(inner_q, k * INNER) for k in range(1, outer)]

    (w_send,) = call(
        split_weight_kernel, [out_weight],
        [shape((out_weight.shape[0], half), bf16)],
    )
    w_other = swap(w_send, 1)

    partial_of = {}
    at = 0
    for i, offsets in enumerate(phases):
        size = len(offsets)
        outs = call(
            functools.partial(
                attention_kernel, outer=outer, first=at, offsets=offsets, rows_all=rows_all,
                keys=keys, heads=heads, width=width,
            ),
            [first_position, *ys, kv_out[0], kv_pair, kv_far[i][2], kv_far[i][3]],
            [shape((rows_all + 16, width), bf16)] * size,
            scratch=[pltpu.VMEM((rows_all, INNER * keys), f32), pltpu.VMEM((rows_all, width), f32)],
            scalars=1, flops=4 * rows_all * INNER * keys * width * size, limit=20,
        )
        at += size
        for kk, out in zip(offsets, outs):
            partial_of[kk] = swap(out, kk * INNER) if kk else out

    (merged,) = call(
        functools.partial(merge_kernel, sources=outer, rows_all=rows_all, heads=heads, width=width),
        [partial_of[k] for k in range(outer)], [shape((rows_all, width), bf16)],
        scratch=[pltpu.VMEM((128, rows_all), f32)],
    )
    other = swap(merged, 1)

    span = 2 * rows
    term_groups = [[kk] for kk in order]
    terms = call(
        functools.partial(project_kernel, groups=term_groups, rows=rows, blocks=blocks),
        [merged, other, out_weight, w_other],
        [shape((span * len(g), half), bf16) for g in term_groups]
        + [shape((span * len(g), half), f32) for g in term_groups],
        flops=4 * rows_all * width * half, limit=20,
    )
    sends, keeps = terms[:outer], terms[outer:]
    gots = [swap(x, 2) for x in sends]
    parts = []
    for i, kk in enumerate(order[:-1]):
        (part,) = call(first_sum_kernel, [keeps[i], gots[i]], [shape((span, half), bf16)])
        parts.append(swap(part, kk * INNER))
    mine, theirs = call(
        functools.partial(last_sum_kernel, rows=rows), [keeps[-1], gots[-1]] + parts,
        [shape((rows, half), bf16)] * 2, scratch=[pltpu.VMEM((span, half), f32)],
    )
    (joined,) = call(join_kernel, [mine, swap(theirs, 1)], [shape((rows, model), bf16)])
    return joined


def solution(mesh):
    in_specs = (
        P(("groups", "seq"), None),
        P(("groups", "seq"), None),
        P(("groups", "seq"), None),
        P(("groups", "seq")),
        P("groups"),
        P("seq", None),
    )
    out_specs = P(("groups", "seq"), None)
    return jax.shard_map(layer, mesh=mesh, in_specs=in_specs, out_specs=out_specs, check_vma=False)
```

time: 214 us -> 81.2 us (0.38)
  Pallas kernels: 138 us -> 7.84 us
  local copies, waits for them, and re-layouts: 5.84 us -> 1.98 us
    pallas_call x10 -> x0, Pallas kernels: 134 us -> none  [the longest x1 69.2 us: layer(): pl.pallas_call(functools.partial(split_kernel, outer=outer, width=width,...]
    pallas_call x2 -> x12, Pallas kernels: 3.84 us -> 7.84 us  [call(): pl.pallas_call(kernel, out_shape=tuple(outs), in_specs=in_specs, out_spec...]
    unnamed x46 -> x10, local copies, waits for them, and re-layouts: 5.84 us -> 1.98 us
    ppermute x25 -> x26, waiting for transfers between devices: 43.3 us -> 44.3 us  [swap(): return lax.ppermute(x, 'seq', [(i, i ^ k) for i in range(devices)])]
    ppermute x25 -> x26, starting transfers between devices: 24.3 us -> 24.5 us  [swap(): return lax.ppermute(x, 'seq', [(i, i ^ k) for i in range(devices)])]
  transfers between devices with their start and end apart: 25 -> 26, of which waited for: 13 -> 16; matrix products, arithmetic and copies ran while one was open for 0% -> 0% of each run, Pallas kernels for 41% -> 7%
where the time goes in v1:
time: 81.2 us; the launch traced here: 80.1 us
  waiting for transfers between devices  44.3 us (55%)
  starting transfers between devices  24.5 us (30%)
  Pallas kernels  7.84 us (10%)
  local copies, waits for them, and re-layouts  1.98 us (2%)
  between operations  1.46 us (2%)
    ppermute x26, waiting for transfers between devices, swap(): return lax.ppermute(x, 'seq', [(i, i ^ k) for i in range(devices)])  44.3 us
    ppermute x26, starting transfers between devices, swap(): return lax.ppermute(x, 'seq', [(i, i ^ k) for i in range(devices)])  24.5 us
    pallas_call x12, Pallas kernels, call(): pl.pallas_call(kernel, out_shape=tuple(outs), in_specs=in_specs, out_spec...  7.84 us
    unnamed x10, local copies, waits for them, and re-layouts  1.98 us
  transfers between devices with their start and end apart: 26, of which 16 were waited for; matrix products, arithmetic and copies ran while one was open for 0% of the time, Pallas kernels for 7%

profile of v1, /device:TPU:0, one launch (start us, length us, event | category | flops | bytes accessed | tf_op | source)
XLA Modules:
  0.0 80.1 jit_solution(11906896712548650181)
XLA Ops:
  0.0 1.8 %copy-done = bf16[256,5376]{1,0:T(8,128)(2,1)S(1)} copy-done((bf16[256,5376]{1,0:T(8,128)(2,1)S(1)}, bf16[256,5376]{1,0:T(8,128)(2,1)}, u32[]{:S(2)}) %copy-start) | copy-done | bytes 2752536
  4.5 2.6 %collective-permute-start.1 = (bf16[4,16,256]{2,1,0:T(8,128)(2,1)S(1)}, bf16[4,16,256]{2,1,0:T(8,128)(2,1)S(1)}, u32[]{:S(2)}, u32[]{:S(2)}) collective-permute-start(bf16[4,16,256]{2,1,0:T(8,128)(2,1)S(1)} %get-tuple-element.31), channel_id=1, source_target_pairs={{0,2},{1,3},{2,0},{3,1},{4,6},{5,7},{6,4},{7,5},{8,10},{9,11},{10,... | collective-permute-start | bytes 98312 | tf_op jit(solution)/shard_map/ppermute | solution.py:241
  7.2 1.8 %collective-permute-done.1 = bf16[4,16,256]{2,1,0:T(8,128)(2,1)S(1)} collective-permute-done((bf16[4,16,256]{2,1,0:T(8,128)(2,1)S(1)}, bf16[4,16,256]{2,1,0:T(8,128)(2,1)S(1)}, u32[]{:S(2)}, u32[]{:S(2)}) %collective-permute-start.1) | collective-permute-done | bytes 32800 | tf_op jit(solution)/shard_map/ppermute | solution.py:241
  9.0 1.4 %collective-permute-done.2 = bf16[4,16,256]{2,1,0:T(8,128)(2,1)S(1)} collective-permute-done((bf16[4,16,256]{2,1,0:T(8,128)(2,1)S(1)}, bf16[4,16,256]{2,1,0:T(8,128)(2,1)S(1)}, u32[]{:S(2)}, u32[]{:S(2)}) %collective-permute-start.2) | collective-permute-done | bytes 32800 | tf_op jit(solution)/shard_map/ppermute | solution.py:241
  10.4 1.6 %collective-permute-start.3 = (bf16[4,4,16,256]{3,2,1,0:T(8,128)(2,1)S(1)}, bf16[4,4,16,256]{3,2,1,0:T(8,128)(2,1)S(1)}, u32[]{:S(2)}, u32[]{:S(2)}) collective-permute-start(bf16[4,4,16,256]{3,2,1,0:T(8,128)(2,1)S(1)} %pad_maximum_fusion.refs_0_), channel_id=1, source_target_pairs={{0,4},{1,5},{2,6},{3,7},{4,0},{5,1},{6,2},{7,3},{8,12},{9,13},{10,... | collective-permute-start | bytes 393224 | tf_op jit(solution)/shard_map/ppermute | solution.py:241
  12.9 2.6 %collective-permute-start.4 = (bf16[4,4,16,256]{3,2,1,0:T(8,128)(2,1)S(1)}, bf16[4,4,16,256]{3,2,1,0:T(8,128)(2,1)S(1)}, u32[]{:S(2)}, u32[]{:S(2)}) collective-permute-start(bf16[4,4,16,256]{3,2,1,0:T(8,128)(2,1)S(1)} %pad_maximum_fusion.refs_0_), channel_id=1, source_target_pairs={{0,8},{1,9},{2,10},{3,11},{4,12},{5,13},{6,14},{7,15},{8,0},{9,1},... | collective-permute-start | bytes 393224 | tf_op jit(solution)/shard_map/ppermute | solution.py:241
  16.1 5.6 %collective-permute-done.4.refs_2_ = bf16[4,4,16,256]{3,2,1,0:T(8,128)(2,1)S(1)} collective-permute-done((bf16[4,4,16,256]{3,2,1,0:T(8,128)(2,1)S(1)}, bf16[4,4,16,256]{3,2,1,0:T(8,128)(2,1)S(1)}, u32[]{:S(2)}, u32[]{:S(2)}) %collective-permute-start.4) | collective-permute-done | bytes 131104 | tf_op jit(solution)/shard_map/ppermute | solution.py:241
  21.6 2.7 %collective-permute-start.5 = (bf16[4,4,16,256]{3,2,1,0:T(8,128)(2,1)S(1)}, bf16[4,4,16,256]{3,2,1,0:T(8,128)(2,1)S(1)}, u32[]{:S(2)}, u32[]{:S(2)}) collective-permute-start(bf16[4,4,16,256]{3,2,1,0:T(8,128)(2,1)S(1)} %pad_maximum_fusion.refs_0_), channel_id=1, source_target_pairs={{0,12},{1,13},{2,14},{3,15},{4,8},{5,9},{6,10},{7,11},{8,4},{9,5},... | collective-permute-start | bytes 393224 | tf_op jit(solution)/shard_map/ppermute | solution.py:241
  24.3 4.1 %collective-permute-done.5.refs_3_ = bf16[4,4,16,256]{3,2,1,0:T(8,128)(2,1)S(1)} collective-permute-done((bf16[4,4,16,256]{3,2,1,0:T(8,128)(2,1)S(1)}, bf16[4,4,16,256]{3,2,1,0:T(8,128)(2,1)S(1)}, u32[]{:S(2)}, u32[]{:S(2)}) %collective-permute-start.5) | collective-permute-done | bytes 131104 | tf_op jit(solution)/shard_map/ppermute | solution.py:241
  31.1 1.2 %collective-permute-start.8 = (bf16[1,528,128]{2,1,0:T(8,128)(2,1)S(1)}, bf16[1,528,128]{2,1,0:T(8,128)(2,1)S(1)}, u32[]{:S(2)}, u32[]{:S(2)}) collective-permute-start(bf16[1,528,128]{2,1,0:T(8,128)(2,1)S(1)} %get-tuple-element.36), channel_id=1, source_target_pairs={{0,3},{1,2},{2,1},{3,0},{4,7},{5,6},{6,5},{7,4},{8,11},{9,10},{10,... | collective-permute-start | bytes 405512 | tf_op jit(solution)/shard_map/ppermute | solution.py:241
  32.4 2.3 %shard_map.67 = (bf16[272,256]{1,0:T(8,128)(2,1)S(1)}, bf16[272,256]{1,0:T(8,128)(2,1)S(1)}) custom-call(s32[1]{0:T(128)S(6)} %copy.8.first_ref, bf16[4,4,16,256]{3,2,1,0:T(8,128)(2,1)S(1)} %pad_maximum_fusion.refs_0_, bf16[4,4,16,256]{3,2,1,0:T(8,128)(2,1)S(1)} %collective-permute-done.3.refs_1_, ...), custom_call_target="tpu_custom_call" | custom-call | flops 536870912 | bytes 2424836 | tf_op jit(solution)/shard_map/pallas_call | solution.py:45
  34.8 1.8 %collective-permute-done.9.refs_6_ = bf16[1,528,128]{2,1,0:T(8,128)(2,1)S(1)} collective-permute-done((bf16[1,528,128]{2,1,0:T(8,128)(2,1)S(1)}, bf16[1,528,128]{2,1,0:T(8,128)(2,1)S(1)}, u32[]{:S(2)}, u32[]{:S(2)}) %collective-permute-start.9) | collective-permute-done | bytes 135200 | tf_op jit(solution)/shard_map/ppermute | solution.py:241
  36.6 2.9 %collective-permute-start.15 = (bf16[272,256]{1,0:T(8,128)(2,1)S(1)}, bf16[272,256]{1,0:T(8,128)(2,1)S(1)}, u32[]{:S(2)}, u32[]{:S(2)}) collective-permute-start(bf16[272,256]{1,0:T(8,128)(2,1)S(1)} %get-tuple-element.42), channel_id=1, source_target_pairs={{0,12},{1,13},{2,14},{3,15},{4,8},{5,9},{6,10},{7,11},{8,4},{9,5},... | collective-permute-start | bytes 417800 | tf_op jit(solution)/shard_map/ppermute | solution.py:241
  40.8 1.9 %collective-permute-done.8.refs_7_ = bf16[1,528,128]{2,1,0:T(8,128)(2,1)S(1)} collective-permute-done((bf16[1,528,128]{2,1,0:T(8,128)(2,1)S(1)}, bf16[1,528,128]{2,1,0:T(8,128)(2,1)S(1)}, u32[]{:S(2)}, u32[]{:S(2)}) %collective-permute-start.8) | collective-permute-done | bytes 135200 | tf_op jit(solution)/shard_map/ppermute | solution.py:241
  43.9 3.6 %collective-permute-done.14.refs_2_ = bf16[272,256]{1,0:T(8,128)(2,1)S(1)} collective-permute-done((bf16[272,256]{1,0:T(8,128)(2,1)S(1)}, bf16[272,256]{1,0:T(8,128)(2,1)S(1)}, u32[]{:S(2)}, u32[]{:S(2)}) %collective-permute-start.14) | collective-permute-done | bytes 139296 | tf_op jit(solution)/shard_map/ppermute | solution.py:241
  47.5 2.7 %collective-permute-done.11.refs_1_ = bf16[272,256]{1,0:T(8,128)(2,1)S(1)} collective-permute-done((bf16[272,256]{1,0:T(8,128)(2,1)S(1)}, bf16[272,256]{1,0:T(8,128)(2,1)S(1)}, u32[]{:S(2)}, u32[]{:S(2)}) %collective-permute-start.11) | collective-permute-done | bytes 139296 | tf_op jit(solution)/shard_map/ppermute | solution.py:241
  50.9 1.3 %collective-permute-done.16.other_ref = bf16[256,256]{1,0:T(8,128)(2,1)S(1)} collective-permute-done((bf16[256,256]{1,0:T(8,128)(2,1)S(1)}, bf16[256,256]{1,0:T(8,128)(2,1)S(1)}, u32[]{:S(2)}, u32[]{:S(2)}) %collective-permute-start.16) | collective-permute-done | bytes 131104 | tf_op jit(solution)/shard_map/ppermute | solution.py:241
  57.3 3.2 %collective-permute-done.23.got_ref = bf16[32,2688]{1,0:T(8,128)(2,1)S(1)} collective-permute-done((bf16[32,2688]{1,0:T(8,128)(2,1)S(1)}, bf16[32,2688]{1,0:T(8,128)(2,1)S(1)}, u32[]{:S(2)}, u32[]{:S(2)}) %collective-permute-start.23) | collective-permute-done | bytes 172064 | tf_op jit(solution)/shard_map/ppermute | solution.py:241
  61.2 3.0 %collective-permute-done.21.got_ref = bf16[32,2688]{1,0:T(8,128)(2,1)S(1)} collective-permute-done((bf16[32,2688]{1,0:T(8,128)(2,1)S(1)}, bf16[32,2688]{1,0:T(8,128)(2,1)S(1)}, u32[]{:S(2)}, u32[]{:S(2)}) %collective-permute-start.21) | collective-permute-done | bytes 172064 | tf_op jit(solution)/shard_map/ppermute | solution.py:241
  64.6 3.3 %collective-permute-done.19.got_ref = bf16[32,2688]{1,0:T(8,128)(2,1)S(1)} collective-permute-done((bf16[32,2688]{1,0:T(8,128)(2,1)S(1)}, bf16[32,2688]{1,0:T(8,128)(2,1)S(1)}, u32[]{:S(2)}, u32[]{:S(2)}) %collective-permute-start.19) | collective-permute-done | bytes 172064 | tf_op jit(solution)/shard_map/ppermute | solution.py:241
  67.9 1.3 %collective-permute-start.20 = (bf16[32,2688]{1,0:T(8,128)(2,1)S(1)}, bf16[32,2688]{1,0:T(8,128)(2,1)S(1)}, u32[]{:S(2)}, u32[]{:S(2)}) collective-permute-start(bf16[32,2688]{1,0:T(8,128)(2,1)S(1)} %shard_map.71), channel_id=1, source_target_pairs={{0,12},{1,13},{2,14},{3,15},{4,8},{5,9},{6,10},{7,11},{8,4},{9,5},... | collective-permute-start | bytes 516104 | tf_op jit(solution)/shard_map/ppermute | solution.py:241
  69.1 1.6 %collective-permute-done.18.got_ref = bf16[32,2688]{1,0:T(8,128)(2,1)S(1)} collective-permute-done((bf16[32,2688]{1,0:T(8,128)(2,1)S(1)}, bf16[32,2688]{1,0:T(8,128)(2,1)S(1)}, u32[]{:S(2)}, u32[]{:S(2)}) %collective-permute-start.18) | collective-permute-done | bytes 172064 | tf_op jit(solution)/shard_map/ppermute | solution.py:241
  70.7 7.2 %collective-permute-done.22.refs_1_ = bf16[32,2688]{1,0:T(8,128)(2,1)S(1)} collective-permute-done((bf16[32,2688]{1,0:T(8,128)(2,1)S(1)}, bf16[32,2688]{1,0:T(8,128)(2,1)S(1)}, u32[]{:S(2)}, u32[]{:S(2)}) %collective-permute-start.22) | collective-permute-done | bytes 172064 | tf_op jit(solution)/shard_map/ppermute | solution.py:241
  78.2 1.3 %collective-permute-done.25.other_ref = bf16[16,2688]{1,0:T(8,128)(2,1)S(1)} collective-permute-done((bf16[16,2688]{1,0:T(8,128)(2,1)S(1)}, bf16[16,2688]{1,0:T(8,128)(2,1)S(1)}, u32[]{:S(2)}, u32[]{:S(2)}) %collective-permute-start.25) | collective-permute-done | bytes 86048 | tf_op jit(solution)/shard_map/ppermute | solution.py:241
  (51 shorter events, 16.0 us)
Async XLA Ops:
  1.9 50.3 %collective-permute-start.17 = (bf16[256,2688]{1,0:T(8,128)(2,1)S(1)}, bf16[256,2688]{1,0:T(8,128)(2,1)S(1)}, u32[]{:S(2)}, u32[]{:S(2)}) collective-permute-start(bf16[256,2688]{1,0:T(8,128)(2,1)S(1)} %shard_map.69), channel_id=1, source_target_pairs={{0,1},{1,0},{2,3},{3,2},{4,5},{5,4},{6,7},{7,6},{8,9},{9,8},{10,11... | collective-permute-start | bytes 4128776 | tf_op jit(solution)/shard_map/ppermute | solution.py:241
  3.9 3.4 %collective-permute-start = (bf16[4,16,256]{2,1,0:T(8,128)(2,1)S(1)}, bf16[4,16,256]{2,1,0:T(8,128)(2,1)S(1)}, u32[]{:S(2)}, u32[]{:S(2)}) collective-permute-start(bf16[4,16,256]{2,1,0:T(8,128)(2,1)S(1)} %get-tuple-element.30), channel_id=1, source_target_pairs={{0,1},{1,0},{2,3},{3,2},{4,5},{5,4},{6,7},{7,6},{8,9},{9,8},{10,11... | collective-permute-start | bytes 98312 | tf_op jit(solution)/shard_map/ppermute | solution.py:241
  4.5 4.6 %collective-permute-start.1 = (bf16[4,16,256]{2,1,0:T(8,128)(2,1)S(1)}, bf16[4,16,256]{2,1,0:T(8,128)(2,1)S(1)}, u32[]{:S(2)}, u32[]{:S(2)}) collective-permute-start(bf16[4,16,256]{2,1,0:T(8,128)(2,1)S(1)} %get-tuple-element.31), channel_id=1, source_target_pairs={{0,2},{1,3},{2,0},{3,1},{4,6},{5,7},{6,4},{7,5},{8,10},{9,11},{10,... | collective-permute-start | bytes 98312 | tf_op jit(solution)/shard_map/ppermute | solution.py:241
  7.0 3.4 %collective-permute-start.2 = (bf16[4,16,256]{2,1,0:T(8,128)(2,1)S(1)}, bf16[4,16,256]{2,1,0:T(8,128)(2,1)S(1)}, u32[]{:S(2)}, u32[]{:S(2)}) collective-permute-start(bf16[4,16,256]{2,1,0:T(8,128)(2,1)S(1)} %get-tuple-element.32), channel_id=1, source_target_pairs={{0,3},{1,2},{2,1},{3,0},{4,7},{5,6},{6,5},{7,4},{8,11},{9,10},{10,... | collective-permute-start | bytes 98312 | tf_op jit(solution)/shard_map/ppermute | solution.py:241
  7.1 24.0 %collective-permute-start.6 = (bf16[4,528,128]{2,1,0:T(8,128)(2,1)S(1)}, bf16[4,528,128]{2,1,0:T(8,128)(2,1)S(1)}, u32[]{:S(2)}, u32[]{:S(2)}) collective-permute-start(bf16[4,528,128]{2,1,0:T(8,128)(2,1)S(1)} %get-tuple-element.34), channel_id=1, source_target_pairs={{0,1},{1,0},{2,3},{3,2},{4,5},{5,4},{6,7},{7,6},{8,9},{9,8},{10,11... | collective-permute-start | bytes 1622024 | tf_op jit(solution)/shard_map/ppermute | solution.py:241
  10.4 5.6 %collective-permute-start.3 = (bf16[4,4,16,256]{3,2,1,0:T(8,128)(2,1)S(1)}, bf16[4,4,16,256]{3,2,1,0:T(8,128)(2,1)S(1)}, u32[]{:S(2)}, u32[]{:S(2)}) collective-permute-start(bf16[4,4,16,256]{3,2,1,0:T(8,128)(2,1)S(1)} %pad_maximum_fusion.refs_0_), channel_id=1, source_target_pairs={{0,4},{1,5},{2,6},{3,7},{4,0},{5,1},{6,2},{7,3},{8,12},{9,13},{10,... | collective-permute-start | bytes 393224 | tf_op jit(solution)/shard_map/ppermute | solution.py:241
  12.1 16.4 %collective-permute-start.12 = (bf16[2,528,128]{2,1,0:T(8,128)(2,1)S(1)}, bf16[2,528,128]{2,1,0:T(8,128)(2,1)S(1)}, u32[]{:S(2)}, u32[]{:S(2)}) collective-permute-start(bf16[2,528,128]{2,1,0:T(8,128)(2,1)S(1)} %get-tuple-element.39), channel_id=1, source_target_pairs={{0,2},{1,3},{2,0},{3,1},{4,6},{5,7},{6,4},{7,5},{8,10},{9,11},{10,... | collective-permute-start | bytes 811016 | tf_op jit(solution)/shard_map/ppermute | solution.py:241
  12.9 8.7 %collective-permute-start.4 = (bf16[4,4,16,256]{3,2,1,0:T(8,128)(2,1)S(1)}, bf16[4,4,16,256]{3,2,1,0:T(8,128)(2,1)S(1)}, u32[]{:S(2)}, u32[]{:S(2)}) collective-permute-start(bf16[4,4,16,256]{3,2,1,0:T(8,128)(2,1)S(1)} %pad_maximum_fusion.refs_0_), channel_id=1, source_target_pairs={{0,8},{1,9},{2,10},{3,11},{4,12},{5,13},{6,14},{7,15},{8,0},{9,1},... | collective-permute-start | bytes 393224 | tf_op jit(solution)/shard_map/ppermute | solution.py:241
  16.1 13.5 %collective-permute-start.13 = (bf16[2,528,128]{2,1,0:T(8,128)(2,1)S(1)}, bf16[2,528,128]{2,1,0:T(8,128)(2,1)S(1)}, u32[]{:S(2)}, u32[]{:S(2)}) collective-permute-start(bf16[2,528,128]{2,1,0:T(8,128)(2,1)S(1)} %get-tuple-element.40), channel_id=1, source_target_pairs={{0,3},{1,2},{2,1},{3,0},{4,7},{5,6},{6,5},{7,4},{8,11},{9,10},{10,... | collective-permute-start | bytes 811016 | tf_op jit(solution)/shard_map/ppermute | solution.py:241
  21.6 6.8 %collective-permute-start.5 = (bf16[4,4,16,256]{3,2,1,0:T(8,128)(2,1)S(1)}, bf16[4,4,16,256]{3,2,1,0:T(8,128)(2,1)S(1)}, u32[]{:S(2)}, u32[]{:S(2)}) collective-permute-start(bf16[4,4,16,256]{3,2,1,0:T(8,128)(2,1)S(1)} %pad_maximum_fusion.refs_0_), channel_id=1, source_target_pairs={{0,12},{1,13},{2,14},{3,15},{4,8},{5,9},{6,10},{7,11},{8,4},{9,5},... | collective-permute-start | bytes 393224 | tf_op jit(solution)/shard_map/ppermute | solution.py:241
  28.4 6.3 %collective-permute-start.10 = (bf16[1,528,128]{2,1,0:T(8,128)(2,1)S(1)}, bf16[1,528,128]{2,1,0:T(8,128)(2,1)S(1)}, u32[]{:S(2)}, u32[]{:S(2)}) collective-permute-start(bf16[1,528,128]{2,1,0:T(8,128)(2,1)S(1)} %get-tuple-element.38), channel_id=1, source_target_pairs={{0,3},{1,2},{2,1},{3,0},{4,7},{5,6},{6,5},{7,4},{8,11},{9,10},{10,... | collective-permute-start | bytes 405512 | tf_op jit(solution)/shard_map/ppermute | solution.py:241
  28.4 8.1 %collective-permute-start.9 = (bf16[1,528,128]{2,1,0:T(8,128)(2,1)S(1)}, bf16[1,528,128]{2,1,0:T(8,128)(2,1)S(1)}, u32[]{:S(2)}, u32[]{:S(2)}) collective-permute-start(bf16[1,528,128]{2,1,0:T(8,128)(2,1)S(1)} %get-tuple-element.37), channel_id=1, source_target_pairs={{0,2},{1,3},{2,0},{3,1},{4,6},{5,7},{6,4},{7,5},{8,10},{9,11},{10,... | collective-permute-start | bytes 405512 | tf_op jit(solution)/shard_map/ppermute | solution.py:241
  29.6 11.1 %collective-permute-start.7 = (bf16[1,528,128]{2,1,0:T(8,128)(2,1)S(1)}, bf16[1,528,128]{2,1,0:T(8,128)(2,1)S(1)}, u32[]{:S(2)}, u32[]{:S(2)}) collective-permute-start(bf16[1,528,128]{2,1,0:T(8,128)(2,1)S(1)} %get-tuple-element.35), channel_id=1, source_target_pairs={{0,2},{1,3},{2,0},{3,1},{4,6},{5,7},{6,4},{7,5},{8,10},{9,11},{10,... | collective-permute-start | bytes 405512 | tf_op jit(solution)/shard_map/ppermute | solution.py:241
  31.1 11.6 %collective-permute-start.8 = (bf16[1,528,128]{2,1,0:T(8,128)(2,1)S(1)}, bf16[1,528,128]{2,1,0:T(8,128)(2,1)S(1)}, u32[]{:S(2)}, u32[]{:S(2)}) collective-permute-start(bf16[1,528,128]{2,1,0:T(8,128)(2,1)S(1)} %get-tuple-element.36), channel_id=1, source_target_pairs={{0,3},{1,2},{2,1},{3,0},{4,7},{5,6},{6,5},{7,4},{8,11},{9,10},{10,... | collective-permute-start | bytes 405512 | tf_op jit(solution)/shard_map/ppermute | solution.py:241
  34.7 12.8 %collective-permute-start.14 = (bf16[272,256]{1,0:T(8,128)(2,1)S(1)}, bf16[272,256]{1,0:T(8,128)(2,1)S(1)}, u32[]{:S(2)}, u32[]{:S(2)}) collective-permute-start(bf16[272,256]{1,0:T(8,128)(2,1)S(1)} %get-tuple-element.41), channel_id=1, source_target_pairs={{0,8},{1,9},{2,10},{3,11},{4,12},{5,13},{6,14},{7,15},{8,0},{9,1},... | collective-permute-start | bytes 417800 | tf_op jit(solution)/shard_map/ppermute | solution.py:241
  36.6 11.0 %collective-permute-start.15 = (bf16[272,256]{1,0:T(8,128)(2,1)S(1)}, bf16[272,256]{1,0:T(8,128)(2,1)S(1)}, u32[]{:S(2)}, u32[]{:S(2)}) collective-permute-start(bf16[272,256]{1,0:T(8,128)(2,1)S(1)} %get-tuple-element.42), channel_id=1, source_target_pairs={{0,12},{1,13},{2,14},{3,15},{4,8},{5,9},{6,10},{7,11},{8,4},{9,5},... | collective-permute-start | bytes 417800 | tf_op jit(solution)/shard_map/ppermute | solution.py:241
  40.7 9.6 %collective-permute-start.11 = (bf16[272,256]{1,0:T(8,128)(2,1)S(1)}, bf16[272,256]{1,0:T(8,128)(2,1)S(1)}, u32[]{:S(2)}, u32[]{:S(2)}) collective-permute-start(bf16[272,256]{1,0:T(8,128)(2,1)S(1)} %shard_map.66), channel_id=1, source_target_pairs={{0,4},{1,5},{2,6},{3,7},{4,0},{5,1},{6,2},{7,3},{8,12},{9,13},{10,... | collective-permute-start | bytes 417800 | tf_op jit(solution)/shard_map/ppermute | solution.py:241
  53.2 7.3 %collective-permute-start.23 = (bf16[32,2688]{1,0:T(8,128)(2,1)S(1)}, bf16[32,2688]{1,0:T(8,128)(2,1)S(1)}, u32[]{:S(2)}, u32[]{:S(2)}) collective-permute-start(bf16[32,2688]{1,0:T(8,128)(2,1)S(1)} %get-tuple-element.50), channel_id=1, source_target_pairs={{0,2},{1,3},{2,0},{3,1},{4,6},{5,7},{6,4},{7,5},{8,10},{9,11},{10,... | collective-permute-start | bytes 516104 | tf_op jit(solution)/shard_map/ppermute | solution.py:241
  54.1 10.1 %collective-permute-start.21 = (bf16[32,2688]{1,0:T(8,128)(2,1)S(1)}, bf16[32,2688]{1,0:T(8,128)(2,1)S(1)}, u32[]{:S(2)}, u32[]{:S(2)}) collective-permute-start(bf16[32,2688]{1,0:T(8,128)(2,1)S(1)} %get-tuple-element.48), channel_id=1, source_target_pairs={{0,2},{1,3},{2,0},{3,1},{4,6},{5,7},{6,4},{7,5},{8,10},{9,11},{10,... | collective-permute-start | bytes 516104 | tf_op jit(solution)/shard_map/ppermute | solution.py:241
  55.3 12.6 %collective-permute-start.19 = (bf16[32,2688]{1,0:T(8,128)(2,1)S(1)}, bf16[32,2688]{1,0:T(8,128)(2,1)S(1)}, u32[]{:S(2)}, u32[]{:S(2)}) collective-permute-start(bf16[32,2688]{1,0:T(8,128)(2,1)S(1)} %get-tuple-element.46), channel_id=1, source_target_pairs={{0,2},{1,3},{2,0},{3,1},{4,6},{5,7},{6,4},{7,5},{8,10},{9,11},{10,... | collective-permute-start | bytes 516104 | tf_op jit(solution)/shard_map/ppermute | solution.py:241
  56.1 14.6 %collective-permute-start.18 = (bf16[32,2688]{1,0:T(8,128)(2,1)S(1)}, bf16[32,2688]{1,0:T(8,128)(2,1)S(1)}, u32[]{:S(2)}, u32[]{:S(2)}) collective-permute-start(bf16[32,2688]{1,0:T(8,128)(2,1)S(1)} %get-tuple-element.44), channel_id=1, source_target_pairs={{0,2},{1,3},{2,0},{3,1},{4,6},{5,7},{6,4},{7,5},{8,10},{9,11},{10,... | collective-permute-start | bytes 516104 | tf_op jit(solution)/shard_map/ppermute | solution.py:241
  60.5 10.2 %collective-permute-start.24 = (bf16[32,2688]{1,0:T(8,128)(2,1)S(1)}, bf16[32,2688]{1,0:T(8,128)(2,1)S(1)}, u32[]{:S(2)}, u32[]{:S(2)}) collective-permute-start(bf16[32,2688]{1,0:T(8,128)(2,1)S(1)} %shard_map.73), channel_id=1, source_target_pairs={{0,4},{1,5},{2,6},{3,7},{4,0},{5,1},{6,2},{7,3},{8,12},{9,13},{10,... | collective-permute-start | bytes 516104 | tf_op jit(solution)/shard_map/ppermute | solution.py:241
  64.2 13.7 %collective-permute-start.22 = (bf16[32,2688]{1,0:T(8,128)(2,1)S(1)}, bf16[32,2688]{1,0:T(8,128)(2,1)S(1)}, u32[]{:S(2)}, u32[]{:S(2)}) collective-permute-start(bf16[32,2688]{1,0:T(8,128)(2,1)S(1)} %shard_map.72), channel_id=1, source_target_pairs={{0,8},{1,9},{2,10},{3,11},{4,12},{5,13},{6,14},{7,15},{8,0},{9,1},... | collective-permute-start | bytes 516104 | tf_op jit(solution)/shard_map/ppermute | solution.py:241
  67.9 10.1 %collective-permute-start.20 = (bf16[32,2688]{1,0:T(8,128)(2,1)S(1)}, bf16[32,2688]{1,0:T(8,128)(2,1)S(1)}, u32[]{:S(2)}, u32[]{:S(2)}) collective-permute-start(bf16[32,2688]{1,0:T(8,128)(2,1)S(1)} %shard_map.71), channel_id=1, source_target_pairs={{0,12},{1,13},{2,14},{3,15},{4,8},{5,9},{6,10},{7,11},{8,4},{9,5},... | collective-permute-start | bytes 516104 | tf_op jit(solution)/shard_map/ppermute | solution.py:241
  (7 other events, 21.7 us)

commit v2 on v1

--- a/solution.py
+++ b/solution.py
@@ -12,6 +12,7 @@
 KEY_VALUE_HEADS = 16
 HEAD_SIZE = 128
 INNER = 4
+SIDES = INNER // 2
 CHUNKS = 3
 
 score_scale = 168.0 ** (-0.5)
@@ -53,16 +54,32 @@
     )(*ins)
 
 
-def split_kernel(live_ref, q_ref, k_ref, v_ref, *refs, outer, width, groups, copies):
+def split_kernel(live_ref, q_hbm, k_hbm, v_hbm, *refs, outer, width, groups, copies):
     _, z, r = place()
-    q_outs = refs[:INNER]
-    kv_outs = refs[INNER:]
+    pair_out = refs[0]
+    q_outs = refs[1:1 + SIDES]
+    kv_outs = refs[1 + SIDES:1 + SIDES + len(groups)]
+    q_ref, k_ref, v_ref, sems = refs[1 + SIDES + len(groups):]
+    loads = [
+        pltpu.make_async_copy(source, target, sems.at[i])
+        for i, (source, target) in enumerate(((q_hbm, q_ref), (k_hbm, k_ref), (v_hbm, v_ref)))
+    ]
+    for load in loads:
+        load.start()
     keys = k_ref.shape[0]
     live = jnp.full((16, HEAD_SIZE), live_ref[0], jnp.int32).astype(f32).astype(bf16)
-    for k, out in enumerate(q_outs):
+    loads[0].wait()
+    for j in range(SIDES):
         for zz in range(outer):
-            col = pl.multiple_of((zz * INNER + lax.bitwise_xor(r, k)) * width, width)
-            out[zz] = q_ref[:, pl.ds(col, width)]
+            for k in range(2):
+                group = zz * INNER + lax.bitwise_xor(r, 2 * j + k)
+                piece = q_ref[:, pl.ds(pl.multiple_of(group * width, width), width)]
+                if k:
+                    pair_out[j, zz] = piece
+                else:
+                    q_outs[j][zz] = piece
+    loads[1].wait()
+    loads[2].wait()
     for (k, offsets), out in zip(groups, kv_outs):
         for i, kk in enumerate(offsets):
             head = lax.bitwise_xor(z, kk) * INNER + lax.bitwise_xor(r, k)
@@ -79,12 +96,12 @@
     out_ref[...] = w_ref[:, pl.ds(col, half)]
 
 
-def attention_kernel(first_ref, *refs, outer, first, offsets, rows_all, keys, heads, width):
-    ys = refs[:outer]
-    kvs = refs[outer:outer + INNER]
-    begin = [first, first] + [0] * (INNER - 2)
-    outs = refs[outer + INNER:outer + INNER + len(offsets)]
-    bias_ref, q_ref = refs[outer + INNER + len(offsets):]
+def attention_kernel(first_ref, *refs, outer, begin, offsets, rows_all, keys, heads, width):
+    pieces = outer * SIDES
+    ys = refs[:pieces]
+    kvs = refs[pieces:pieces + INNER]
+    outs = refs[pieces + INNER:pieces + INNER + len(offsets)]
+    bias_ref, q_ref = refs[pieces + INNER + len(offsets):]
     _, z, r = place()
     rows = rows_all // (outer * INNER)
     q_pos = first_ref[0] + lax.broadcasted_iota(jnp.int32, (rows_all, keys), 0)
@@ -103,7 +120,7 @@
             for k in range(INNER):
                 src = lax.bitwise_xor(z, k2) * INNER + lax.bitwise_xor(r, k)
                 at = pl.multiple_of(src * rows, rows)
-                q_ref[pl.ds(at, rows), :] = ys[k2][k, zz].astype(f32)
+                q_ref[pl.ds(at, rows), :] = ys[k2 * SIDES + k // 2][k % 2, zz].astype(f32)
         stats = jnp.zeros((rows_all, 128), f32)
         for h in range(heads):
             cols = slice(h * HEAD_SIZE, (h + 1) * HEAD_SIZE)
@@ -240,25 +257,37 @@
     def swap(x, k):
         return lax.ppermute(x, "seq", [(i, i ^ k) for i in range(devices)])
 
-    order = list(range(outer - 1, -1, -1))
+    far_first = list(range(outer - 1, -1, -1))
+    order = [outer - 1, 1] + far_first[1:-2] + [0]
     phases = [order[:outer // 2], order[outer // 2:3 * outer // 4], order[3 * outer // 4:]]
     groups = [(0, order), (1, order)] + [(k, p) for p in phases for k in range(2, INNER)]
-    outs = [shape((outer, rows, width), bf16)] * INNER + [
+    outs = [shape((SIDES, outer, rows, width), bf16)] + [shape((outer, rows, width), bf16)] * SIDES
+    outs += [
         shape((len(p), 2 * keys + 16, HEAD_SIZE), bf16) for k, p in groups
     ]
-    split = call(
+    inputs = [query_block, cache_keys, stored_values]
+    split = pl.pallas_call(
         functools.partial(split_kernel, outer=outer, width=width, groups=groups, copies=copies),
-        [live_counts, query_block, cache_keys, stored_values], outs, scalars=1,
-    )
-    q_out, kv_out = split[:INNER], split[INNER:]
-    q_got = {k: swap(q_out[k], k) for k in (2, 3, 1)}
+        out_shape=tuple(outs),
+        in_specs=[sspec()] + [pl.BlockSpec(memory_space=pltpu.MemorySpace.HBM)] * 3,
+        out_specs=tuple(vspec() for _ in outs),
+        scratch_shapes=[pltpu.VMEM(x.shape, x.dtype) for x in inputs]
+        + [pltpu.SemaphoreType.DMA((3,))],
+        name="split",
+        compiler_params=pltpu.CompilerParams(vmem_limit_bytes=8 << 20),
+    )(live_counts, *inputs)
+    q_own, kv_out = split[1:1 + SIDES], split[1 + SIDES:]
+    q_pair = swap(split[0], 1)
     kv_pair = swap(kv_out[1], 1)
     kv_far = [
         {k: swap(kv_out[2 + 2 * i + k - 2], k) for k in range(2, INNER)}
         for i in range(len(phases))
     ]
-    inner_q = jnp.stack([q_out[0], q_got[1], q_got[2], q_got[3]])
-    ys = [inner_q] + [swap(inner_q, k * INNER) for k in range(1, outer)]
+    pair_q = [jnp.stack([q_own[j], q_pair[j]]) for j in range(SIDES)]
+    ys = [
+        swap(pair_q[j], k * INNER + 2 * j) if k or j else pair_q[0]
+        for k in range(outer) for j in range(SIDES)
+    ]
 
     (w_send,) = call(
         split_weight_kernel, [out_weight],
@@ -267,22 +296,20 @@
     w_other = swap(w_send, 1)
 
     partial_of = {}
-    at = 0
-    for i, offsets in enumerate(phases):
-        size = len(offsets)
-        outs = call(
+    for near, kk in enumerate(order):
+        i = [kk in p for p in phases].index(True)
+        far = phases[i].index(kk)
+        (out,) = call(
             functools.partial(
-                attention_kernel, outer=outer, first=at, offsets=offsets, rows_all=rows_all,
-                keys=keys, heads=heads, width=width,
+                attention_kernel, outer=outer, begin=(near, near) + (far,) * (INNER - 2),
+                offsets=[kk], rows_all=rows_all, keys=keys, heads=heads, width=width,
             ),
             [first_position, *ys, kv_out[0], kv_pair, kv_far[i][2], kv_far[i][3]],
-            [shape((rows_all + 16, width), bf16)] * size,
+            [shape((rows_all + 16, width), bf16)],
             scratch=[pltpu.VMEM((rows_all, INNER * keys), f32), pltpu.VMEM((rows_all, width), f32)],
-            scalars=1, flops=4 * rows_all * INNER * keys * width * size, limit=20,
+            scalars=1, flops=4 * rows_all * INNER * keys * width, limit=16,
         )
-        at += size
-        for kk, out in zip(offsets, outs):
-            partial_of[kk] = swap(out, kk * INNER) if kk else out
+        partial_of[kk] = swap(out, kk * INNER) if kk else out
 
     (merged,) = call(
         functools.partial(merge_kernel, sources=outer, rows_all=rows_all, heads=heads, width=width),
@@ -292,7 +319,7 @@
     other = swap(merged, 1)
 
     span = 2 * rows
-    term_groups = [[kk] for kk in order]
+    term_groups = [[kk] for kk in far_first]
     terms = call(
         functools.partial(project_kernel, groups=term_groups, rows=rows, blocks=blocks),
         [merged, other, out_weight, w_other],
@@ -303,7 +330,7 @@
     sends, keeps = terms[:outer], terms[outer:]
     gots = [swap(x, 2) for x in sends]
     parts = []
-    for i, kk in enumerate(order[:-1]):
+    for i, kk in enumerate(far_first[:-1]):
         (part,) = call(first_sum_kernel, [keeps[i], gots[i]], [shape((span, half), bf16)])
         parts.append(swap(part, kk * INNER))
     mine, theirs = call(

time: 81.2 us -> 93.3 us (1.15)
  starting transfers between devices: 24.5 us -> 38.6 us
  waiting for transfers between devices: 44.3 us -> 41.6 us
    ppermute x26 -> x28, starting transfers between devices: 24.5 us -> 38.6 us  [swap(): return lax.ppermute(x, 'seq', [(i, i ^ k) for i in range(devices)])]
    ppermute x26 -> x28, waiting for transfers between devices: 44.3 us -> 41.6 us  [swap(): return lax.ppermute(x, 'seq', [(i, i ^ k) for i in range(devices)])]
  transfers between devices with their start and end apart: 26 -> 28, of which waited for: 16 -> 17; matrix products, arithmetic and copies ran while one was open for 0% -> 0% of each run, Pallas kernels for 7% -> 7%
where the time goes in v2:
time: 93.3 us; the launch traced here: 92 us
  waiting for transfers between devices  41.6 us (45%)
  starting transfers between devices  38.6 us (41%)
  Pallas kernels  8.3 us (9%)
  local copies, waits for them, and re-layouts  1.98 us (2%)
  between operations  1.5 us (2%)
    ppermute x28, waiting for transfers between devices, swap(): return lax.ppermute(x, 'seq', [(i, i ^ k) for i in range(devices)])  41.6 us
    ppermute x28, starting transfers between devices, swap(): return lax.ppermute(x, 'seq', [(i, i ^ k) for i in range(devices)])  38.6 us
    pallas_call x12, Pallas kernels, call(): pl.pallas_call(kernel, out_shape=tuple(outs), in_specs=in_specs, out_spec...  7.4 us
    unnamed x10, local copies, waits for them, and re-layouts  1.98 us
  transfers between devices with their start and end apart: 28, of which 17 were waited for; matrix products, arithmetic and copies ran while one was open for 0% of the time, Pallas kernels for 7%

profile of v2, /device:TPU:0, one launch (start us, length us, event | category | flops | bytes accessed | tf_op | source)
XLA Modules:
  0.0 92.0 jit_solution(5930817624238147409)
XLA Ops:
  0.0 1.8 %copy-done = bf16[256,5376]{1,0:T(8,128)(2,1)S(1)} copy-done((bf16[256,5376]{1,0:T(8,128)(2,1)S(1)}, bf16[256,5376]{1,0:T(8,128)(2,1)}, u32[]{:S(2)}) %copy-start) | copy-done | bytes 2752536
  5.7 3.0 %collective-permute-start.2 = (bf16[2,4,16,256]{3,2,1,0:T(8,128)(2,1)S(1)}, bf16[2,4,16,256]{3,2,1,0:T(8,128)(2,1)S(1)}, u32[]{:S(2)}, u32[]{:S(2)}) collective-permute-start(bf16[2,4,16,256]{3,2,1,0:T(8,128)(2,1)S(1)} %pad_maximum_fusion.refs_0_), channel_id=1, source_target_pairs={{0,4},{1,5},{2,6},{3,7},{4,0},{5,1},{6,2},{7,3},{8,12},{9,13},{10,... | collective-permute-start | bytes 196616 | tf_op jit(solution)/shard_map/ppermute | solution.py:258
  8.7 1.5 %collective-permute-start.11 = (bf16[2,528,128]{2,1,0:T(8,128)(2,1)S(1)}, bf16[2,528,128]{2,1,0:T(8,128)(2,1)S(1)}, u32[]{:S(2)}, u32[]{:S(2)}) collective-permute-start(bf16[2,528,128]{2,1,0:T(8,128)(2,1)S(1)} %get-tuple-element.33), channel_id=1, source_target_pairs={{0,2},{1,3},{2,0},{3,1},{4,6},{5,7},{6,4},{7,5},{8,10},{9,11},{10,... | collective-permute-start | bytes 811016 | tf_op jit(solution)/shard_map/ppermute | solution.py:258
  10.2 2.6 %collective-permute-start.4 = (bf16[2,4,16,256]{3,2,1,0:T(8,128)(2,1)S(1)}, bf16[2,4,16,256]{3,2,1,0:T(8,128)(2,1)S(1)}, u32[]{:S(2)}, u32[]{:S(2)}) collective-permute-start(bf16[2,4,16,256]{3,2,1,0:T(8,128)(2,1)S(1)} %pad_maximum_fusion.refs_0_), channel_id=1, source_target_pairs={{0,8},{1,9},{2,10},{3,11},{4,12},{5,13},{6,14},{7,15},{8,0},{9,1},... | collective-permute-start | bytes 196616 | tf_op jit(solution)/shard_map/ppermute | solution.py:258
  12.8 2.2 %collective-permute-start.6 = (bf16[2,4,16,256]{3,2,1,0:T(8,128)(2,1)S(1)}, bf16[2,4,16,256]{3,2,1,0:T(8,128)(2,1)S(1)}, u32[]{:S(2)}, u32[]{:S(2)}) collective-permute-start(bf16[2,4,16,256]{3,2,1,0:T(8,128)(2,1)S(1)} %pad_maximum_fusion.refs_0_), channel_id=1, source_target_pairs={{0,12},{1,13},{2,14},{3,15},{4,8},{5,9},{6,10},{7,11},{8,4},{9,5},... | collective-permute-start | bytes 196616 | tf_op jit(solution)/shard_map/ppermute | solution.py:258
  15.0 1.7 %collective-permute-done.4.refs_4_ = bf16[2,4,16,256]{3,2,1,0:T(8,128)(2,1)S(1)} collective-permute-done((bf16[2,4,16,256]{3,2,1,0:T(8,128)(2,1)S(1)}, bf16[2,4,16,256]{3,2,1,0:T(8,128)(2,1)S(1)}, u32[]{:S(2)}, u32[]{:S(2)}) %collective-permute-start.4) | collective-permute-done | bytes 65568 | tf_op jit(solution)/shard_map/ppermute | solution.py:258
  17.5 1.3 %collective-permute-done.6.refs_6_ = bf16[2,4,16,256]{3,2,1,0:T(8,128)(2,1)S(1)} collective-permute-done((bf16[2,4,16,256]{3,2,1,0:T(8,128)(2,1)S(1)}, bf16[2,4,16,256]{3,2,1,0:T(8,128)(2,1)S(1)}, u32[]{:S(2)}, u32[]{:S(2)}) %collective-permute-start.6) | collective-permute-done | bytes 65568 | tf_op jit(solution)/shard_map/ppermute | solution.py:258
  18.9 2.1 %collective-permute-done.1.refs_1_ = bf16[2,4,16,256]{3,2,1,0:T(8,128)(2,1)S(1)} collective-permute-done((bf16[2,4,16,256]{3,2,1,0:T(8,128)(2,1)S(1)}, bf16[2,4,16,256]{3,2,1,0:T(8,128)(2,1)S(1)}, u32[]{:S(2)}, u32[]{:S(2)}) %collective-permute-start.1) | collective-permute-done | bytes 65568 | tf_op jit(solution)/shard_map/ppermute | solution.py:258
  21.6 4.7 %collective-permute-done.3.refs_3_ = bf16[2,4,16,256]{3,2,1,0:T(8,128)(2,1)S(1)} collective-permute-done((bf16[2,4,16,256]{3,2,1,0:T(8,128)(2,1)S(1)}, bf16[2,4,16,256]{3,2,1,0:T(8,128)(2,1)S(1)}, u32[]{:S(2)}, u32[]{:S(2)}) %collective-permute-start.3) | collective-permute-done | bytes 65568 | tf_op jit(solution)/shard_map/ppermute | solution.py:258
  26.2 3.9 %collective-permute-start.5 = (bf16[2,4,16,256]{3,2,1,0:T(8,128)(2,1)S(1)}, bf16[2,4,16,256]{3,2,1,0:T(8,128)(2,1)S(1)}, u32[]{:S(2)}, u32[]{:S(2)}) collective-permute-start(bf16[2,4,16,256]{3,2,1,0:T(8,128)(2,1)S(1)} %pad_maximum_fusion.1), channel_id=1, source_target_pairs={{0,10},{1,11},{2,8},{3,9},{4,14},{5,15},{6,12},{7,13},{8,2},{9,3},... | collective-permute-start | bytes 196616 | tf_op jit(solution)/shard_map/ppermute | solution.py:258
  30.1 3.0 %collective-permute-done.5.refs_5_ = bf16[2,4,16,256]{3,2,1,0:T(8,128)(2,1)S(1)} collective-permute-done((bf16[2,4,16,256]{3,2,1,0:T(8,128)(2,1)S(1)}, bf16[2,4,16,256]{3,2,1,0:T(8,128)(2,1)S(1)}, u32[]{:S(2)}, u32[]{:S(2)}) %collective-permute-start.5) | collective-permute-done | bytes 65568 | tf_op jit(solution)/shard_map/ppermute | solution.py:258
  33.1 5.4 %collective-permute-start.7 = (bf16[2,4,16,256]{3,2,1,0:T(8,128)(2,1)S(1)}, bf16[2,4,16,256]{3,2,1,0:T(8,128)(2,1)S(1)}, u32[]{:S(2)}, u32[]{:S(2)}) collective-permute-start(bf16[2,4,16,256]{3,2,1,0:T(8,128)(2,1)S(1)} %pad_maximum_fusion.1), channel_id=1, source_target_pairs={{0,14},{1,15},{2,12},{3,13},{4,10},{5,11},{6,8},{7,9},{8,6},{9,7},... | collective-permute-start | bytes 196616 | tf_op jit(solution)/shard_map/ppermute | solution.py:258
  38.5 2.2 %collective-permute-done.7.refs_7_ = bf16[2,4,16,256]{3,2,1,0:T(8,128)(2,1)S(1)} collective-permute-done((bf16[2,4,16,256]{3,2,1,0:T(8,128)(2,1)S(1)}, bf16[2,4,16,256]{3,2,1,0:T(8,128)(2,1)S(1)}, u32[]{:S(2)}, u32[]{:S(2)}) %collective-permute-start.7) | collective-permute-done | bytes 65568 | tf_op jit(solution)/shard_map/ppermute | solution.py:258
  41.4 1.7 %collective-permute-start.10 = (bf16[1,528,128]{2,1,0:T(8,128)(2,1)S(1)}, bf16[1,528,128]{2,1,0:T(8,128)(2,1)S(1)}, u32[]{:S(2)}, u32[]{:S(2)}) collective-permute-start(bf16[1,528,128]{2,1,0:T(8,128)(2,1)S(1)} %get-tuple-element.32), channel_id=1, source_target_pairs={{0,3},{1,2},{2,1},{3,0},{4,7},{5,6},{6,5},{7,4},{8,11},{9,10},{10,... | collective-permute-start | bytes 405512 | tf_op jit(solution)/shard_map/ppermute | solution.py:258
  43.8 1.5 %collective-permute-start.9 = (bf16[1,528,128]{2,1,0:T(8,128)(2,1)S(1)}, bf16[1,528,128]{2,1,0:T(8,128)(2,1)S(1)}, u32[]{:S(2)}, u32[]{:S(2)}) collective-permute-start(bf16[1,528,128]{2,1,0:T(8,128)(2,1)S(1)} %get-tuple-element.31), channel_id=1, source_target_pairs={{0,2},{1,3},{2,0},{3,1},{4,6},{5,7},{6,4},{7,5},{8,10},{9,11},{10,... | collective-permute-start | bytes 405512 | tf_op jit(solution)/shard_map/ppermute | solution.py:258
  47.1 3.3 %collective-permute-start.17 = (bf16[272,256]{1,0:T(8,128)(2,1)S(1)}, bf16[272,256]{1,0:T(8,128)(2,1)S(1)}, u32[]{:S(2)}, u32[]{:S(2)}) collective-permute-start(bf16[272,256]{1,0:T(8,128)(2,1)S(1)} %shard_map.67), channel_id=1, source_target_pairs={{0,12},{1,13},{2,14},{3,15},{4,8},{5,9},{6,10},{7,11},{8,4},{9,5},... | collective-permute-start | bytes 417800 | tf_op jit(solution)/shard_map/ppermute | solution.py:258
  53.0 3.0 %collective-permute-start.13 = (bf16[272,256]{1,0:T(8,128)(2,1)S(1)}, bf16[272,256]{1,0:T(8,128)(2,1)S(1)}, u32[]{:S(2)}, u32[]{:S(2)}) collective-permute-start(bf16[272,256]{1,0:T(8,128)(2,1)S(1)} %shard_map.65), channel_id=1, source_target_pairs={{0,4},{1,5},{2,6},{3,7},{4,0},{5,1},{6,2},{7,3},{8,12},{9,13},{10,... | collective-permute-start | bytes 417800 | tf_op jit(solution)/shard_map/ppermute | solution.py:258
  57.2 3.8 %collective-permute-done.16.refs_2_ = bf16[272,256]{1,0:T(8,128)(2,1)S(1)} collective-permute-done((bf16[272,256]{1,0:T(8,128)(2,1)S(1)}, bf16[272,256]{1,0:T(8,128)(2,1)S(1)}, u32[]{:S(2)}, u32[]{:S(2)}) %collective-permute-start.16) | collective-permute-done | bytes 139296 | tf_op jit(solution)/shard_map/ppermute | solution.py:258
  61.0 1.4 %collective-permute-done.13.refs_1_ = bf16[272,256]{1,0:T(8,128)(2,1)S(1)} collective-permute-done((bf16[272,256]{1,0:T(8,128)(2,1)S(1)}, bf16[272,256]{1,0:T(8,128)(2,1)S(1)}, u32[]{:S(2)}, u32[]{:S(2)}) %collective-permute-start.13) | collective-permute-done | bytes 139296 | tf_op jit(solution)/shard_map/ppermute | solution.py:258
  69.4 3.2 %collective-permute-done.25.got_ref = bf16[32,2688]{1,0:T(8,128)(2,1)S(1)} collective-permute-done((bf16[32,2688]{1,0:T(8,128)(2,1)S(1)}, bf16[32,2688]{1,0:T(8,128)(2,1)S(1)}, u32[]{:S(2)}, u32[]{:S(2)}) %collective-permute-start.25) | collective-permute-done | bytes 172064 | tf_op jit(solution)/shard_map/ppermute | solution.py:258
  72.7 3.6 %collective-permute-done.23.got_ref = bf16[32,2688]{1,0:T(8,128)(2,1)S(1)} collective-permute-done((bf16[32,2688]{1,0:T(8,128)(2,1)S(1)}, bf16[32,2688]{1,0:T(8,128)(2,1)S(1)}, u32[]{:S(2)}, u32[]{:S(2)}) %collective-permute-start.23) | collective-permute-done | bytes 172064 | tf_op jit(solution)/shard_map/ppermute | solution.py:258
  76.9 3.1 %collective-permute-done.21.got_ref = bf16[32,2688]{1,0:T(8,128)(2,1)S(1)} collective-permute-done((bf16[32,2688]{1,0:T(8,128)(2,1)S(1)}, bf16[32,2688]{1,0:T(8,128)(2,1)S(1)}, u32[]{:S(2)}, u32[]{:S(2)}) %collective-permute-start.21) | collective-permute-done | bytes 172064 | tf_op jit(solution)/shard_map/ppermute | solution.py:258
  80.0 2.4 %collective-permute-start.22 = (bf16[32,2688]{1,0:T(8,128)(2,1)S(1)}, bf16[32,2688]{1,0:T(8,128)(2,1)S(1)}, u32[]{:S(2)}, u32[]{:S(2)}) collective-permute-start(bf16[32,2688]{1,0:T(8,128)(2,1)S(1)} %shard_map.71), channel_id=1, source_target_pairs={{0,12},{1,13},{2,14},{3,15},{4,8},{5,9},{6,10},{7,11},{8,4},{9,5},... | collective-permute-start | bytes 516104 | tf_op jit(solution)/shard_map/ppermute | solution.py:258
  82.8 7.0 %collective-permute-done.24.refs_1_ = bf16[32,2688]{1,0:T(8,128)(2,1)S(1)} collective-permute-done((bf16[32,2688]{1,0:T(8,128)(2,1)S(1)}, bf16[32,2688]{1,0:T(8,128)(2,1)S(1)}, u32[]{:S(2)}, u32[]{:S(2)}) %collective-permute-start.24) | collective-permute-done | bytes 172064 | tf_op jit(solution)/shard_map/ppermute | solution.py:258
  (58 shorter events, 21.3 us)
Async XLA Ops:
  1.9 62.4 %collective-permute-start.19 = (bf16[256,2688]{1,0:T(8,128)(2,1)S(1)}, bf16[256,2688]{1,0:T(8,128)(2,1)S(1)}, u32[]{:S(2)}, u32[]{:S(2)}) collective-permute-start(bf16[256,2688]{1,0:T(8,128)(2,1)S(1)} %shard_map.69), channel_id=1, source_target_pairs={{0,1},{1,0},{2,3},{3,2},{4,5},{5,4},{6,7},{7,6},{8,9},{9,8},{10,11... | collective-permute-start | bytes 4128776 | tf_op jit(solution)/shard_map/ppermute | solution.py:258
  5.7 7.1 %collective-permute-start.2 = (bf16[2,4,16,256]{3,2,1,0:T(8,128)(2,1)S(1)}, bf16[2,4,16,256]{3,2,1,0:T(8,128)(2,1)S(1)}, u32[]{:S(2)}, u32[]{:S(2)}) collective-permute-start(bf16[2,4,16,256]{3,2,1,0:T(8,128)(2,1)S(1)} %pad_maximum_fusion.refs_0_), channel_id=1, source_target_pairs={{0,4},{1,5},{2,6},{3,7},{4,0},{5,1},{6,2},{7,3},{8,12},{9,13},{10,... | collective-permute-start | bytes 196616 | tf_op jit(solution)/shard_map/ppermute | solution.py:258
  8.7 35.1 %collective-permute-start.8 = (bf16[4,528,128]{2,1,0:T(8,128)(2,1)S(1)}, bf16[4,528,128]{2,1,0:T(8,128)(2,1)S(1)}, u32[]{:S(2)}, u32[]{:S(2)}) collective-permute-start(bf16[4,528,128]{2,1,0:T(8,128)(2,1)S(1)} %get-tuple-element.30), channel_id=1, source_target_pairs={{0,1},{1,0},{2,3},{3,2},{4,5},{5,4},{6,7},{7,6},{8,9},{9,8},{10,11... | collective-permute-start | bytes 1622024 | tf_op jit(solution)/shard_map/ppermute | solution.py:258
  8.7 32.6 %collective-permute-start.11 = (bf16[2,528,128]{2,1,0:T(8,128)(2,1)S(1)}, bf16[2,528,128]{2,1,0:T(8,128)(2,1)S(1)}, u32[]{:S(2)}, u32[]{:S(2)}) collective-permute-start(bf16[2,528,128]{2,1,0:T(8,128)(2,1)S(1)} %get-tuple-element.33), channel_id=1, source_target_pairs={{0,2},{1,3},{2,0},{3,1},{4,6},{5,7},{6,4},{7,5},{8,10},{9,11},{10,... | collective-permute-start | bytes 811016 | tf_op jit(solution)/shard_map/ppermute | solution.py:258
  10.2 6.5 %collective-permute-start.4 = (bf16[2,4,16,256]{3,2,1,0:T(8,128)(2,1)S(1)}, bf16[2,4,16,256]{3,2,1,0:T(8,128)(2,1)S(1)}, u32[]{:S(2)}, u32[]{:S(2)}) collective-permute-start(bf16[2,4,16,256]{3,2,1,0:T(8,128)(2,1)S(1)} %pad_maximum_fusion.refs_0_), channel_id=1, source_target_pairs={{0,8},{1,9},{2,10},{3,11},{4,12},{5,13},{6,14},{7,15},{8,0},{9,1},... | collective-permute-start | bytes 196616 | tf_op jit(solution)/shard_map/ppermute | solution.py:258
  12.8 6.1 %collective-permute-start.6 = (bf16[2,4,16,256]{3,2,1,0:T(8,128)(2,1)S(1)}, bf16[2,4,16,256]{3,2,1,0:T(8,128)(2,1)S(1)}, u32[]{:S(2)}, u32[]{:S(2)}) collective-permute-start(bf16[2,4,16,256]{3,2,1,0:T(8,128)(2,1)S(1)} %pad_maximum_fusion.refs_0_), channel_id=1, source_target_pairs={{0,12},{1,13},{2,14},{3,15},{4,8},{5,9},{6,10},{7,11},{8,4},{9,5},... | collective-permute-start | bytes 196616 | tf_op jit(solution)/shard_map/ppermute | solution.py:258
  18.9 22.5 %collective-permute-start.12 = (bf16[2,528,128]{2,1,0:T(8,128)(2,1)S(1)}, bf16[2,528,128]{2,1,0:T(8,128)(2,1)S(1)}, u32[]{:S(2)}, u32[]{:S(2)}) collective-permute-start(bf16[2,528,128]{2,1,0:T(8,128)(2,1)S(1)} %get-tuple-element.34), channel_id=1, source_target_pairs={{0,3},{1,2},{2,1},{3,0},{4,7},{5,6},{6,5},{7,4},{8,11},{9,10},{10,... | collective-permute-start | bytes 811016 | tf_op jit(solution)/shard_map/ppermute | solution.py:258
  21.0 5.3 %collective-permute-start.3 = (bf16[2,4,16,256]{3,2,1,0:T(8,128)(2,1)S(1)}, bf16[2,4,16,256]{3,2,1,0:T(8,128)(2,1)S(1)}, u32[]{:S(2)}, u32[]{:S(2)}) collective-permute-start(bf16[2,4,16,256]{3,2,1,0:T(8,128)(2,1)S(1)} %pad_maximum_fusion.1), channel_id=1, source_target_pairs={{0,6},{1,7},{2,4},{3,5},{4,2},{5,3},{6,0},{7,1},{8,14},{9,15},{10,... | collective-permute-start | bytes 196616 | tf_op jit(solution)/shard_map/ppermute | solution.py:258
  26.2 6.9 %collective-permute-start.5 = (bf16[2,4,16,256]{3,2,1,0:T(8,128)(2,1)S(1)}, bf16[2,4,16,256]{3,2,1,0:T(8,128)(2,1)S(1)}, u32[]{:S(2)}, u32[]{:S(2)}) collective-permute-start(bf16[2,4,16,256]{3,2,1,0:T(8,128)(2,1)S(1)} %pad_maximum_fusion.1), channel_id=1, source_target_pairs={{0,10},{1,11},{2,8},{3,9},{4,14},{5,15},{6,12},{7,13},{8,2},{9,3},... | collective-permute-start | bytes 196616 | tf_op jit(solution)/shard_map/ppermute | solution.py:258
  33.1 7.6 %collective-permute-start.7 = (bf16[2,4,16,256]{3,2,1,0:T(8,128)(2,1)S(1)}, bf16[2,4,16,256]{3,2,1,0:T(8,128)(2,1)S(1)}, u32[]{:S(2)}, u32[]{:S(2)}) collective-permute-start(bf16[2,4,16,256]{3,2,1,0:T(8,128)(2,1)S(1)} %pad_maximum_fusion.1), channel_id=1, source_target_pairs={{0,14},{1,15},{2,12},{3,13},{4,10},{5,11},{6,8},{7,9},{8,6},{9,7},... | collective-permute-start | bytes 196616 | tf_op jit(solution)/shard_map/ppermute | solution.py:258
  40.7 6.4 %collective-permute-start.14 = (bf16[1,528,128]{2,1,0:T(8,128)(2,1)S(1)}, bf16[1,528,128]{2,1,0:T(8,128)(2,1)S(1)}, u32[]{:S(2)}, u32[]{:S(2)}) collective-permute-start(bf16[1,528,128]{2,1,0:T(8,128)(2,1)S(1)} %get-tuple-element.35), channel_id=1, source_target_pairs={{0,2},{1,3},{2,0},{3,1},{4,6},{5,7},{6,4},{7,5},{8,10},{9,11},{10,... | collective-permute-start | bytes 405512 | tf_op jit(solution)/shard_map/ppermute | solution.py:258
  41.3 9.1 %collective-permute-start.15 = (bf16[1,528,128]{2,1,0:T(8,128)(2,1)S(1)}, bf16[1,528,128]{2,1,0:T(8,128)(2,1)S(1)}, u32[]{:S(2)}, u32[]{:S(2)}) collective-permute-start(bf16[1,528,128]{2,1,0:T(8,128)(2,1)S(1)} %get-tuple-element.36), channel_id=1, source_target_pairs={{0,3},{1,2},{2,1},{3,0},{4,7},{5,6},{6,5},{7,4},{8,11},{9,10},{10,... | collective-permute-start | bytes 405512 | tf_op jit(solution)/shard_map/ppermute | solution.py:258
  41.4 11.6 %collective-permute-start.10 = (bf16[1,528,128]{2,1,0:T(8,128)(2,1)S(1)}, bf16[1,528,128]{2,1,0:T(8,128)(2,1)S(1)}, u32[]{:S(2)}, u32[]{:S(2)}) collective-permute-start(bf16[1,528,128]{2,1,0:T(8,128)(2,1)S(1)} %get-tuple-element.32), channel_id=1, source_target_pairs={{0,3},{1,2},{2,1},{3,0},{4,7},{5,6},{6,5},{7,4},{8,11},{9,10},{10,... | collective-permute-start | bytes 405512 | tf_op jit(solution)/shard_map/ppermute | solution.py:258
  43.8 12.3 %collective-permute-start.9 = (bf16[1,528,128]{2,1,0:T(8,128)(2,1)S(1)}, bf16[1,528,128]{2,1,0:T(8,128)(2,1)S(1)}, u32[]{:S(2)}, u32[]{:S(2)}) collective-permute-start(bf16[1,528,128]{2,1,0:T(8,128)(2,1)S(1)} %get-tuple-element.31), channel_id=1, source_target_pairs={{0,2},{1,3},{2,0},{3,1},{4,6},{5,7},{6,4},{7,5},{8,10},{9,11},{10,... | collective-permute-start | bytes 405512 | tf_op jit(solution)/shard_map/ppermute | solution.py:258
  47.1 10.1 %collective-permute-start.17 = (bf16[272,256]{1,0:T(8,128)(2,1)S(1)}, bf16[272,256]{1,0:T(8,128)(2,1)S(1)}, u32[]{:S(2)}, u32[]{:S(2)}) collective-permute-start(bf16[272,256]{1,0:T(8,128)(2,1)S(1)} %shard_map.67), channel_id=1, source_target_pairs={{0,12},{1,13},{2,14},{3,15},{4,8},{5,9},{6,10},{7,11},{8,4},{9,5},... | collective-permute-start | bytes 417800 | tf_op jit(solution)/shard_map/ppermute | solution.py:258
  51.6 9.4 %collective-permute-start.16 = (bf16[272,256]{1,0:T(8,128)(2,1)S(1)}, bf16[272,256]{1,0:T(8,128)(2,1)S(1)}, u32[]{:S(2)}, u32[]{:S(2)}) collective-permute-start(bf16[272,256]{1,0:T(8,128)(2,1)S(1)} %shard_map.66), channel_id=1, source_target_pairs={{0,8},{1,9},{2,10},{3,11},{4,12},{5,13},{6,14},{7,15},{8,0},{9,1},... | collective-permute-start | bytes 417800 | tf_op jit(solution)/shard_map/ppermute | solution.py:258
  53.0 9.4 %collective-permute-start.13 = (bf16[272,256]{1,0:T(8,128)(2,1)S(1)}, bf16[272,256]{1,0:T(8,128)(2,1)S(1)}, u32[]{:S(2)}, u32[]{:S(2)}) collective-permute-start(bf16[272,256]{1,0:T(8,128)(2,1)S(1)} %shard_map.65), channel_id=1, source_target_pairs={{0,4},{1,5},{2,6},{3,7},{4,0},{5,1},{6,2},{7,3},{8,12},{9,13},{10,... | collective-permute-start | bytes 417800 | tf_op jit(solution)/shard_map/ppermute | solution.py:258
  65.3 7.3 %collective-permute-start.25 = (bf16[32,2688]{1,0:T(8,128)(2,1)S(1)}, bf16[32,2688]{1,0:T(8,128)(2,1)S(1)}, u32[]{:S(2)}, u32[]{:S(2)}) collective-permute-start(bf16[32,2688]{1,0:T(8,128)(2,1)S(1)} %get-tuple-element.44), channel_id=1, source_target_pairs={{0,2},{1,3},{2,0},{3,1},{4,6},{5,7},{6,4},{7,5},{8,10},{9,11},{10,... | collective-permute-start | bytes 516104 | tf_op jit(solution)/shard_map/ppermute | solution.py:258
  66.3 10.0 %collective-permute-start.23 = (bf16[32,2688]{1,0:T(8,128)(2,1)S(1)}, bf16[32,2688]{1,0:T(8,128)(2,1)S(1)}, u32[]{:S(2)}, u32[]{:S(2)}) collective-permute-start(bf16[32,2688]{1,0:T(8,128)(2,1)S(1)} %get-tuple-element.42), channel_id=1, source_target_pairs={{0,2},{1,3},{2,0},{3,1},{4,6},{5,7},{6,4},{7,5},{8,10},{9,11},{10,... | collective-permute-start | bytes 516104 | tf_op jit(solution)/shard_map/ppermute | solution.py:258
  67.4 12.6 %collective-permute-start.21 = (bf16[32,2688]{1,0:T(8,128)(2,1)S(1)}, bf16[32,2688]{1,0:T(8,128)(2,1)S(1)}, u32[]{:S(2)}, u32[]{:S(2)}) collective-permute-start(bf16[32,2688]{1,0:T(8,128)(2,1)S(1)} %get-tuple-element.40), channel_id=1, source_target_pairs={{0,2},{1,3},{2,0},{3,1},{4,6},{5,7},{6,4},{7,5},{8,10},{9,11},{10,... | collective-permute-start | bytes 516104 | tf_op jit(solution)/shard_map/ppermute | solution.py:258
  68.3 14.6 %collective-permute-start.20 = (bf16[32,2688]{1,0:T(8,128)(2,1)S(1)}, bf16[32,2688]{1,0:T(8,128)(2,1)S(1)}, u32[]{:S(2)}, u32[]{:S(2)}) collective-permute-start(bf16[32,2688]{1,0:T(8,128)(2,1)S(1)} %get-tuple-element.38), channel_id=1, source_target_pairs={{0,2},{1,3},{2,0},{3,1},{4,6},{5,7},{6,4},{7,5},{8,10},{9,11},{10,... | collective-permute-start | bytes 516104 | tf_op jit(solution)/shard_map/ppermute | solution.py:258
  72.6 10.2 %collective-permute-start.26 = (bf16[32,2688]{1,0:T(8,128)(2,1)S(1)}, bf16[32,2688]{1,0:T(8,128)(2,1)S(1)}, u32[]{:S(2)}, u32[]{:S(2)}) collective-permute-start(bf16[32,2688]{1,0:T(8,128)(2,1)S(1)} %shard_map.73), channel_id=1, source_target_pairs={{0,4},{1,5},{2,6},{3,7},{4,0},{5,1},{6,2},{7,3},{8,12},{9,13},{10,... | collective-permute-start | bytes 516104 | tf_op jit(solution)/shard_map/ppermute | solution.py:258
  76.3 13.5 %collective-permute-start.24 = (bf16[32,2688]{1,0:T(8,128)(2,1)S(1)}, bf16[32,2688]{1,0:T(8,128)(2,1)S(1)}, u32[]{:S(2)}, u32[]{:S(2)}) collective-permute-start(bf16[32,2688]{1,0:T(8,128)(2,1)S(1)} %shard_map.72), channel_id=1, source_target_pairs={{0,8},{1,9},{2,10},{3,11},{4,12},{5,13},{6,14},{7,15},{8,0},{9,1},... | collective-permute-start | bytes 516104 | tf_op jit(solution)/shard_map/ppermute | solution.py:258
  80.0 9.8 %collective-permute-start.22 = (bf16[32,2688]{1,0:T(8,128)(2,1)S(1)}, bf16[32,2688]{1,0:T(8,128)(2,1)S(1)}, u32[]{:S(2)}, u32[]{:S(2)}) collective-permute-start(bf16[32,2688]{1,0:T(8,128)(2,1)S(1)} %shard_map.71), channel_id=1, source_target_pairs={{0,12},{1,13},{2,14},{3,15},{4,8},{5,9},{6,10},{7,11},{8,4},{9,5},... | collective-permute-start | bytes 516104 | tf_op jit(solution)/shard_map/ppermute | solution.py:258
  (9 other events, 27.3 us)

commit v3 on v1

--- a/solution.py
+++ b/solution.py
@@ -53,16 +53,18 @@
     )(*ins)
 
 
-def split_kernel(live_ref, q_ref, k_ref, v_ref, *refs, outer, width, groups, copies):
-    _, z, r = place()
-    q_outs = refs[:INNER]
-    kv_outs = refs[INNER:]
-    keys = k_ref.shape[0]
-    live = jnp.full((16, HEAD_SIZE), live_ref[0], jnp.int32).astype(f32).astype(bf16)
+def split_queries_kernel(q_ref, *q_outs, outer, width):
+    _, _, r = place()
     for k, out in enumerate(q_outs):
         for zz in range(outer):
             col = pl.multiple_of((zz * INNER + lax.bitwise_xor(r, k)) * width, width)
             out[zz] = q_ref[:, pl.ds(col, width)]
+
+
+def split_cache_kernel(live_ref, k_ref, v_ref, *kv_outs, groups, copies):
+    _, z, r = place()
+    keys = k_ref.shape[0]
+    live = jnp.full((16, HEAD_SIZE), live_ref[0], jnp.int32).astype(f32).astype(bf16)
     for (k, offsets), out in zip(groups, kv_outs):
         for i, kk in enumerate(offsets):
             head = lax.bitwise_xor(z, kk) * INNER + lax.bitwise_xor(r, k)
@@ -243,14 +245,15 @@
     order = list(range(outer - 1, -1, -1))
     phases = [order[:outer // 2], order[outer // 2:3 * outer // 4], order[3 * outer // 4:]]
     groups = [(0, order), (1, order)] + [(k, p) for p in phases for k in range(2, INNER)]
-    outs = [shape((outer, rows, width), bf16)] * INNER + [
-        shape((len(p), 2 * keys + 16, HEAD_SIZE), bf16) for k, p in groups
-    ]
-    split = call(
-        functools.partial(split_kernel, outer=outer, width=width, groups=groups, copies=copies),
-        [live_counts, query_block, cache_keys, stored_values], outs, scalars=1,
-    )
-    q_out, kv_out = split[:INNER], split[INNER:]
+    q_out = call(
+        functools.partial(split_queries_kernel, outer=outer, width=width),
+        [query_block], [shape((outer, rows, width), bf16)] * INNER,
+    )
+    kv_out = call(
+        functools.partial(split_cache_kernel, groups=groups, copies=copies),
+        [live_counts, cache_keys, stored_values],
+        [shape((len(p), 2 * keys + 16, HEAD_SIZE), bf16) for k, p in groups], scalars=1,
+    )
     q_got = {k: swap(q_out[k], k) for k in (2, 3, 1)}
     kv_pair = swap(kv_out[1], 1)
     kv_far = [

time: 81.2 us -> 80 us (0.985)
  waiting for transfers between devices: 44.3 us -> 43 us
    ppermute x26, waiting for transfers between devices: 44.3 us -> 43 us  [swap(): return lax.ppermute(x, 'seq', [(i, i ^ k) for i in range(devices)])]
    pallas_call x12 -> x13, Pallas kernels: 7.84 us -> 7.86 us  [call(): pl.pallas_call(kernel, out_shape=tuple(outs), in_specs=in_specs, out_spec...]
  transfers between devices with their start and end apart: 26 -> 26, of which waited for: 16 -> 16; matrix products, arithmetic and copies ran while one was open for 0% -> 0% of each run, Pallas kernels for 7% -> 8%
where the time goes in v3:
time: 80 us; the launch traced here: 78.9 us
  waiting for transfers between devices  43 us (54%)
  starting transfers between devices  24.6 us (31%)
  Pallas kernels  7.86 us (10%)
  local copies, waits for them, and re-layouts  2.03 us (3%)
  between operations  1.44 us (2%)
    ppermute x26, waiting for transfers between devices, swap(): return lax.ppermute(x, 'seq', [(i, i ^ k) for i in range(devices)])  43 us
    ppermute x26, starting transfers between devices, swap(): return lax.ppermute(x, 'seq', [(i, i ^ k) for i in range(devices)])  24.6 us
    pallas_call x13, Pallas kernels, call(): pl.pallas_call(kernel, out_shape=tuple(outs), in_specs=in_specs, out_spec...  7.86 us
    unnamed x10, local copies, waits for them, and re-layouts  2.03 us
  transfers between devices with their start and end apart: 26, of which 16 were waited for; matrix products, arithmetic and copies ran while one was open for 0% of the time, Pallas kernels for 8%

profile of v3, /device:TPU:0, one launch (start us, length us, event | category | flops | bytes accessed | tf_op | source)
XLA Modules:
  0.0 78.9 jit_solution(12735013804823872751)
XLA Ops:
  0.0 1.8 %copy-done = bf16[256,5376]{1,0:T(8,128)(2,1)S(1)} copy-done((bf16[256,5376]{1,0:T(8,128)(2,1)S(1)}, bf16[256,5376]{1,0:T(8,128)(2,1)}, u32[]{:S(2)}) %copy-start) | copy-done | bytes 2752536
  3.3 2.6 %collective-permute-start.1 = (bf16[4,16,256]{2,1,0:T(8,128)(2,1)S(1)}, bf16[4,16,256]{2,1,0:T(8,128)(2,1)S(1)}, u32[]{:S(2)}, u32[]{:S(2)}) collective-permute-start(bf16[4,16,256]{2,1,0:T(8,128)(2,1)S(1)} %get-tuple-element.31), channel_id=1, source_target_pairs={{0,2},{1,3},{2,0},{3,1},{4,6},{5,7},{6,4},{7,5},{8,10},{9,11},{10,... | collective-permute-start | bytes 98312 | tf_op jit(solution)/shard_map/ppermute | solution.py:243
  7.8 1.4 %collective-permute-done.2 = bf16[4,16,256]{2,1,0:T(8,128)(2,1)S(1)} collective-permute-done((bf16[4,16,256]{2,1,0:T(8,128)(2,1)S(1)}, bf16[4,16,256]{2,1,0:T(8,128)(2,1)S(1)}, u32[]{:S(2)}, u32[]{:S(2)}) %collective-permute-start.2) | collective-permute-done | bytes 32800 | tf_op jit(solution)/shard_map/ppermute | solution.py:243
  9.2 1.6 %collective-permute-start.3 = (bf16[4,4,16,256]{3,2,1,0:T(8,128)(2,1)S(1)}, bf16[4,4,16,256]{3,2,1,0:T(8,128)(2,1)S(1)}, u32[]{:S(2)}, u32[]{:S(2)}) collective-permute-start(bf16[4,4,16,256]{3,2,1,0:T(8,128)(2,1)S(1)} %pad_maximum_fusion.refs_0_), channel_id=1, source_target_pairs={{0,4},{1,5},{2,6},{3,7},{4,0},{5,1},{6,2},{7,3},{8,12},{9,13},{10,... | collective-permute-start | bytes 393224 | tf_op jit(solution)/shard_map/ppermute | solution.py:243
  11.7 2.6 %collective-permute-start.4 = (bf16[4,4,16,256]{3,2,1,0:T(8,128)(2,1)S(1)}, bf16[4,4,16,256]{3,2,1,0:T(8,128)(2,1)S(1)}, u32[]{:S(2)}, u32[]{:S(2)}) collective-permute-start(bf16[4,4,16,256]{3,2,1,0:T(8,128)(2,1)S(1)} %pad_maximum_fusion.refs_0_), channel_id=1, source_target_pairs={{0,8},{1,9},{2,10},{3,11},{4,12},{5,13},{6,14},{7,15},{8,0},{9,1},... | collective-permute-start | bytes 393224 | tf_op jit(solution)/shard_map/ppermute | solution.py:243
  14.9 5.6 %collective-permute-done.4.refs_2_ = bf16[4,4,16,256]{3,2,1,0:T(8,128)(2,1)S(1)} collective-permute-done((bf16[4,4,16,256]{3,2,1,0:T(8,128)(2,1)S(1)}, bf16[4,4,16,256]{3,2,1,0:T(8,128)(2,1)S(1)}, u32[]{:S(2)}, u32[]{:S(2)}) %collective-permute-start.4) | collective-permute-done | bytes 131104 | tf_op jit(solution)/shard_map/ppermute | solution.py:243
  20.4 2.7 %collective-permute-start.5 = (bf16[4,4,16,256]{3,2,1,0:T(8,128)(2,1)S(1)}, bf16[4,4,16,256]{3,2,1,0:T(8,128)(2,1)S(1)}, u32[]{:S(2)}, u32[]{:S(2)}) collective-permute-start(bf16[4,4,16,256]{3,2,1,0:T(8,128)(2,1)S(1)} %pad_maximum_fusion.refs_0_), channel_id=1, source_target_pairs={{0,12},{1,13},{2,14},{3,15},{4,8},{5,9},{6,10},{7,11},{8,4},{9,5},... | collective-permute-start | bytes 393224 | tf_op jit(solution)/shard_map/ppermute | solution.py:243
  23.1 4.1 %collective-permute-done.5.refs_3_ = bf16[4,4,16,256]{3,2,1,0:T(8,128)(2,1)S(1)} collective-permute-done((bf16[4,4,16,256]{3,2,1,0:T(8,128)(2,1)S(1)}, bf16[4,4,16,256]{3,2,1,0:T(8,128)(2,1)S(1)}, u32[]{:S(2)}, u32[]{:S(2)}) %collective-permute-start.5) | collective-permute-done | bytes 131104 | tf_op jit(solution)/shard_map/ppermute | solution.py:243
  29.9 1.2 %collective-permute-start.8 = (bf16[1,528,128]{2,1,0:T(8,128)(2,1)S(1)}, bf16[1,528,128]{2,1,0:T(8,128)(2,1)S(1)}, u32[]{:S(2)}, u32[]{:S(2)}) collective-permute-start(bf16[1,528,128]{2,1,0:T(8,128)(2,1)S(1)} %get-tuple-element.36), channel_id=1, source_target_pairs={{0,3},{1,2},{2,1},{3,0},{4,7},{5,6},{6,5},{7,4},{8,11},{9,10},{10,... | collective-permute-start | bytes 405512 | tf_op jit(solution)/shard_map/ppermute | solution.py:243
  31.2 2.3 %shard_map.68 = (bf16[272,256]{1,0:T(8,128)(2,1)S(1)}, bf16[272,256]{1,0:T(8,128)(2,1)S(1)}) custom-call(s32[1]{0:T(128)S(6)} %copy.8.first_ref, bf16[4,4,16,256]{3,2,1,0:T(8,128)(2,1)S(1)} %pad_maximum_fusion.refs_0_, bf16[4,4,16,256]{3,2,1,0:T(8,128)(2,1)S(1)} %collective-permute-done.3.refs_1_, ...), custom_call_target="tpu_custom_call" | custom-call | flops 536870912 | bytes 2424836 | tf_op jit(solution)/shard_map/pallas_call | solution.py:45
  33.6 1.8 %collective-permute-done.9.refs_6_ = bf16[1,528,128]{2,1,0:T(8,128)(2,1)S(1)} collective-permute-done((bf16[1,528,128]{2,1,0:T(8,128)(2,1)S(1)}, bf16[1,528,128]{2,1,0:T(8,128)(2,1)S(1)}, u32[]{:S(2)}, u32[]{:S(2)}) %collective-permute-start.9) | collective-permute-done | bytes 135200 | tf_op jit(solution)/shard_map/ppermute | solution.py:243
  35.4 2.9 %collective-permute-start.15 = (bf16[272,256]{1,0:T(8,128)(2,1)S(1)}, bf16[272,256]{1,0:T(8,128)(2,1)S(1)}, u32[]{:S(2)}, u32[]{:S(2)}) collective-permute-start(bf16[272,256]{1,0:T(8,128)(2,1)S(1)} %get-tuple-element.42), channel_id=1, source_target_pairs={{0,12},{1,13},{2,14},{3,15},{4,8},{5,9},{6,10},{7,11},{8,4},{9,5},... | collective-permute-start | bytes 417800 | tf_op jit(solution)/shard_map/ppermute | solution.py:243
  38.2 1.2 %shard_map.67 = bf16[272,256]{1,0:T(8,128)(2,1)S(1)} custom-call(s32[1]{0:T(128)S(6)} %copy.8.first_ref, bf16[4,4,16,256]{3,2,1,0:T(8,128)(2,1)S(1)} %pad_maximum_fusion.refs_0_, bf16[4,4,16,256]{3,2,1,0:T(8,128)(2,1)S(1)} %collective-permute-done.3.refs_1_, bf16[4,4,16,256]{3,2,1,0:T(8,128)(2,1)S(1)} %collective-permute-done.4.refs_2_, ...), custom_call_target="tpu_custom_call" | custom-call | flops 268435456 | bytes 2015236 | tf_op jit(solution)/shard_map/pallas_call | solution.py:45
  39.5 1.9 %collective-permute-done.8.refs_7_ = bf16[1,528,128]{2,1,0:T(8,128)(2,1)S(1)} collective-permute-done((bf16[1,528,128]{2,1,0:T(8,128)(2,1)S(1)}, bf16[1,528,128]{2,1,0:T(8,128)(2,1)S(1)}, u32[]{:S(2)}, u32[]{:S(2)}) %collective-permute-start.8) | collective-permute-done | bytes 135200 | tf_op jit(solution)/shard_map/ppermute | solution.py:243
  42.7 3.6 %collective-permute-done.14.refs_2_ = bf16[272,256]{1,0:T(8,128)(2,1)S(1)} collective-permute-done((bf16[272,256]{1,0:T(8,128)(2,1)S(1)}, bf16[272,256]{1,0:T(8,128)(2,1)S(1)}, u32[]{:S(2)}, u32[]{:S(2)}) %collective-permute-start.14) | collective-permute-done | bytes 139296 | tf_op jit(solution)/shard_map/ppermute | solution.py:243
  46.3 2.7 %collective-permute-done.11.refs_1_ = bf16[272,256]{1,0:T(8,128)(2,1)S(1)} collective-permute-done((bf16[272,256]{1,0:T(8,128)(2,1)S(1)}, bf16[272,256]{1,0:T(8,128)(2,1)S(1)}, u32[]{:S(2)}, u32[]{:S(2)}) %collective-permute-start.11) | collective-permute-done | bytes 139296 | tf_op jit(solution)/shard_map/ppermute | solution.py:243
  49.7 1.3 %collective-permute-done.16.other_ref = bf16[256,256]{1,0:T(8,128)(2,1)S(1)} collective-permute-done((bf16[256,256]{1,0:T(8,128)(2,1)S(1)}, bf16[256,256]{1,0:T(8,128)(2,1)S(1)}, u32[]{:S(2)}, u32[]{:S(2)}) %collective-permute-start.16) | collective-permute-done | bytes 131104 | tf_op jit(solution)/shard_map/ppermute | solution.py:243
  56.1 3.2 %collective-permute-done.23.got_ref = bf16[32,2688]{1,0:T(8,128)(2,1)S(1)} collective-permute-done((bf16[32,2688]{1,0:T(8,128)(2,1)S(1)}, bf16[32,2688]{1,0:T(8,128)(2,1)S(1)}, u32[]{:S(2)}, u32[]{:S(2)}) %collective-permute-start.23) | collective-permute-done | bytes 172064 | tf_op jit(solution)/shard_map/ppermute | solution.py:243
  60.0 3.0 %collective-permute-done.21.got_ref = bf16[32,2688]{1,0:T(8,128)(2,1)S(1)} collective-permute-done((bf16[32,2688]{1,0:T(8,128)(2,1)S(1)}, bf16[32,2688]{1,0:T(8,128)(2,1)S(1)}, u32[]{:S(2)}, u32[]{:S(2)}) %collective-permute-start.21) | collective-permute-done | bytes 172064 | tf_op jit(solution)/shard_map/ppermute | solution.py:243
  63.4 3.3 %collective-permute-done.19.got_ref = bf16[32,2688]{1,0:T(8,128)(2,1)S(1)} collective-permute-done((bf16[32,2688]{1,0:T(8,128)(2,1)S(1)}, bf16[32,2688]{1,0:T(8,128)(2,1)S(1)}, u32[]{:S(2)}, u32[]{:S(2)}) %collective-permute-start.19) | collective-permute-done | bytes 172064 | tf_op jit(solution)/shard_map/ppermute | solution.py:243
  66.7 1.3 %collective-permute-start.20 = (bf16[32,2688]{1,0:T(8,128)(2,1)S(1)}, bf16[32,2688]{1,0:T(8,128)(2,1)S(1)}, u32[]{:S(2)}, u32[]{:S(2)}) collective-permute-start(bf16[32,2688]{1,0:T(8,128)(2,1)S(1)} %shard_map.72), channel_id=1, source_target_pairs={{0,12},{1,13},{2,14},{3,15},{4,8},{5,9},{6,10},{7,11},{8,4},{9,5},... | collective-permute-start | bytes 516104 | tf_op jit(solution)/shard_map/ppermute | solution.py:243
  67.9 1.6 %collective-permute-done.18.got_ref = bf16[32,2688]{1,0:T(8,128)(2,1)S(1)} collective-permute-done((bf16[32,2688]{1,0:T(8,128)(2,1)S(1)}, bf16[32,2688]{1,0:T(8,128)(2,1)S(1)}, u32[]{:S(2)}, u32[]{:S(2)}) %collective-permute-start.18) | collective-permute-done | bytes 172064 | tf_op jit(solution)/shard_map/ppermute | solution.py:243
  69.5 7.2 %collective-permute-done.22.refs_1_ = bf16[32,2688]{1,0:T(8,128)(2,1)S(1)} collective-permute-done((bf16[32,2688]{1,0:T(8,128)(2,1)S(1)}, bf16[32,2688]{1,0:T(8,128)(2,1)S(1)}, u32[]{:S(2)}, u32[]{:S(2)}) %collective-permute-start.22) | collective-permute-done | bytes 172064 | tf_op jit(solution)/shard_map/ppermute | solution.py:243
  77.0 1.3 %collective-permute-done.25.other_ref = bf16[16,2688]{1,0:T(8,128)(2,1)S(1)} collective-permute-done((bf16[16,2688]{1,0:T(8,128)(2,1)S(1)}, bf16[16,2688]{1,0:T(8,128)(2,1)S(1)}, u32[]{:S(2)}, u32[]{:S(2)}) %collective-permute-start.25) | collective-permute-done | bytes 86048 | tf_op jit(solution)/shard_map/ppermute | solution.py:243
  (52 shorter events, 15.4 us)
Async XLA Ops:
  1.9 49.1 %collective-permute-start.17 = (bf16[256,2688]{1,0:T(8,128)(2,1)S(1)}, bf16[256,2688]{1,0:T(8,128)(2,1)S(1)}, u32[]{:S(2)}, u32[]{:S(2)}) collective-permute-start(bf16[256,2688]{1,0:T(8,128)(2,1)S(1)} %shard_map.70), channel_id=1, source_target_pairs={{0,1},{1,0},{2,3},{3,2},{4,5},{5,4},{6,7},{7,6},{8,9},{9,8},{10,11... | collective-permute-start | bytes 4128776 | tf_op jit(solution)/shard_map/ppermute | solution.py:243
  2.7 4.6 %collective-permute-start = (bf16[4,16,256]{2,1,0:T(8,128)(2,1)S(1)}, bf16[4,16,256]{2,1,0:T(8,128)(2,1)S(1)}, u32[]{:S(2)}, u32[]{:S(2)}) collective-permute-start(bf16[4,16,256]{2,1,0:T(8,128)(2,1)S(1)} %get-tuple-element.30), channel_id=1, source_target_pairs={{0,1},{1,0},{2,3},{3,2},{4,5},{5,4},{6,7},{7,6},{8,9},{9,8},{10,11... | collective-permute-start | bytes 98312 | tf_op jit(solution)/shard_map/ppermute | solution.py:243
  3.3 4.6 %collective-permute-start.1 = (bf16[4,16,256]{2,1,0:T(8,128)(2,1)S(1)}, bf16[4,16,256]{2,1,0:T(8,128)(2,1)S(1)}, u32[]{:S(2)}, u32[]{:S(2)}) collective-permute-start(bf16[4,16,256]{2,1,0:T(8,128)(2,1)S(1)} %get-tuple-element.31), channel_id=1, source_target_pairs={{0,2},{1,3},{2,0},{3,1},{4,6},{5,7},{6,4},{7,5},{8,10},{9,11},{10,... | collective-permute-start | bytes 98312 | tf_op jit(solution)/shard_map/ppermute | solution.py:243
  5.8 3.4 %collective-permute-start.2 = (bf16[4,16,256]{2,1,0:T(8,128)(2,1)S(1)}, bf16[4,16,256]{2,1,0:T(8,128)(2,1)S(1)}, u32[]{:S(2)}, u32[]{:S(2)}) collective-permute-start(bf16[4,16,256]{2,1,0:T(8,128)(2,1)S(1)} %get-tuple-element.32), channel_id=1, source_target_pairs={{0,3},{1,2},{2,1},{3,0},{4,7},{5,6},{6,5},{7,4},{8,11},{9,10},{10,... | collective-permute-start | bytes 98312 | tf_op jit(solution)/shard_map/ppermute | solution.py:243
  7.1 22.8 %collective-permute-start.6 = (bf16[4,528,128]{2,1,0:T(8,128)(2,1)S(1)}, bf16[4,528,128]{2,1,0:T(8,128)(2,1)S(1)}, u32[]{:S(2)}, u32[]{:S(2)}) collective-permute-start(bf16[4,528,128]{2,1,0:T(8,128)(2,1)S(1)} %get-tuple-element.34), channel_id=1, source_target_pairs={{0,1},{1,0},{2,3},{3,2},{4,5},{5,4},{6,7},{7,6},{8,9},{9,8},{10,11... | collective-permute-start | bytes 1622024 | tf_op jit(solution)/shard_map/ppermute | solution.py:243
  9.2 5.6 %collective-permute-start.3 = (bf16[4,4,16,256]{3,2,1,0:T(8,128)(2,1)S(1)}, bf16[4,4,16,256]{3,2,1,0:T(8,128)(2,1)S(1)}, u32[]{:S(2)}, u32[]{:S(2)}) collective-permute-start(bf16[4,4,16,256]{3,2,1,0:T(8,128)(2,1)S(1)} %pad_maximum_fusion.refs_0_), channel_id=1, source_target_pairs={{0,4},{1,5},{2,6},{3,7},{4,0},{5,1},{6,2},{7,3},{8,12},{9,13},{10,... | collective-permute-start | bytes 393224 | tf_op jit(solution)/shard_map/ppermute | solution.py:243
  10.9 16.4 %collective-permute-start.12 = (bf16[2,528,128]{2,1,0:T(8,128)(2,1)S(1)}, bf16[2,528,128]{2,1,0:T(8,128)(2,1)S(1)}, u32[]{:S(2)}, u32[]{:S(2)}) collective-permute-start(bf16[2,528,128]{2,1,0:T(8,128)(2,1)S(1)} %get-tuple-element.39), channel_id=1, source_target_pairs={{0,2},{1,3},{2,0},{3,1},{4,6},{5,7},{6,4},{7,5},{8,10},{9,11},{10,... | collective-permute-start | bytes 811016 | tf_op jit(solution)/shard_map/ppermute | solution.py:243
  11.7 8.7 %collective-permute-start.4 = (bf16[4,4,16,256]{3,2,1,0:T(8,128)(2,1)S(1)}, bf16[4,4,16,256]{3,2,1,0:T(8,128)(2,1)S(1)}, u32[]{:S(2)}, u32[]{:S(2)}) collective-permute-start(bf16[4,4,16,256]{3,2,1,0:T(8,128)(2,1)S(1)} %pad_maximum_fusion.refs_0_), channel_id=1, source_target_pairs={{0,8},{1,9},{2,10},{3,11},{4,12},{5,13},{6,14},{7,15},{8,0},{9,1},... | collective-permute-start | bytes 393224 | tf_op jit(solution)/shard_map/ppermute | solution.py:243
  14.9 13.5 %collective-permute-start.13 = (bf16[2,528,128]{2,1,0:T(8,128)(2,1)S(1)}, bf16[2,528,128]{2,1,0:T(8,128)(2,1)S(1)}, u32[]{:S(2)}, u32[]{:S(2)}) collective-permute-start(bf16[2,528,128]{2,1,0:T(8,128)(2,1)S(1)} %get-tuple-element.40), channel_id=1, source_target_pairs={{0,3},{1,2},{2,1},{3,0},{4,7},{5,6},{6,5},{7,4},{8,11},{9,10},{10,... | collective-permute-start | bytes 811016 | tf_op jit(solution)/shard_map/ppermute | solution.py:243
  20.4 6.8 %collective-permute-start.5 = (bf16[4,4,16,256]{3,2,1,0:T(8,128)(2,1)S(1)}, bf16[4,4,16,256]{3,2,1,0:T(8,128)(2,1)S(1)}, u32[]{:S(2)}, u32[]{:S(2)}) collective-permute-start(bf16[4,4,16,256]{3,2,1,0:T(8,128)(2,1)S(1)} %pad_maximum_fusion.refs_0_), channel_id=1, source_target_pairs={{0,12},{1,13},{2,14},{3,15},{4,8},{5,9},{6,10},{7,11},{8,4},{9,5},... | collective-permute-start | bytes 393224 | tf_op jit(solution)/shard_map/ppermute | solution.py:243
  27.2 6.3 %collective-permute-start.10 = (bf16[1,528,128]{2,1,0:T(8,128)(2,1)S(1)}, bf16[1,528,128]{2,1,0:T(8,128)(2,1)S(1)}, u32[]{:S(2)}, u32[]{:S(2)}) collective-permute-start(bf16[1,528,128]{2,1,0:T(8,128)(2,1)S(1)} %get-tuple-element.38), channel_id=1, source_target_pairs={{0,3},{1,2},{2,1},{3,0},{4,7},{5,6},{6,5},{7,4},{8,11},{9,10},{10,... | collective-permute-start | bytes 405512 | tf_op jit(solution)/shard_map/ppermute | solution.py:243
  27.2 8.1 %collective-permute-start.9 = (bf16[1,528,128]{2,1,0:T(8,128)(2,1)S(1)}, bf16[1,528,128]{2,1,0:T(8,128)(2,1)S(1)}, u32[]{:S(2)}, u32[]{:S(2)}) collective-permute-start(bf16[1,528,128]{2,1,0:T(8,128)(2,1)S(1)} %get-tuple-element.37), channel_id=1, source_target_pairs={{0,2},{1,3},{2,0},{3,1},{4,6},{5,7},{6,4},{7,5},{8,10},{9,11},{10,... | collective-permute-start | bytes 405512 | tf_op jit(solution)/shard_map/ppermute | solution.py:243
  28.4 11.1 %collective-permute-start.7 = (bf16[1,528,128]{2,1,0:T(8,128)(2,1)S(1)}, bf16[1,528,128]{2,1,0:T(8,128)(2,1)S(1)}, u32[]{:S(2)}, u32[]{:S(2)}) collective-permute-start(bf16[1,528,128]{2,1,0:T(8,128)(2,1)S(1)} %get-tuple-element.35), channel_id=1, source_target_pairs={{0,2},{1,3},{2,0},{3,1},{4,6},{5,7},{6,4},{7,5},{8,10},{9,11},{10,... | collective-permute-start | bytes 405512 | tf_op jit(solution)/shard_map/ppermute | solution.py:243
  29.9 11.6 %collective-permute-start.8 = (bf16[1,528,128]{2,1,0:T(8,128)(2,1)S(1)}, bf16[1,528,128]{2,1,0:T(8,128)(2,1)S(1)}, u32[]{:S(2)}, u32[]{:S(2)}) collective-permute-start(bf16[1,528,128]{2,1,0:T(8,128)(2,1)S(1)} %get-tuple-element.36), channel_id=1, source_target_pairs={{0,3},{1,2},{2,1},{3,0},{4,7},{5,6},{6,5},{7,4},{8,11},{9,10},{10,... | collective-permute-start | bytes 405512 | tf_op jit(solution)/shard_map/ppermute | solution.py:243
  33.5 12.8 %collective-permute-start.14 = (bf16[272,256]{1,0:T(8,128)(2,1)S(1)}, bf16[272,256]{1,0:T(8,128)(2,1)S(1)}, u32[]{:S(2)}, u32[]{:S(2)}) collective-permute-start(bf16[272,256]{1,0:T(8,128)(2,1)S(1)} %get-tuple-element.41), channel_id=1, source_target_pairs={{0,8},{1,9},{2,10},{3,11},{4,12},{5,13},{6,14},{7,15},{8,0},{9,1},... | collective-permute-start | bytes 417800 | tf_op jit(solution)/shard_map/ppermute | solution.py:243
  35.4 11.0 %collective-permute-start.15 = (bf16[272,256]{1,0:T(8,128)(2,1)S(1)}, bf16[272,256]{1,0:T(8,128)(2,1)S(1)}, u32[]{:S(2)}, u32[]{:S(2)}) collective-permute-start(bf16[272,256]{1,0:T(8,128)(2,1)S(1)} %get-tuple-element.42), channel_id=1, source_target_pairs={{0,12},{1,13},{2,14},{3,15},{4,8},{5,9},{6,10},{7,11},{8,4},{9,5},... | collective-permute-start | bytes 417800 | tf_op jit(solution)/shard_map/ppermute | solution.py:243
  39.5 9.6 %collective-permute-start.11 = (bf16[272,256]{1,0:T(8,128)(2,1)S(1)}, bf16[272,256]{1,0:T(8,128)(2,1)S(1)}, u32[]{:S(2)}, u32[]{:S(2)}) collective-permute-start(bf16[272,256]{1,0:T(8,128)(2,1)S(1)} %shard_map.67), channel_id=1, source_target_pairs={{0,4},{1,5},{2,6},{3,7},{4,0},{5,1},{6,2},{7,3},{8,12},{9,13},{10,... | collective-permute-start | bytes 417800 | tf_op jit(solution)/shard_map/ppermute | solution.py:243
  52.0 7.3 %collective-permute-start.23 = (bf16[32,2688]{1,0:T(8,128)(2,1)S(1)}, bf16[32,2688]{1,0:T(8,128)(2,1)S(1)}, u32[]{:S(2)}, u32[]{:S(2)}) collective-permute-start(bf16[32,2688]{1,0:T(8,128)(2,1)S(1)} %get-tuple-element.50), channel_id=1, source_target_pairs={{0,2},{1,3},{2,0},{3,1},{4,6},{5,7},{6,4},{7,5},{8,10},{9,11},{10,... | collective-permute-start | bytes 516104 | tf_op jit(solution)/shard_map/ppermute | solution.py:243
  52.9 10.1 %collective-permute-start.21 = (bf16[32,2688]{1,0:T(8,128)(2,1)S(1)}, bf16[32,2688]{1,0:T(8,128)(2,1)S(1)}, u32[]{:S(2)}, u32[]{:S(2)}) collective-permute-start(bf16[32,2688]{1,0:T(8,128)(2,1)S(1)} %get-tuple-element.48), channel_id=1, source_target_pairs={{0,2},{1,3},{2,0},{3,1},{4,6},{5,7},{6,4},{7,5},{8,10},{9,11},{10,... | collective-permute-start | bytes 516104 | tf_op jit(solution)/shard_map/ppermute | solution.py:243
  54.1 12.6 %collective-permute-start.19 = (bf16[32,2688]{1,0:T(8,128)(2,1)S(1)}, bf16[32,2688]{1,0:T(8,128)(2,1)S(1)}, u32[]{:S(2)}, u32[]{:S(2)}) collective-permute-start(bf16[32,2688]{1,0:T(8,128)(2,1)S(1)} %get-tuple-element.46), channel_id=1, source_target_pairs={{0,2},{1,3},{2,0},{3,1},{4,6},{5,7},{6,4},{7,5},{8,10},{9,11},{10,... | collective-permute-start | bytes 516104 | tf_op jit(solution)/shard_map/ppermute | solution.py:243
  54.9 14.6 %collective-permute-start.18 = (bf16[32,2688]{1,0:T(8,128)(2,1)S(1)}, bf16[32,2688]{1,0:T(8,128)(2,1)S(1)}, u32[]{:S(2)}, u32[]{:S(2)}) collective-permute-start(bf16[32,2688]{1,0:T(8,128)(2,1)S(1)} %get-tuple-element.44), channel_id=1, source_target_pairs={{0,2},{1,3},{2,0},{3,1},{4,6},{5,7},{6,4},{7,5},{8,10},{9,11},{10,... | collective-permute-start | bytes 516104 | tf_op jit(solution)/shard_map/ppermute | solution.py:243
  59.3 10.2 %collective-permute-start.24 = (bf16[32,2688]{1,0:T(8,128)(2,1)S(1)}, bf16[32,2688]{1,0:T(8,128)(2,1)S(1)}, u32[]{:S(2)}, u32[]{:S(2)}) collective-permute-start(bf16[32,2688]{1,0:T(8,128)(2,1)S(1)} %shard_map.74), channel_id=1, source_target_pairs={{0,4},{1,5},{2,6},{3,7},{4,0},{5,1},{6,2},{7,3},{8,12},{9,13},{10,... | collective-permute-start | bytes 516104 | tf_op jit(solution)/shard_map/ppermute | solution.py:243
  63.0 13.7 %collective-permute-start.22 = (bf16[32,2688]{1,0:T(8,128)(2,1)S(1)}, bf16[32,2688]{1,0:T(8,128)(2,1)S(1)}, u32[]{:S(2)}, u32[]{:S(2)}) collective-permute-start(bf16[32,2688]{1,0:T(8,128)(2,1)S(1)} %shard_map.73), channel_id=1, source_target_pairs={{0,8},{1,9},{2,10},{3,11},{4,12},{5,13},{6,14},{7,15},{8,0},{9,1},... | collective-permute-start | bytes 516104 | tf_op jit(solution)/shard_map/ppermute | solution.py:243
  66.7 10.1 %collective-permute-start.20 = (bf16[32,2688]{1,0:T(8,128)(2,1)S(1)}, bf16[32,2688]{1,0:T(8,128)(2,1)S(1)}, u32[]{:S(2)}, u32[]{:S(2)}) collective-permute-start(bf16[32,2688]{1,0:T(8,128)(2,1)S(1)} %shard_map.72), channel_id=1, source_target_pairs={{0,12},{1,13},{2,14},{3,15},{4,8},{5,9},{6,10},{7,11},{8,4},{9,5},... | collective-permute-start | bytes 516104 | tf_op jit(solution)/shard_map/ppermute | solution.py:243
  (7 other events, 27.7 us)

commit v4 on v3

--- a/solution.py
+++ b/solution.py
@@ -61,10 +61,20 @@
             out[zz] = q_ref[:, pl.ds(col, width)]
 
 
-def split_cache_kernel(live_ref, k_ref, v_ref, *kv_outs, groups, copies):
+def split_cache_kernel(live_ref, k_hbm, v_hbm, *refs, groups, copies):
     _, z, r = place()
+    kv_outs = refs[:len(groups)]
+    k_ref, v_ref, sems = refs[len(groups):]
     keys = k_ref.shape[0]
+    loads = [
+        pltpu.make_async_copy(source, target, sems.at[i])
+        for i, (source, target) in enumerate(((k_hbm, k_ref), (v_hbm, v_ref)))
+    ]
+    for load in loads:
+        load.start()
     live = jnp.full((16, HEAD_SIZE), live_ref[0], jnp.int32).astype(f32).astype(bf16)
+    for load in loads:
+        load.wait()
     for (k, offsets), out in zip(groups, kv_outs):
         for i, kk in enumerate(offsets):
             head = lax.bitwise_xor(z, kk) * INNER + lax.bitwise_xor(r, k)
@@ -81,10 +91,9 @@
     out_ref[...] = w_ref[:, pl.ds(col, half)]
 
 
-def attention_kernel(first_ref, *refs, outer, first, offsets, rows_all, keys, heads, width):
+def attention_kernel(first_ref, *refs, outer, begin, offsets, rows_all, keys, heads, width):
     ys = refs[:outer]
     kvs = refs[outer:outer + INNER]
-    begin = [first, first] + [0] * (INNER - 2)
     outs = refs[outer + INNER:outer + INNER + len(offsets)]
     bias_ref, q_ref = refs[outer + INNER + len(offsets):]
     _, z, r = place()
@@ -249,11 +258,19 @@
         functools.partial(split_queries_kernel, outer=outer, width=width),
         [query_block], [shape((outer, rows, width), bf16)] * INNER,
     )
-    kv_out = call(
+    caches = [pltpu.with_memory_space_constraint(x, pltpu.MemorySpace.HBM) for x in (cache_keys, stored_values)]
+    kv_out = pl.pallas_call(
         functools.partial(split_cache_kernel, groups=groups, copies=copies),
-        [live_counts, cache_keys, stored_values],
-        [shape((len(p), 2 * keys + 16, HEAD_SIZE), bf16) for k, p in groups], scalars=1,
-    )
+        out_shape=tuple(
+            shape((len(p), 2 * keys + 16, HEAD_SIZE), bf16) for k, p in groups
+        ),
+        in_specs=[sspec()] + [pl.BlockSpec(memory_space=pltpu.MemorySpace.HBM)] * 2,
+        out_specs=tuple(vspec() for _ in groups),
+        scratch_shapes=[pltpu.VMEM(x.shape, x.dtype) for x in caches]
+        + [pltpu.SemaphoreType.DMA((2,))],
+        name="split_cache",
+        compiler_params=pltpu.CompilerParams(vmem_limit_bytes=8 << 20),
+    )(live_counts, *caches)
     q_got = {k: swap(q_out[k], k) for k in (2, 3, 1)}
     kv_pair = swap(kv_out[1], 1)
     kv_far = [
@@ -270,22 +287,20 @@
     w_other = swap(w_send, 1)
 
     partial_of = {}
-    at = 0
-    for i, offsets in enumerate(phases):
-        size = len(offsets)
-        outs = call(
+    for near, kk in enumerate(order):
+        i = [kk in p for p in phases].index(True)
+        far = phases[i].index(kk)
+        (out,) = call(
             functools.partial(
-                attention_kernel, outer=outer, first=at, offsets=offsets, rows_all=rows_all,
-                keys=keys, heads=heads, width=width,
+                attention_kernel, outer=outer, begin=(near, near) + (far,) * (INNER - 2),
+                offsets=[kk], rows_all=rows_all, keys=keys, heads=heads, width=width,
             ),
             [first_position, *ys, kv_out[0], kv_pair, kv_far[i][2], kv_far[i][3]],
-            [shape((rows_all + 16, width), bf16)] * size,
+            [shape((rows_all + 16, width), bf16)],
             scratch=[pltpu.VMEM((rows_all, INNER * keys), f32), pltpu.VMEM((rows_all, width), f32)],
-            scalars=1, flops=4 * rows_all * INNER * keys * width * size, limit=20,
+            scalars=1, flops=4 * rows_all * INNER * keys * width, limit=16,
         )
-        at += size
-        for kk, out in zip(offsets, outs):
-            partial_of[kk] = swap(out, kk * INNER) if kk else out
+        partial_of[kk] = swap(out, kk * INNER) if kk else out
 
     (merged,) = call(
         functools.partial(merge_kernel, sources=outer, rows_all=rows_all, heads=heads, width=width),

time: 80 us -> 79.4 us (level)
  waiting for transfers between devices: 43 us -> 37.7 us
  starting transfers between devices: 24.6 us -> 27.1 us
  Pallas kernels: 7.86 us -> 9.54 us
    ppermute x26, waiting for transfers between devices: 43 us -> 37.7 us  [swap(): return lax.ppermute(x, 'seq', [(i, i ^ k) for i in range(devices)])]
    ppermute x26, starting transfers between devices: 24.6 us -> 27.1 us  [swap(): return lax.ppermute(x, 'seq', [(i, i ^ k) for i in range(devices)])]
    pallas_call x0 -> x1, Pallas kernels: none -> 2.11 us  [layer(): pl.pallas_call(functools.partial(split_cache_kernel, groups=groups, copie...]
    unnamed x10 -> x6, local copies, waits for them, and re-layouts: 2.03 us -> 2.03 us
  transfers between devices with their start and end apart: 26 -> 26, of which waited for: 16 -> 12; matrix products, arithmetic and copies ran while one was open for 0% -> 0% of each run, Pallas kernels for 8% -> 10%
where the time goes in v4:
time: 79.4 us; the launch traced here: 77.9 us
  waiting for transfers between devices  37.7 us (47%)
  starting transfers between devices  27.1 us (34%)
  Pallas kernels  9.54 us (12%)
  local copies, waits for them, and re-layouts  2.03 us (3%)
  between operations  1.45 us (2%)
    ppermute x26, waiting for transfers between devices, swap(): return lax.ppermute(x, 'seq', [(i, i ^ k) for i in range(devices)])  37.7 us
    ppermute x26, starting transfers between devices, swap(): return lax.ppermute(x, 'seq', [(i, i ^ k) for i in range(devices)])  27.1 us
    pallas_call x13, Pallas kernels, call(): pl.pallas_call(kernel, out_shape=tuple(outs), in_specs=in_specs, out_spec...  7.43 us
    pallas_call x1, Pallas kernels, layer(): pl.pallas_call(functools.partial(split_cache_kernel, groups=groups, copie...  2.11 us
    unnamed x6, local copies, waits for them, and re-layouts  2.03 us
  transfers between devices with their start and end apart: 26, of which 12 were waited for; matrix products, arithmetic and copies ran while one was open for 0% of the time, Pallas kernels for 10%

profile of v4, /device:TPU:0, one launch (start us, length us, event | category | flops | bytes accessed | tf_op | source)
XLA Modules:
  0.0 77.9 jit_solution(12034633171612586838)
XLA Ops:
  0.0 1.8 %copy-done = bf16[256,5376]{1,0:T(8,128)(2,1)S(1)} copy-done((bf16[256,5376]{1,0:T(8,128)(2,1)S(1)}, bf16[256,5376]{1,0:T(8,128)(2,1)}, u32[]{:S(2)}) %copy-start) | copy-done | bytes 2752536
  3.3 2.6 %collective-permute-start.1 = (bf16[4,16,256]{2,1,0:T(8,128)(2,1)S(1)}, bf16[4,16,256]{2,1,0:T(8,128)(2,1)S(1)}, u32[]{:S(2)}, u32[]{:S(2)}) collective-permute-start(bf16[4,16,256]{2,1,0:T(8,128)(2,1)S(1)} %get-tuple-element.29), channel_id=1, source_target_pairs={{0,2},{1,3},{2,0},{3,1},{4,6},{5,7},{6,4},{7,5},{8,10},{9,11},{10,... | collective-permute-start | bytes 98312 | tf_op jit(solution)/shard_map/ppermute | solution.py:252
  6.5 2.1 %split_cache.1 = (bf16[4,528,128]{2,1,0:T(8,128)(2,1)S(1)}, bf16[4,528,128]{2,1,0:T(8,128)(2,1)S(1)}, bf16[2,528,128]{2,1,0:T(8,128)(2,1)S(1)}, bf16[2,528,128]{...) custom-call(s32[1]{0:T(128)S(6)} %copy.7.live_ref, ...), custom_call_target="tpu_custom_call" | custom-call | tf_op jit(solution)/shard_map/split_cache/pallas_call | solution.py:262
  9.2 1.8 %collective-permute-start.3 = (bf16[4,4,16,256]{3,2,1,0:T(8,128)(2,1)S(1)}, bf16[4,4,16,256]{3,2,1,0:T(8,128)(2,1)S(1)}, u32[]{:S(2)}, u32[]{:S(2)}) collective-permute-start(bf16[4,4,16,256]{3,2,1,0:T(8,128)(2,1)S(1)} %pad_maximum_fusion.refs_0_), channel_id=1, source_target_pairs={{0,4},{1,5},{2,6},{3,7},{4,0},{5,1},{6,2},{7,3},{8,12},{9,13},{10,... | collective-permute-start | bytes 393224 | tf_op jit(solution)/shard_map/ppermute | solution.py:252
  11.0 1.5 %collective-permute-start.12 = (bf16[2,528,128]{2,1,0:T(8,128)(2,1)S(1)}, bf16[2,528,128]{2,1,0:T(8,128)(2,1)S(1)}, u32[]{:S(2)}, u32[]{:S(2)}) collective-permute-start(bf16[2,528,128]{2,1,0:T(8,128)(2,1)S(1)} %get-tuple-element.37), channel_id=1, source_target_pairs={{0,2},{1,3},{2,0},{3,1},{4,6},{5,7},{6,4},{7,5},{8,10},{9,11},{10,... | collective-permute-start | bytes 811016 | tf_op jit(solution)/shard_map/ppermute | solution.py:252
  12.5 2.6 %collective-permute-start.4 = (bf16[4,4,16,256]{3,2,1,0:T(8,128)(2,1)S(1)}, bf16[4,4,16,256]{3,2,1,0:T(8,128)(2,1)S(1)}, u32[]{:S(2)}, u32[]{:S(2)}) collective-permute-start(bf16[4,4,16,256]{3,2,1,0:T(8,128)(2,1)S(1)} %pad_maximum_fusion.refs_0_), channel_id=1, source_target_pairs={{0,8},{1,9},{2,10},{3,11},{4,12},{5,13},{6,14},{7,15},{8,0},{9,1},... | collective-permute-start | bytes 393224 | tf_op jit(solution)/shard_map/ppermute | solution.py:252
  15.4 5.8 %collective-permute-done.4.refs_2_ = bf16[4,4,16,256]{3,2,1,0:T(8,128)(2,1)S(1)} collective-permute-done((bf16[4,4,16,256]{3,2,1,0:T(8,128)(2,1)S(1)}, bf16[4,4,16,256]{3,2,1,0:T(8,128)(2,1)S(1)}, u32[]{:S(2)}, u32[]{:S(2)}) %collective-permute-start.4) | collective-permute-done | bytes 131104 | tf_op jit(solution)/shard_map/ppermute | solution.py:252
  21.2 2.7 %collective-permute-start.5 = (bf16[4,4,16,256]{3,2,1,0:T(8,128)(2,1)S(1)}, bf16[4,4,16,256]{3,2,1,0:T(8,128)(2,1)S(1)}, u32[]{:S(2)}, u32[]{:S(2)}) collective-permute-start(bf16[4,4,16,256]{3,2,1,0:T(8,128)(2,1)S(1)} %pad_maximum_fusion.refs_0_), channel_id=1, source_target_pairs={{0,12},{1,13},{2,14},{3,15},{4,8},{5,9},{6,10},{7,11},{8,4},{9,5},... | collective-permute-start | bytes 393224 | tf_op jit(solution)/shard_map/ppermute | solution.py:252
  23.9 4.0 %collective-permute-done.5.refs_3_ = bf16[4,4,16,256]{3,2,1,0:T(8,128)(2,1)S(1)} collective-permute-done((bf16[4,4,16,256]{3,2,1,0:T(8,128)(2,1)S(1)}, bf16[4,4,16,256]{3,2,1,0:T(8,128)(2,1)S(1)}, u32[]{:S(2)}, u32[]{:S(2)}) %collective-permute-start.5) | collective-permute-done | bytes 131104 | tf_op jit(solution)/shard_map/ppermute | solution.py:252
  28.6 1.4 %collective-permute-start.7 = (bf16[1,528,128]{2,1,0:T(8,128)(2,1)S(1)}, bf16[1,528,128]{2,1,0:T(8,128)(2,1)S(1)}, u32[]{:S(2)}, u32[]{:S(2)}) collective-permute-start(bf16[1,528,128]{2,1,0:T(8,128)(2,1)S(1)} %get-tuple-element.33), channel_id=1, source_target_pairs={{0,2},{1,3},{2,0},{3,1},{4,6},{5,7},{6,4},{7,5},{8,10},{9,11},{10,... | collective-permute-start | bytes 405512 | tf_op jit(solution)/shard_map/ppermute | solution.py:252
  30.7 1.2 %collective-permute-start.8 = (bf16[1,528,128]{2,1,0:T(8,128)(2,1)S(1)}, bf16[1,528,128]{2,1,0:T(8,128)(2,1)S(1)}, u32[]{:S(2)}, u32[]{:S(2)}) collective-permute-start(bf16[1,528,128]{2,1,0:T(8,128)(2,1)S(1)} %get-tuple-element.34), channel_id=1, source_target_pairs={{0,3},{1,2},{2,1},{3,0},{4,7},{5,6},{6,5},{7,4},{8,11},{9,10},{10,... | collective-permute-start | bytes 405512 | tf_op jit(solution)/shard_map/ppermute | solution.py:252
  34.4 2.8 %collective-permute-start.15 = (bf16[272,256]{1,0:T(8,128)(2,1)S(1)}, bf16[272,256]{1,0:T(8,128)(2,1)S(1)}, u32[]{:S(2)}, u32[]{:S(2)}) collective-permute-start(bf16[272,256]{1,0:T(8,128)(2,1)S(1)} %shard_map.68), channel_id=1, source_target_pairs={{0,12},{1,13},{2,14},{3,15},{4,8},{5,9},{6,10},{7,11},{8,4},{9,5},... | collective-permute-start | bytes 417800 | tf_op jit(solution)/shard_map/ppermute | solution.py:252
  38.5 1.7 %collective-permute-start.11 = (bf16[272,256]{1,0:T(8,128)(2,1)S(1)}, bf16[272,256]{1,0:T(8,128)(2,1)S(1)}, u32[]{:S(2)}, u32[]{:S(2)}) collective-permute-start(bf16[272,256]{1,0:T(8,128)(2,1)S(1)} %shard_map.66), channel_id=1, source_target_pairs={{0,4},{1,5},{2,6},{3,7},{4,0},{5,1},{6,2},{7,3},{8,12},{9,13},{10,... | collective-permute-start | bytes 417800 | tf_op jit(solution)/shard_map/ppermute | solution.py:252
  40.2 1.6 %collective-permute-done.8.refs_7_ = bf16[1,528,128]{2,1,0:T(8,128)(2,1)S(1)} collective-permute-done((bf16[1,528,128]{2,1,0:T(8,128)(2,1)S(1)}, bf16[1,528,128]{2,1,0:T(8,128)(2,1)S(1)}, u32[]{:S(2)}, u32[]{:S(2)}) %collective-permute-start.8) | collective-permute-done | bytes 135200 | tf_op jit(solution)/shard_map/ppermute | solution.py:252
  43.0 5.8 %collective-permute-done.14.refs_2_ = bf16[272,256]{1,0:T(8,128)(2,1)S(1)} collective-permute-done((bf16[272,256]{1,0:T(8,128)(2,1)S(1)}, bf16[272,256]{1,0:T(8,128)(2,1)S(1)}, u32[]{:S(2)}, u32[]{:S(2)}) %collective-permute-start.14) | collective-permute-done | bytes 139296 | tf_op jit(solution)/shard_map/ppermute | solution.py:252
  49.4 1.3 %collective-permute-done.16.other_ref = bf16[256,256]{1,0:T(8,128)(2,1)S(1)} collective-permute-done((bf16[256,256]{1,0:T(8,128)(2,1)S(1)}, bf16[256,256]{1,0:T(8,128)(2,1)S(1)}, u32[]{:S(2)}, u32[]{:S(2)}) %collective-permute-start.16) | collective-permute-done | bytes 131104 | tf_op jit(solution)/shard_map/ppermute | solution.py:252
  51.7 1.5 %collective-permute-start.23 = (bf16[32,2688]{1,0:T(8,128)(2,1)S(1)}, bf16[32,2688]{1,0:T(8,128)(2,1)S(1)}, u32[]{:S(2)}, u32[]{:S(2)}) collective-permute-start(bf16[32,2688]{1,0:T(8,128)(2,1)S(1)} %get-tuple-element.46), channel_id=1, source_target_pairs={{0,2},{1,3},{2,0},{3,1},{4,6},{5,7},{6,4},{7,5},{8,10},{9,11},{10,... | collective-permute-start | bytes 516104 | tf_op jit(solution)/shard_map/ppermute | solution.py:252
  53.8 1.5 %collective-permute-start.19 = (bf16[32,2688]{1,0:T(8,128)(2,1)S(1)}, bf16[32,2688]{1,0:T(8,128)(2,1)S(1)}, u32[]{:S(2)}, u32[]{:S(2)}) collective-permute-start(bf16[32,2688]{1,0:T(8,128)(2,1)S(1)} %get-tuple-element.42), channel_id=1, source_target_pairs={{0,2},{1,3},{2,0},{3,1},{4,6},{5,7},{6,4},{7,5},{8,10},{9,11},{10,... | collective-permute-start | bytes 516104 | tf_op jit(solution)/shard_map/ppermute | solution.py:252
  55.8 3.2 %collective-permute-done.23.got_ref = bf16[32,2688]{1,0:T(8,128)(2,1)S(1)} collective-permute-done((bf16[32,2688]{1,0:T(8,128)(2,1)S(1)}, bf16[32,2688]{1,0:T(8,128)(2,1)S(1)}, u32[]{:S(2)}, u32[]{:S(2)}) %collective-permute-start.23) | collective-permute-done | bytes 172064 | tf_op jit(solution)/shard_map/ppermute | solution.py:252
  59.2 3.6 %collective-permute-done.21.got_ref = bf16[32,2688]{1,0:T(8,128)(2,1)S(1)} collective-permute-done((bf16[32,2688]{1,0:T(8,128)(2,1)S(1)}, bf16[32,2688]{1,0:T(8,128)(2,1)S(1)}, u32[]{:S(2)}, u32[]{:S(2)}) %collective-permute-start.21) | collective-permute-done | bytes 172064 | tf_op jit(solution)/shard_map/ppermute | solution.py:252
  62.9 3.5 %collective-permute-done.19.got_ref = bf16[32,2688]{1,0:T(8,128)(2,1)S(1)} collective-permute-done((bf16[32,2688]{1,0:T(8,128)(2,1)S(1)}, bf16[32,2688]{1,0:T(8,128)(2,1)S(1)}, u32[]{:S(2)}, u32[]{:S(2)}) %collective-permute-start.19) | collective-permute-done | bytes 172064 | tf_op jit(solution)/shard_map/ppermute | solution.py:252
  66.5 2.0 %collective-permute-start.20 = (bf16[32,2688]{1,0:T(8,128)(2,1)S(1)}, bf16[32,2688]{1,0:T(8,128)(2,1)S(1)}, u32[]{:S(2)}, u32[]{:S(2)}) collective-permute-start(bf16[32,2688]{1,0:T(8,128)(2,1)S(1)} %shard_map.72), channel_id=1, source_target_pairs={{0,12},{1,13},{2,14},{3,15},{4,8},{5,9},{6,10},{7,11},{8,4},{9,5},... | collective-permute-start | bytes 516104 | tf_op jit(solution)/shard_map/ppermute | solution.py:252
  69.3 6.4 %collective-permute-done.22.refs_1_ = bf16[32,2688]{1,0:T(8,128)(2,1)S(1)} collective-permute-done((bf16[32,2688]{1,0:T(8,128)(2,1)S(1)}, bf16[32,2688]{1,0:T(8,128)(2,1)S(1)}, u32[]{:S(2)}, u32[]{:S(2)}) %collective-permute-start.22) | collective-permute-done | bytes 172064 | tf_op jit(solution)/shard_map/ppermute | solution.py:252
  75.9 1.3 %collective-permute-done.25.other_ref = bf16[16,2688]{1,0:T(8,128)(2,1)S(1)} collective-permute-done((bf16[16,2688]{1,0:T(8,128)(2,1)S(1)}, bf16[16,2688]{1,0:T(8,128)(2,1)S(1)}, u32[]{:S(2)}, u32[]{:S(2)}) %collective-permute-start.25) | collective-permute-done | bytes 86048 | tf_op jit(solution)/shard_map/ppermute | solution.py:252
  (49 shorter events, 12.6 us)
Async XLA Ops:
  1.9 48.9 %collective-permute-start.17 = (bf16[256,2688]{1,0:T(8,128)(2,1)S(1)}, bf16[256,2688]{1,0:T(8,128)(2,1)S(1)}, u32[]{:S(2)}, u32[]{:S(2)}) collective-permute-start(bf16[256,2688]{1,0:T(8,128)(2,1)S(1)} %shard_map.70), channel_id=1, source_target_pairs={{0,1},{1,0},{2,3},{3,2},{4,5},{5,4},{6,7},{7,6},{8,9},{9,8},{10,11... | collective-permute-start | bytes 4128776 | tf_op jit(solution)/shard_map/ppermute | solution.py:252
  2.7 6.2 %collective-permute-start = (bf16[4,16,256]{2,1,0:T(8,128)(2,1)S(1)}, bf16[4,16,256]{2,1,0:T(8,128)(2,1)S(1)}, u32[]{:S(2)}, u32[]{:S(2)}) collective-permute-start(bf16[4,16,256]{2,1,0:T(8,128)(2,1)S(1)} %get-tuple-element.28), channel_id=1, source_target_pairs={{0,1},{1,0},{2,3},{3,2},{4,5},{5,4},{6,7},{7,6},{8,9},{9,8},{10,11... | collective-permute-start | bytes 98312 | tf_op jit(solution)/shard_map/ppermute | solution.py:252
  3.3 5.6 %collective-permute-start.1 = (bf16[4,16,256]{2,1,0:T(8,128)(2,1)S(1)}, bf16[4,16,256]{2,1,0:T(8,128)(2,1)S(1)}, u32[]{:S(2)}, u32[]{:S(2)}) collective-permute-start(bf16[4,16,256]{2,1,0:T(8,128)(2,1)S(1)} %get-tuple-element.29), channel_id=1, source_target_pairs={{0,2},{1,3},{2,0},{3,1},{4,6},{5,7},{6,4},{7,5},{8,10},{9,11},{10,... | collective-permute-start | bytes 98312 | tf_op jit(solution)/shard_map/ppermute | solution.py:252
  5.8 3.4 %collective-permute-start.2 = (bf16[4,16,256]{2,1,0:T(8,128)(2,1)S(1)}, bf16[4,16,256]{2,1,0:T(8,128)(2,1)S(1)}, u32[]{:S(2)}, u32[]{:S(2)}) collective-permute-start(bf16[4,16,256]{2,1,0:T(8,128)(2,1)S(1)} %get-tuple-element.30), channel_id=1, source_target_pairs={{0,3},{1,2},{2,1},{3,0},{4,7},{5,6},{6,5},{7,4},{8,11},{9,10},{10,... | collective-permute-start | bytes 98312 | tf_op jit(solution)/shard_map/ppermute | solution.py:252
  8.7 22.0 %collective-permute-start.6 = (bf16[4,528,128]{2,1,0:T(8,128)(2,1)S(1)}, bf16[4,528,128]{2,1,0:T(8,128)(2,1)S(1)}, u32[]{:S(2)}, u32[]{:S(2)}) collective-permute-start(bf16[4,528,128]{2,1,0:T(8,128)(2,1)S(1)} %get-tuple-element.32), channel_id=1, source_target_pairs={{0,1},{1,0},{2,3},{3,2},{4,5},{5,4},{6,7},{7,6},{8,9},{9,8},{10,11... | collective-permute-start | bytes 1622024 | tf_op jit(solution)/shard_map/ppermute | solution.py:252
  9.2 5.9 %collective-permute-start.3 = (bf16[4,4,16,256]{3,2,1,0:T(8,128)(2,1)S(1)}, bf16[4,4,16,256]{3,2,1,0:T(8,128)(2,1)S(1)}, u32[]{:S(2)}, u32[]{:S(2)}) collective-permute-start(bf16[4,4,16,256]{3,2,1,0:T(8,128)(2,1)S(1)} %pad_maximum_fusion.refs_0_), channel_id=1, source_target_pairs={{0,4},{1,5},{2,6},{3,7},{4,0},{5,1},{6,2},{7,3},{8,12},{9,13},{10,... | collective-permute-start | bytes 393224 | tf_op jit(solution)/shard_map/ppermute | solution.py:252
  11.0 17.0 %collective-permute-start.12 = (bf16[2,528,128]{2,1,0:T(8,128)(2,1)S(1)}, bf16[2,528,128]{2,1,0:T(8,128)(2,1)S(1)}, u32[]{:S(2)}, u32[]{:S(2)}) collective-permute-start(bf16[2,528,128]{2,1,0:T(8,128)(2,1)S(1)} %get-tuple-element.37), channel_id=1, source_target_pairs={{0,2},{1,3},{2,0},{3,1},{4,6},{5,7},{6,4},{7,5},{8,10},{9,11},{10,... | collective-permute-start | bytes 811016 | tf_op jit(solution)/shard_map/ppermute | solution.py:252
  12.5 8.7 %collective-permute-start.4 = (bf16[4,4,16,256]{3,2,1,0:T(8,128)(2,1)S(1)}, bf16[4,4,16,256]{3,2,1,0:T(8,128)(2,1)S(1)}, u32[]{:S(2)}, u32[]{:S(2)}) collective-permute-start(bf16[4,4,16,256]{3,2,1,0:T(8,128)(2,1)S(1)} %pad_maximum_fusion.refs_0_), channel_id=1, source_target_pairs={{0,8},{1,9},{2,10},{3,11},{4,12},{5,13},{6,14},{7,15},{8,0},{9,1},... | collective-permute-start | bytes 393224 | tf_op jit(solution)/shard_map/ppermute | solution.py:252
  15.1 13.5 %collective-permute-start.13 = (bf16[2,528,128]{2,1,0:T(8,128)(2,1)S(1)}, bf16[2,528,128]{2,1,0:T(8,128)(2,1)S(1)}, u32[]{:S(2)}, u32[]{:S(2)}) collective-permute-start(bf16[2,528,128]{2,1,0:T(8,128)(2,1)S(1)} %get-tuple-element.38), channel_id=1, source_target_pairs={{0,3},{1,2},{2,1},{3,0},{4,7},{5,6},{6,5},{7,4},{8,11},{9,10},{10,... | collective-permute-start | bytes 811016 | tf_op jit(solution)/shard_map/ppermute | solution.py:252
  21.2 6.8 %collective-permute-start.5 = (bf16[4,4,16,256]{3,2,1,0:T(8,128)(2,1)S(1)}, bf16[4,4,16,256]{3,2,1,0:T(8,128)(2,1)S(1)}, u32[]{:S(2)}, u32[]{:S(2)}) collective-permute-start(bf16[4,4,16,256]{3,2,1,0:T(8,128)(2,1)S(1)} %pad_maximum_fusion.refs_0_), channel_id=1, source_target_pairs={{0,12},{1,13},{2,14},{3,15},{4,8},{5,9},{6,10},{7,11},{8,4},{9,5},... | collective-permute-start | bytes 393224 | tf_op jit(solution)/shard_map/ppermute | solution.py:252
  28.0 6.4 %collective-permute-start.10 = (bf16[1,528,128]{2,1,0:T(8,128)(2,1)S(1)}, bf16[1,528,128]{2,1,0:T(8,128)(2,1)S(1)}, u32[]{:S(2)}, u32[]{:S(2)}) collective-permute-start(bf16[1,528,128]{2,1,0:T(8,128)(2,1)S(1)} %get-tuple-element.36), channel_id=1, source_target_pairs={{0,3},{1,2},{2,1},{3,0},{4,7},{5,6},{6,5},{7,4},{8,11},{9,10},{10,... | collective-permute-start | bytes 405512 | tf_op jit(solution)/shard_map/ppermute | solution.py:252
  28.0 9.2 %collective-permute-start.9 = (bf16[1,528,128]{2,1,0:T(8,128)(2,1)S(1)}, bf16[1,528,128]{2,1,0:T(8,128)(2,1)S(1)}, u32[]{:S(2)}, u32[]{:S(2)}) collective-permute-start(bf16[1,528,128]{2,1,0:T(8,128)(2,1)S(1)} %get-tuple-element.35), channel_id=1, source_target_pairs={{0,2},{1,3},{2,0},{3,1},{4,6},{5,7},{6,4},{7,5},{8,10},{9,11},{10,... | collective-permute-start | bytes 405512 | tf_op jit(solution)/shard_map/ppermute | solution.py:252
  28.6 9.8 %collective-permute-start.7 = (bf16[1,528,128]{2,1,0:T(8,128)(2,1)S(1)}, bf16[1,528,128]{2,1,0:T(8,128)(2,1)S(1)}, u32[]{:S(2)}, u32[]{:S(2)}) collective-permute-start(bf16[1,528,128]{2,1,0:T(8,128)(2,1)S(1)} %get-tuple-element.33), channel_id=1, source_target_pairs={{0,2},{1,3},{2,0},{3,1},{4,6},{5,7},{6,4},{7,5},{8,10},{9,11},{10,... | collective-permute-start | bytes 405512 | tf_op jit(solution)/shard_map/ppermute | solution.py:252
  30.7 11.1 %collective-permute-start.8 = (bf16[1,528,128]{2,1,0:T(8,128)(2,1)S(1)}, bf16[1,528,128]{2,1,0:T(8,128)(2,1)S(1)}, u32[]{:S(2)}, u32[]{:S(2)}) collective-permute-start(bf16[1,528,128]{2,1,0:T(8,128)(2,1)S(1)} %get-tuple-element.34), channel_id=1, source_target_pairs={{0,3},{1,2},{2,1},{3,0},{4,7},{5,6},{6,5},{7,4},{8,11},{9,10},{10,... | collective-permute-start | bytes 405512 | tf_op jit(solution)/shard_map/ppermute | solution.py:252
  34.4 8.6 %collective-permute-start.15 = (bf16[272,256]{1,0:T(8,128)(2,1)S(1)}, bf16[272,256]{1,0:T(8,128)(2,1)S(1)}, u32[]{:S(2)}, u32[]{:S(2)}) collective-permute-start(bf16[272,256]{1,0:T(8,128)(2,1)S(1)} %shard_map.68), channel_id=1, source_target_pairs={{0,12},{1,13},{2,14},{3,15},{4,8},{5,9},{6,10},{7,11},{8,4},{9,5},... | collective-permute-start | bytes 417800 | tf_op jit(solution)/shard_map/ppermute | solution.py:252
  37.2 11.6 %collective-permute-start.14 = (bf16[272,256]{1,0:T(8,128)(2,1)S(1)}, bf16[272,256]{1,0:T(8,128)(2,1)S(1)}, u32[]{:S(2)}, u32[]{:S(2)}) collective-permute-start(bf16[272,256]{1,0:T(8,128)(2,1)S(1)} %shard_map.67), channel_id=1, source_target_pairs={{0,8},{1,9},{2,10},{3,11},{4,12},{5,13},{6,14},{7,15},{8,0},{9,1},... | collective-permute-start | bytes 417800 | tf_op jit(solution)/shard_map/ppermute | solution.py:252
  38.5 10.4 %collective-permute-start.11 = (bf16[272,256]{1,0:T(8,128)(2,1)S(1)}, bf16[272,256]{1,0:T(8,128)(2,1)S(1)}, u32[]{:S(2)}, u32[]{:S(2)}) collective-permute-start(bf16[272,256]{1,0:T(8,128)(2,1)S(1)} %shard_map.66), channel_id=1, source_target_pairs={{0,4},{1,5},{2,6},{3,7},{4,0},{5,1},{6,2},{7,3},{8,12},{9,13},{10,... | collective-permute-start | bytes 417800 | tf_op jit(solution)/shard_map/ppermute | solution.py:252
  51.7 7.3 %collective-permute-start.23 = (bf16[32,2688]{1,0:T(8,128)(2,1)S(1)}, bf16[32,2688]{1,0:T(8,128)(2,1)S(1)}, u32[]{:S(2)}, u32[]{:S(2)}) collective-permute-start(bf16[32,2688]{1,0:T(8,128)(2,1)S(1)} %get-tuple-element.46), channel_id=1, source_target_pairs={{0,2},{1,3},{2,0},{3,1},{4,6},{5,7},{6,4},{7,5},{8,10},{9,11},{10,... | collective-permute-start | bytes 516104 | tf_op jit(solution)/shard_map/ppermute | solution.py:252
  53.3 9.5 %collective-permute-start.21 = (bf16[32,2688]{1,0:T(8,128)(2,1)S(1)}, bf16[32,2688]{1,0:T(8,128)(2,1)S(1)}, u32[]{:S(2)}, u32[]{:S(2)}) collective-permute-start(bf16[32,2688]{1,0:T(8,128)(2,1)S(1)} %get-tuple-element.44), channel_id=1, source_target_pairs={{0,2},{1,3},{2,0},{3,1},{4,6},{5,7},{6,4},{7,5},{8,10},{9,11},{10,... | collective-permute-start | bytes 516104 | tf_op jit(solution)/shard_map/ppermute | solution.py:252
  53.8 12.6 %collective-permute-start.19 = (bf16[32,2688]{1,0:T(8,128)(2,1)S(1)}, bf16[32,2688]{1,0:T(8,128)(2,1)S(1)}, u32[]{:S(2)}, u32[]{:S(2)}) collective-permute-start(bf16[32,2688]{1,0:T(8,128)(2,1)S(1)} %get-tuple-element.42), channel_id=1, source_target_pairs={{0,2},{1,3},{2,0},{3,1},{4,6},{5,7},{6,4},{7,5},{8,10},{9,11},{10,... | collective-permute-start | bytes 516104 | tf_op jit(solution)/shard_map/ppermute | solution.py:252
  55.3 14.0 %collective-permute-start.18 = (bf16[32,2688]{1,0:T(8,128)(2,1)S(1)}, bf16[32,2688]{1,0:T(8,128)(2,1)S(1)}, u32[]{:S(2)}, u32[]{:S(2)}) collective-permute-start(bf16[32,2688]{1,0:T(8,128)(2,1)S(1)} %get-tuple-element.40), channel_id=1, source_target_pairs={{0,2},{1,3},{2,0},{3,1},{4,6},{5,7},{6,4},{7,5},{8,10},{9,11},{10,... | collective-permute-start | bytes 516104 | tf_op jit(solution)/shard_map/ppermute | solution.py:252
  59.1 10.2 %collective-permute-start.24 = (bf16[32,2688]{1,0:T(8,128)(2,1)S(1)}, bf16[32,2688]{1,0:T(8,128)(2,1)S(1)}, u32[]{:S(2)}, u32[]{:S(2)}) collective-permute-start(bf16[32,2688]{1,0:T(8,128)(2,1)S(1)} %shard_map.74), channel_id=1, source_target_pairs={{0,4},{1,5},{2,6},{3,7},{4,0},{5,1},{6,2},{7,3},{8,12},{9,13},{10,... | collective-permute-start | bytes 516104 | tf_op jit(solution)/shard_map/ppermute | solution.py:252
  62.8 12.9 %collective-permute-start.22 = (bf16[32,2688]{1,0:T(8,128)(2,1)S(1)}, bf16[32,2688]{1,0:T(8,128)(2,1)S(1)}, u32[]{:S(2)}, u32[]{:S(2)}) collective-permute-start(bf16[32,2688]{1,0:T(8,128)(2,1)S(1)} %shard_map.73), channel_id=1, source_target_pairs={{0,8},{1,9},{2,10},{3,11},{4,12},{5,13},{6,14},{7,15},{8,0},{9,1},... | collective-permute-start | bytes 516104 | tf_op jit(solution)/shard_map/ppermute | solution.py:252
  66.5 9.2 %collective-permute-start.20 = (bf16[32,2688]{1,0:T(8,128)(2,1)S(1)}, bf16[32,2688]{1,0:T(8,128)(2,1)S(1)}, u32[]{:S(2)}, u32[]{:S(2)}) collective-permute-start(bf16[32,2688]{1,0:T(8,128)(2,1)S(1)} %shard_map.72), channel_id=1, source_target_pairs={{0,12},{1,13},{2,14},{3,15},{4,8},{5,9},{6,10},{7,11},{8,4},{9,5},... | collective-permute-start | bytes 516104 | tf_op jit(solution)/shard_map/ppermute | solution.py:252
  (5 other events, 19.0 us)

commit v5 on v4

--- a/solution.py
+++ b/solution.py
@@ -310,7 +310,8 @@
     other = swap(merged, 1)
 
     span = 2 * rows
-    term_groups = [[kk] for kk in order]
+    turns = [outer - 1, 1] + order[1:-2] + [0]
+    term_groups = [[kk] for kk in turns]
     terms = call(
         functools.partial(project_kernel, groups=term_groups, rows=rows, blocks=blocks),
         [merged, other, out_weight, w_other],
@@ -321,7 +322,7 @@
     sends, keeps = terms[:outer], terms[outer:]
     gots = [swap(x, 2) for x in sends]
     parts = []
-    for i, kk in enumerate(order[:-1]):
+    for i, kk in enumerate(turns[:-1]):
         (part,) = call(first_sum_kernel, [keeps[i], gots[i]], [shape((span, half), bf16)])
         parts.append(swap(part, kk * INNER))
     mine, theirs = call(

time: 79.4 us -> 77 us (0.970); the launches traced: 77.9 us -> 76.8 us
  waiting for transfers between devices: 37.7 us -> 36.6 us
    ppermute x26, waiting for transfers between devices: 37.7 us -> 36.6 us  [swap(): return lax.ppermute(x, 'seq', [(i, i ^ k) for i in range(devices)])]
where the time goes in v5:
time: 77 us; the launch traced here: 76.8 us
  waiting for transfers between devices  36.6 us (48%)
  starting transfers between devices  27.1 us (35%)
  Pallas kernels  9.54 us (12%)
  local copies, waits for them, and re-layouts  2.03 us (3%)
  between operations  1.45 us (2%)
    ppermute x26, waiting for transfers between devices, swap(): return lax.ppermute(x, 'seq', [(i, i ^ k) for i in range(devices)])  36.6 us
    ppermute x26, starting transfers between devices, swap(): return lax.ppermute(x, 'seq', [(i, i ^ k) for i in range(devices)])  27.1 us
    pallas_call x13, Pallas kernels, call(): pl.pallas_call(kernel, out_shape=tuple(outs), in_specs=in_specs, out_spec...  7.43 us
    pallas_call x1, Pallas kernels, layer(): pl.pallas_call(functools.partial(split_cache_kernel, groups=groups, copie...  2.11 us
    unnamed x6, local copies, waits for them, and re-layouts  2.03 us
  transfers between devices with their start and end apart: 26, of which 12 were waited for; matrix products, arithmetic and copies ran while one was open for 0% of the time, Pallas kernels for 10%

profile of v5, /device:TPU:0, one launch (start us, length us, event | category | flops | bytes accessed | tf_op | source)
XLA Modules:
  0.0 76.8 jit_solution(10728664770260923369)
XLA Ops:
  0.0 1.8 %copy-done = bf16[256,5376]{1,0:T(8,128)(2,1)S(1)} copy-done((bf16[256,5376]{1,0:T(8,128)(2,1)S(1)}, bf16[256,5376]{1,0:T(8,128)(2,1)}, u32[]{:S(2)}) %copy-start) | copy-done | bytes 2752536
  3.3 2.6 %collective-permute-start.1 = (bf16[4,16,256]{2,1,0:T(8,128)(2,1)S(1)}, bf16[4,16,256]{2,1,0:T(8,128)(2,1)S(1)}, u32[]{:S(2)}, u32[]{:S(2)}) collective-permute-start(bf16[4,16,256]{2,1,0:T(8,128)(2,1)S(1)} %get-tuple-element.29), channel_id=1, source_target_pairs={{0,2},{1,3},{2,0},{3,1},{4,6},{5,7},{6,4},{7,5},{8,10},{9,11},{10,... | collective-permute-start | bytes 98312 | tf_op jit(solution)/shard_map/ppermute | solution.py:252
  6.5 2.1 %split_cache.1 = (bf16[4,528,128]{2,1,0:T(8,128)(2,1)S(1)}, bf16[4,528,128]{2,1,0:T(8,128)(2,1)S(1)}, bf16[2,528,128]{2,1,0:T(8,128)(2,1)S(1)}, bf16[2,528,128]{...) custom-call(s32[1]{0:T(128)S(6)} %copy.7.live_ref, ...), custom_call_target="tpu_custom_call" | custom-call | tf_op jit(solution)/shard_map/split_cache/pallas_call | solution.py:262
  9.2 1.8 %collective-permute-start.3 = (bf16[4,4,16,256]{3,2,1,0:T(8,128)(2,1)S(1)}, bf16[4,4,16,256]{3,2,1,0:T(8,128)(2,1)S(1)}, u32[]{:S(2)}, u32[]{:S(2)}) collective-permute-start(bf16[4,4,16,256]{3,2,1,0:T(8,128)(2,1)S(1)} %pad_maximum_fusion.refs_0_), channel_id=1, source_target_pairs={{0,4},{1,5},{2,6},{3,7},{4,0},{5,1},{6,2},{7,3},{8,12},{9,13},{10,... | collective-permute-start | bytes 393224 | tf_op jit(solution)/shard_map/ppermute | solution.py:252
  11.0 1.5 %collective-permute-start.12 = (bf16[2,528,128]{2,1,0:T(8,128)(2,1)S(1)}, bf16[2,528,128]{2,1,0:T(8,128)(2,1)S(1)}, u32[]{:S(2)}, u32[]{:S(2)}) collective-permute-start(bf16[2,528,128]{2,1,0:T(8,128)(2,1)S(1)} %get-tuple-element.37), channel_id=1, source_target_pairs={{0,2},{1,3},{2,0},{3,1},{4,6},{5,7},{6,4},{7,5},{8,10},{9,11},{10,... | collective-permute-start | bytes 811016 | tf_op jit(solution)/shard_map/ppermute | solution.py:252
  12.5 2.6 %collective-permute-start.4 = (bf16[4,4,16,256]{3,2,1,0:T(8,128)(2,1)S(1)}, bf16[4,4,16,256]{3,2,1,0:T(8,128)(2,1)S(1)}, u32[]{:S(2)}, u32[]{:S(2)}) collective-permute-start(bf16[4,4,16,256]{3,2,1,0:T(8,128)(2,1)S(1)} %pad_maximum_fusion.refs_0_), channel_id=1, source_target_pairs={{0,8},{1,9},{2,10},{3,11},{4,12},{5,13},{6,14},{7,15},{8,0},{9,1},... | collective-permute-start | bytes 393224 | tf_op jit(solution)/shard_map/ppermute | solution.py:252
  15.4 5.8 %collective-permute-done.4.refs_2_ = bf16[4,4,16,256]{3,2,1,0:T(8,128)(2,1)S(1)} collective-permute-done((bf16[4,4,16,256]{3,2,1,0:T(8,128)(2,1)S(1)}, bf16[4,4,16,256]{3,2,1,0:T(8,128)(2,1)S(1)}, u32[]{:S(2)}, u32[]{:S(2)}) %collective-permute-start.4) | collective-permute-done | bytes 131104 | tf_op jit(solution)/shard_map/ppermute | solution.py:252
  21.2 2.7 %collective-permute-start.5 = (bf16[4,4,16,256]{3,2,1,0:T(8,128)(2,1)S(1)}, bf16[4,4,16,256]{3,2,1,0:T(8,128)(2,1)S(1)}, u32[]{:S(2)}, u32[]{:S(2)}) collective-permute-start(bf16[4,4,16,256]{3,2,1,0:T(8,128)(2,1)S(1)} %pad_maximum_fusion.refs_0_), channel_id=1, source_target_pairs={{0,12},{1,13},{2,14},{3,15},{4,8},{5,9},{6,10},{7,11},{8,4},{9,5},... | collective-permute-start | bytes 393224 | tf_op jit(solution)/shard_map/ppermute | solution.py:252
  23.9 4.0 %collective-permute-done.5.refs_3_ = bf16[4,4,16,256]{3,2,1,0:T(8,128)(2,1)S(1)} collective-permute-done((bf16[4,4,16,256]{3,2,1,0:T(8,128)(2,1)S(1)}, bf16[4,4,16,256]{3,2,1,0:T(8,128)(2,1)S(1)}, u32[]{:S(2)}, u32[]{:S(2)}) %collective-permute-start.5) | collective-permute-done | bytes 131104 | tf_op jit(solution)/shard_map/ppermute | solution.py:252
  28.6 1.4 %collective-permute-start.7 = (bf16[1,528,128]{2,1,0:T(8,128)(2,1)S(1)}, bf16[1,528,128]{2,1,0:T(8,128)(2,1)S(1)}, u32[]{:S(2)}, u32[]{:S(2)}) collective-permute-start(bf16[1,528,128]{2,1,0:T(8,128)(2,1)S(1)} %get-tuple-element.33), channel_id=1, source_target_pairs={{0,2},{1,3},{2,0},{3,1},{4,6},{5,7},{6,4},{7,5},{8,10},{9,11},{10,... | collective-permute-start | bytes 405512 | tf_op jit(solution)/shard_map/ppermute | solution.py:252
  30.7 1.2 %collective-permute-start.8 = (bf16[1,528,128]{2,1,0:T(8,128)(2,1)S(1)}, bf16[1,528,128]{2,1,0:T(8,128)(2,1)S(1)}, u32[]{:S(2)}, u32[]{:S(2)}) collective-permute-start(bf16[1,528,128]{2,1,0:T(8,128)(2,1)S(1)} %get-tuple-element.34), channel_id=1, source_target_pairs={{0,3},{1,2},{2,1},{3,0},{4,7},{5,6},{6,5},{7,4},{8,11},{9,10},{10,... | collective-permute-start | bytes 405512 | tf_op jit(solution)/shard_map/ppermute | solution.py:252
  34.4 2.8 %collective-permute-start.15 = (bf16[272,256]{1,0:T(8,128)(2,1)S(1)}, bf16[272,256]{1,0:T(8,128)(2,1)S(1)}, u32[]{:S(2)}, u32[]{:S(2)}) collective-permute-start(bf16[272,256]{1,0:T(8,128)(2,1)S(1)} %shard_map.68), channel_id=1, source_target_pairs={{0,12},{1,13},{2,14},{3,15},{4,8},{5,9},{6,10},{7,11},{8,4},{9,5},... | collective-permute-start | bytes 417800 | tf_op jit(solution)/shard_map/ppermute | solution.py:252
  38.5 1.7 %collective-permute-start.11 = (bf16[272,256]{1,0:T(8,128)(2,1)S(1)}, bf16[272,256]{1,0:T(8,128)(2,1)S(1)}, u32[]{:S(2)}, u32[]{:S(2)}) collective-permute-start(bf16[272,256]{1,0:T(8,128)(2,1)S(1)} %shard_map.66), channel_id=1, source_target_pairs={{0,4},{1,5},{2,6},{3,7},{4,0},{5,1},{6,2},{7,3},{8,12},{9,13},{10,... | collective-permute-start | bytes 417800 | tf_op jit(solution)/shard_map/ppermute | solution.py:252
  40.2 1.6 %collective-permute-done.8.refs_7_ = bf16[1,528,128]{2,1,0:T(8,128)(2,1)S(1)} collective-permute-done((bf16[1,528,128]{2,1,0:T(8,128)(2,1)S(1)}, bf16[1,528,128]{2,1,0:T(8,128)(2,1)S(1)}, u32[]{:S(2)}, u32[]{:S(2)}) %collective-permute-start.8) | collective-permute-done | bytes 135200 | tf_op jit(solution)/shard_map/ppermute | solution.py:252
  43.0 5.8 %collective-permute-done.14.refs_2_ = bf16[272,256]{1,0:T(8,128)(2,1)S(1)} collective-permute-done((bf16[272,256]{1,0:T(8,128)(2,1)S(1)}, bf16[272,256]{1,0:T(8,128)(2,1)S(1)}, u32[]{:S(2)}, u32[]{:S(2)}) %collective-permute-start.14) | collective-permute-done | bytes 139296 | tf_op jit(solution)/shard_map/ppermute | solution.py:252
  49.4 1.3 %collective-permute-done.16.other_ref = bf16[256,256]{1,0:T(8,128)(2,1)S(1)} collective-permute-done((bf16[256,256]{1,0:T(8,128)(2,1)S(1)}, bf16[256,256]{1,0:T(8,128)(2,1)S(1)}, u32[]{:S(2)}, u32[]{:S(2)}) %collective-permute-start.16) | collective-permute-done | bytes 131104 | tf_op jit(solution)/shard_map/ppermute | solution.py:252
  51.7 1.5 %collective-permute-start.23 = (bf16[32,2688]{1,0:T(8,128)(2,1)S(1)}, bf16[32,2688]{1,0:T(8,128)(2,1)S(1)}, u32[]{:S(2)}, u32[]{:S(2)}) collective-permute-start(bf16[32,2688]{1,0:T(8,128)(2,1)S(1)} %get-tuple-element.46), channel_id=1, source_target_pairs={{0,2},{1,3},{2,0},{3,1},{4,6},{5,7},{6,4},{7,5},{8,10},{9,11},{10,... | collective-permute-start | bytes 516104 | tf_op jit(solution)/shard_map/ppermute | solution.py:252
  53.8 1.5 %collective-permute-start.19 = (bf16[32,2688]{1,0:T(8,128)(2,1)S(1)}, bf16[32,2688]{1,0:T(8,128)(2,1)S(1)}, u32[]{:S(2)}, u32[]{:S(2)}) collective-permute-start(bf16[32,2688]{1,0:T(8,128)(2,1)S(1)} %get-tuple-element.42), channel_id=1, source_target_pairs={{0,2},{1,3},{2,0},{3,1},{4,6},{5,7},{6,4},{7,5},{8,10},{9,11},{10,... | collective-permute-start | bytes 516104 | tf_op jit(solution)/shard_map/ppermute | solution.py:252
  55.8 3.2 %collective-permute-done.23.got_ref = bf16[32,2688]{1,0:T(8,128)(2,1)S(1)} collective-permute-done((bf16[32,2688]{1,0:T(8,128)(2,1)S(1)}, bf16[32,2688]{1,0:T(8,128)(2,1)S(1)}, u32[]{:S(2)}, u32[]{:S(2)}) %collective-permute-start.23) | collective-permute-done | bytes 172064 | tf_op jit(solution)/shard_map/ppermute | solution.py:252
  59.2 3.5 %collective-permute-done.21.got_ref = bf16[32,2688]{1,0:T(8,128)(2,1)S(1)} collective-permute-done((bf16[32,2688]{1,0:T(8,128)(2,1)S(1)}, bf16[32,2688]{1,0:T(8,128)(2,1)S(1)}, u32[]{:S(2)}, u32[]{:S(2)}) %collective-permute-start.21) | collective-permute-done | bytes 172064 | tf_op jit(solution)/shard_map/ppermute | solution.py:252
  62.8 3.6 %collective-permute-done.19.got_ref = bf16[32,2688]{1,0:T(8,128)(2,1)S(1)} collective-permute-done((bf16[32,2688]{1,0:T(8,128)(2,1)S(1)}, bf16[32,2688]{1,0:T(8,128)(2,1)S(1)}, u32[]{:S(2)}, u32[]{:S(2)}) %collective-permute-start.19) | collective-permute-done | bytes 172064 | tf_op jit(solution)/shard_map/ppermute | solution.py:252
  66.5 2.0 %collective-permute-start.20 = (bf16[32,2688]{1,0:T(8,128)(2,1)S(1)}, bf16[32,2688]{1,0:T(8,128)(2,1)S(1)}, u32[]{:S(2)}, u32[]{:S(2)}) collective-permute-start(bf16[32,2688]{1,0:T(8,128)(2,1)S(1)} %shard_map.72), channel_id=1, source_target_pairs={{0,12},{1,13},{2,14},{3,15},{4,8},{5,9},{6,10},{7,11},{8,4},{9,5},... | collective-permute-start | bytes 516104 | tf_op jit(solution)/shard_map/ppermute | solution.py:252
  69.3 5.3 %collective-permute-done.22.refs_1_ = bf16[32,2688]{1,0:T(8,128)(2,1)S(1)} collective-permute-done((bf16[32,2688]{1,0:T(8,128)(2,1)S(1)}, bf16[32,2688]{1,0:T(8,128)(2,1)S(1)}, u32[]{:S(2)}, u32[]{:S(2)}) %collective-permute-start.22) | collective-permute-done | bytes 172064 | tf_op jit(solution)/shard_map/ppermute | solution.py:252
  74.8 1.3 %collective-permute-done.25.other_ref = bf16[16,2688]{1,0:T(8,128)(2,1)S(1)} collective-permute-done((bf16[16,2688]{1,0:T(8,128)(2,1)S(1)}, bf16[16,2688]{1,0:T(8,128)(2,1)S(1)}, u32[]{:S(2)}, u32[]{:S(2)}) %collective-permute-start.25) | collective-permute-done | bytes 86048 | tf_op jit(solution)/shard_map/ppermute | solution.py:252
  (49 shorter events, 12.6 us)
Async XLA Ops:
  1.9 48.9 %collective-permute-start.17 = (bf16[256,2688]{1,0:T(8,128)(2,1)S(1)}, bf16[256,2688]{1,0:T(8,128)(2,1)S(1)}, u32[]{:S(2)}, u32[]{:S(2)}) collective-permute-start(bf16[256,2688]{1,0:T(8,128)(2,1)S(1)} %shard_map.70), channel_id=1, source_target_pairs={{0,1},{1,0},{2,3},{3,2},{4,5},{5,4},{6,7},{7,6},{8,9},{9,8},{10,11... | collective-permute-start | bytes 4128776 | tf_op jit(solution)/shard_map/ppermute | solution.py:252
  2.7 6.2 %collective-permute-start = (bf16[4,16,256]{2,1,0:T(8,128)(2,1)S(1)}, bf16[4,16,256]{2,1,0:T(8,128)(2,1)S(1)}, u32[]{:S(2)}, u32[]{:S(2)}) collective-permute-start(bf16[4,16,256]{2,1,0:T(8,128)(2,1)S(1)} %get-tuple-element.28), channel_id=1, source_target_pairs={{0,1},{1,0},{2,3},{3,2},{4,5},{5,4},{6,7},{7,6},{8,9},{9,8},{10,11... | collective-permute-start | bytes 98312 | tf_op jit(solution)/shard_map/ppermute | solution.py:252
  3.3 5.6 %collective-permute-start.1 = (bf16[4,16,256]{2,1,0:T(8,128)(2,1)S(1)}, bf16[4,16,256]{2,1,0:T(8,128)(2,1)S(1)}, u32[]{:S(2)}, u32[]{:S(2)}) collective-permute-start(bf16[4,16,256]{2,1,0:T(8,128)(2,1)S(1)} %get-tuple-element.29), channel_id=1, source_target_pairs={{0,2},{1,3},{2,0},{3,1},{4,6},{5,7},{6,4},{7,5},{8,10},{9,11},{10,... | collective-permute-start | bytes 98312 | tf_op jit(solution)/shard_map/ppermute | solution.py:252
  5.8 3.4 %collective-permute-start.2 = (bf16[4,16,256]{2,1,0:T(8,128)(2,1)S(1)}, bf16[4,16,256]{2,1,0:T(8,128)(2,1)S(1)}, u32[]{:S(2)}, u32[]{:S(2)}) collective-permute-start(bf16[4,16,256]{2,1,0:T(8,128)(2,1)S(1)} %get-tuple-element.30), channel_id=1, source_target_pairs={{0,3},{1,2},{2,1},{3,0},{4,7},{5,6},{6,5},{7,4},{8,11},{9,10},{10,... | collective-permute-start | bytes 98312 | tf_op jit(solution)/shard_map/ppermute | solution.py:252
  8.7 22.0 %collective-permute-start.6 = (bf16[4,528,128]{2,1,0:T(8,128)(2,1)S(1)}, bf16[4,528,128]{2,1,0:T(8,128)(2,1)S(1)}, u32[]{:S(2)}, u32[]{:S(2)}) collective-permute-start(bf16[4,528,128]{2,1,0:T(8,128)(2,1)S(1)} %get-tuple-element.32), channel_id=1, source_target_pairs={{0,1},{1,0},{2,3},{3,2},{4,5},{5,4},{6,7},{7,6},{8,9},{9,8},{10,11... | collective-permute-start | bytes 1622024 | tf_op jit(solution)/shard_map/ppermute | solution.py:252
  9.2 5.9 %collective-permute-start.3 = (bf16[4,4,16,256]{3,2,1,0:T(8,128)(2,1)S(1)}, bf16[4,4,16,256]{3,2,1,0:T(8,128)(2,1)S(1)}, u32[]{:S(2)}, u32[]{:S(2)}) collective-permute-start(bf16[4,4,16,256]{3,2,1,0:T(8,128)(2,1)S(1)} %pad_maximum_fusion.refs_0_), channel_id=1, source_target_pairs={{0,4},{1,5},{2,6},{3,7},{4,0},{5,1},{6,2},{7,3},{8,12},{9,13},{10,... | collective-permute-start | bytes 393224 | tf_op jit(solution)/shard_map/ppermute | solution.py:252
  11.0 17.0 %collective-permute-start.12 = (bf16[2,528,128]{2,1,0:T(8,128)(2,1)S(1)}, bf16[2,528,128]{2,1,0:T(8,128)(2,1)S(1)}, u32[]{:S(2)}, u32[]{:S(2)}) collective-permute-start(bf16[2,528,128]{2,1,0:T(8,128)(2,1)S(1)} %get-tuple-element.37), channel_id=1, source_target_pairs={{0,2},{1,3},{2,0},{3,1},{4,6},{5,7},{6,4},{7,5},{8,10},{9,11},{10,... | collective-permute-start | bytes 811016 | tf_op jit(solution)/shard_map/ppermute | solution.py:252
  12.5 8.7 %collective-permute-start.4 = (bf16[4,4,16,256]{3,2,1,0:T(8,128)(2,1)S(1)}, bf16[4,4,16,256]{3,2,1,0:T(8,128)(2,1)S(1)}, u32[]{:S(2)}, u32[]{:S(2)}) collective-permute-start(bf16[4,4,16,256]{3,2,1,0:T(8,128)(2,1)S(1)} %pad_maximum_fusion.refs_0_), channel_id=1, source_target_pairs={{0,8},{1,9},{2,10},{3,11},{4,12},{5,13},{6,14},{7,15},{8,0},{9,1},... | collective-permute-start | bytes 393224 | tf_op jit(solution)/shard_map/ppermute | solution.py:252
  15.1 13.5 %collective-permute-start.13 = (bf16[2,528,128]{2,1,0:T(8,128)(2,1)S(1)}, bf16[2,528,128]{2,1,0:T(8,128)(2,1)S(1)}, u32[]{:S(2)}, u32[]{:S(2)}) collective-permute-start(bf16[2,528,128]{2,1,0:T(8,128)(2,1)S(1)} %get-tuple-element.38), channel_id=1, source_target_pairs={{0,3},{1,2},{2,1},{3,0},{4,7},{5,6},{6,5},{7,4},{8,11},{9,10},{10,... | collective-permute-start | bytes 811016 | tf_op jit(solution)/shard_map/ppermute | solution.py:252
  21.2 6.8 %collective-permute-start.5 = (bf16[4,4,16,256]{3,2,1,0:T(8,128)(2,1)S(1)}, bf16[4,4,16,256]{3,2,1,0:T(8,128)(2,1)S(1)}, u32[]{:S(2)}, u32[]{:S(2)}) collective-permute-start(bf16[4,4,16,256]{3,2,1,0:T(8,128)(2,1)S(1)} %pad_maximum_fusion.refs_0_), channel_id=1, source_target_pairs={{0,12},{1,13},{2,14},{3,15},{4,8},{5,9},{6,10},{7,11},{8,4},{9,5},... | collective-permute-start | bytes 393224 | tf_op jit(solution)/shard_map/ppermute | solution.py:252
  28.0 6.4 %collective-permute-start.10 = (bf16[1,528,128]{2,1,0:T(8,128)(2,1)S(1)}, bf16[1,528,128]{2,1,0:T(8,128)(2,1)S(1)}, u32[]{:S(2)}, u32[]{:S(2)}) collective-permute-start(bf16[1,528,128]{2,1,0:T(8,128)(2,1)S(1)} %get-tuple-element.36), channel_id=1, source_target_pairs={{0,3},{1,2},{2,1},{3,0},{4,7},{5,6},{6,5},{7,4},{8,11},{9,10},{10,... | collective-permute-start | bytes 405512 | tf_op jit(solution)/shard_map/ppermute | solution.py:252
  28.0 9.2 %collective-permute-start.9 = (bf16[1,528,128]{2,1,0:T(8,128)(2,1)S(1)}, bf16[1,528,128]{2,1,0:T(8,128)(2,1)S(1)}, u32[]{:S(2)}, u32[]{:S(2)}) collective-permute-start(bf16[1,528,128]{2,1,0:T(8,128)(2,1)S(1)} %get-tuple-element.35), channel_id=1, source_target_pairs={{0,2},{1,3},{2,0},{3,1},{4,6},{5,7},{6,4},{7,5},{8,10},{9,11},{10,... | collective-permute-start | bytes 405512 | tf_op jit(solution)/shard_map/ppermute | solution.py:252
  28.6 9.8 %collective-permute-start.7 = (bf16[1,528,128]{2,1,0:T(8,128)(2,1)S(1)}, bf16[1,528,128]{2,1,0:T(8,128)(2,1)S(1)}, u32[]{:S(2)}, u32[]{:S(2)}) collective-permute-start(bf16[1,528,128]{2,1,0:T(8,128)(2,1)S(1)} %get-tuple-element.33), channel_id=1, source_target_pairs={{0,2},{1,3},{2,0},{3,1},{4,6},{5,7},{6,4},{7,5},{8,10},{9,11},{10,... | collective-permute-start | bytes 405512 | tf_op jit(solution)/shard_map/ppermute | solution.py:252
  30.7 11.1 %collective-permute-start.8 = (bf16[1,528,128]{2,1,0:T(8,128)(2,1)S(1)}, bf16[1,528,128]{2,1,0:T(8,128)(2,1)S(1)}, u32[]{:S(2)}, u32[]{:S(2)}) collective-permute-start(bf16[1,528,128]{2,1,0:T(8,128)(2,1)S(1)} %get-tuple-element.34), channel_id=1, source_target_pairs={{0,3},{1,2},{2,1},{3,0},{4,7},{5,6},{6,5},{7,4},{8,11},{9,10},{10,... | collective-permute-start | bytes 405512 | tf_op jit(solution)/shard_map/ppermute | solution.py:252
  34.4 8.6 %collective-permute-start.15 = (bf16[272,256]{1,0:T(8,128)(2,1)S(1)}, bf16[272,256]{1,0:T(8,128)(2,1)S(1)}, u32[]{:S(2)}, u32[]{:S(2)}) collective-permute-start(bf16[272,256]{1,0:T(8,128)(2,1)S(1)} %shard_map.68), channel_id=1, source_target_pairs={{0,12},{1,13},{2,14},{3,15},{4,8},{5,9},{6,10},{7,11},{8,4},{9,5},... | collective-permute-start | bytes 417800 | tf_op jit(solution)/shard_map/ppermute | solution.py:252
  37.2 11.6 %collective-permute-start.14 = (bf16[272,256]{1,0:T(8,128)(2,1)S(1)}, bf16[272,256]{1,0:T(8,128)(2,1)S(1)}, u32[]{:S(2)}, u32[]{:S(2)}) collective-permute-start(bf16[272,256]{1,0:T(8,128)(2,1)S(1)} %shard_map.67), channel_id=1, source_target_pairs={{0,8},{1,9},{2,10},{3,11},{4,12},{5,13},{6,14},{7,15},{8,0},{9,1},... | collective-permute-start | bytes 417800 | tf_op jit(solution)/shard_map/ppermute | solution.py:252
  38.5 10.4 %collective-permute-start.11 = (bf16[272,256]{1,0:T(8,128)(2,1)S(1)}, bf16[272,256]{1,0:T(8,128)(2,1)S(1)}, u32[]{:S(2)}, u32[]{:S(2)}) collective-permute-start(bf16[272,256]{1,0:T(8,128)(2,1)S(1)} %shard_map.66), channel_id=1, source_target_pairs={{0,4},{1,5},{2,6},{3,7},{4,0},{5,1},{6,2},{7,3},{8,12},{9,13},{10,... | collective-permute-start | bytes 417800 | tf_op jit(solution)/shard_map/ppermute | solution.py:252
  51.7 7.3 %collective-permute-start.23 = (bf16[32,2688]{1,0:T(8,128)(2,1)S(1)}, bf16[32,2688]{1,0:T(8,128)(2,1)S(1)}, u32[]{:S(2)}, u32[]{:S(2)}) collective-permute-start(bf16[32,2688]{1,0:T(8,128)(2,1)S(1)} %get-tuple-element.46), channel_id=1, source_target_pairs={{0,2},{1,3},{2,0},{3,1},{4,6},{5,7},{6,4},{7,5},{8,10},{9,11},{10,... | collective-permute-start | bytes 516104 | tf_op jit(solution)/shard_map/ppermute | solution.py:252
  53.3 9.5 %collective-permute-start.21 = (bf16[32,2688]{1,0:T(8,128)(2,1)S(1)}, bf16[32,2688]{1,0:T(8,128)(2,1)S(1)}, u32[]{:S(2)}, u32[]{:S(2)}) collective-permute-start(bf16[32,2688]{1,0:T(8,128)(2,1)S(1)} %get-tuple-element.44), channel_id=1, source_target_pairs={{0,2},{1,3},{2,0},{3,1},{4,6},{5,7},{6,4},{7,5},{8,10},{9,11},{10,... | collective-permute-start | bytes 516104 | tf_op jit(solution)/shard_map/ppermute | solution.py:252
  53.8 12.6 %collective-permute-start.19 = (bf16[32,2688]{1,0:T(8,128)(2,1)S(1)}, bf16[32,2688]{1,0:T(8,128)(2,1)S(1)}, u32[]{:S(2)}, u32[]{:S(2)}) collective-permute-start(bf16[32,2688]{1,0:T(8,128)(2,1)S(1)} %get-tuple-element.42), channel_id=1, source_target_pairs={{0,2},{1,3},{2,0},{3,1},{4,6},{5,7},{6,4},{7,5},{8,10},{9,11},{10,... | collective-permute-start | bytes 516104 | tf_op jit(solution)/shard_map/ppermute | solution.py:252
  55.3 14.0 %collective-permute-start.18 = (bf16[32,2688]{1,0:T(8,128)(2,1)S(1)}, bf16[32,2688]{1,0:T(8,128)(2,1)S(1)}, u32[]{:S(2)}, u32[]{:S(2)}) collective-permute-start(bf16[32,2688]{1,0:T(8,128)(2,1)S(1)} %get-tuple-element.40), channel_id=1, source_target_pairs={{0,2},{1,3},{2,0},{3,1},{4,6},{5,7},{6,4},{7,5},{8,10},{9,11},{10,... | collective-permute-start | bytes 516104 | tf_op jit(solution)/shard_map/ppermute | solution.py:252
  59.1 10.2 %collective-permute-start.24 = (bf16[32,2688]{1,0:T(8,128)(2,1)S(1)}, bf16[32,2688]{1,0:T(8,128)(2,1)S(1)}, u32[]{:S(2)}, u32[]{:S(2)}) collective-permute-start(bf16[32,2688]{1,0:T(8,128)(2,1)S(1)} %shard_map.74), channel_id=1, source_target_pairs={{0,8},{1,9},{2,10},{3,11},{4,12},{5,13},{6,14},{7,15},{8,0},{9,1},... | collective-permute-start | bytes 516104 | tf_op jit(solution)/shard_map/ppermute | solution.py:252
  62.8 11.8 %collective-permute-start.22 = (bf16[32,2688]{1,0:T(8,128)(2,1)S(1)}, bf16[32,2688]{1,0:T(8,128)(2,1)S(1)}, u32[]{:S(2)}, u32[]{:S(2)}) collective-permute-start(bf16[32,2688]{1,0:T(8,128)(2,1)S(1)} %shard_map.73), channel_id=1, source_target_pairs={{0,4},{1,5},{2,6},{3,7},{4,0},{5,1},{6,2},{7,3},{8,12},{9,13},{10,... | collective-permute-start | bytes 516104 | tf_op jit(solution)/shard_map/ppermute | solution.py:252
  66.5 8.1 %collective-permute-start.20 = (bf16[32,2688]{1,0:T(8,128)(2,1)S(1)}, bf16[32,2688]{1,0:T(8,128)(2,1)S(1)}, u32[]{:S(2)}, u32[]{:S(2)}) collective-permute-start(bf16[32,2688]{1,0:T(8,128)(2,1)S(1)} %shard_map.72), channel_id=1, source_target_pairs={{0,12},{1,13},{2,14},{3,15},{4,8},{5,9},{6,10},{7,11},{8,4},{9,5},... | collective-permute-start | bytes 516104 | tf_op jit(solution)/shard_map/ppermute | solution.py:252
  (5 other events, 19.0 us)

commit v6 on v1

--- a/solution.py
+++ b/solution.py
@@ -53,16 +53,26 @@
     )(*ins)
 
 
-def split_kernel(live_ref, q_ref, k_ref, v_ref, *refs, outer, width, groups, copies):
+def split_kernel(live_ref, q_hbm, k_hbm, v_hbm, *refs, outer, width, groups, copies):
     _, z, r = place()
     q_outs = refs[:INNER]
-    kv_outs = refs[INNER:]
+    kv_outs = refs[INNER:INNER + len(groups)]
+    q_ref, k_ref, v_ref, sems = refs[INNER + len(groups):]
     keys = k_ref.shape[0]
+    loads = [
+        pltpu.make_async_copy(source, target, sems.at[i])
+        for i, (source, target) in enumerate(((q_hbm, q_ref), (k_hbm, k_ref), (v_hbm, v_ref)))
+    ]
+    for load in loads:
+        load.start()
     live = jnp.full((16, HEAD_SIZE), live_ref[0], jnp.int32).astype(f32).astype(bf16)
+    loads[0].wait()
     for k, out in enumerate(q_outs):
         for zz in range(outer):
             col = pl.multiple_of((zz * INNER + lax.bitwise_xor(r, k)) * width, width)
             out[zz] = q_ref[:, pl.ds(col, width)]
+    loads[1].wait()
+    loads[2].wait()
     for (k, offsets), out in zip(groups, kv_outs):
         for i, kk in enumerate(offsets):
             head = lax.bitwise_xor(z, kk) * INNER + lax.bitwise_xor(r, k)
@@ -79,10 +89,9 @@
     out_ref[...] = w_ref[:, pl.ds(col, half)]
 
 
-def attention_kernel(first_ref, *refs, outer, first, offsets, rows_all, keys, heads, width):
+def attention_kernel(first_ref, *refs, outer, begin, offsets, rows_all, keys, heads, width):
     ys = refs[:outer]
     kvs = refs[outer:outer + INNER]
-    begin = [first, first] + [0] * (INNER - 2)
     outs = refs[outer + INNER:outer + INNER + len(offsets)]
     bias_ref, q_ref = refs[outer + INNER + len(offsets):]
     _, z, r = place()
@@ -240,16 +249,25 @@
     def swap(x, k):
         return lax.ppermute(x, "seq", [(i, i ^ k) for i in range(devices)])
 
-    order = list(range(outer - 1, -1, -1))
+    order = [outer - 1, 1] + list(range(outer - 2, 1, -1)) + [0]
     phases = [order[:outer // 2], order[outer // 2:3 * outer // 4], order[3 * outer // 4:]]
     groups = [(0, order), (1, order)] + [(k, p) for p in phases for k in range(2, INNER)]
-    outs = [shape((outer, rows, width), bf16)] * INNER + [
-        shape((len(p), 2 * keys + 16, HEAD_SIZE), bf16) for k, p in groups
+    inputs = [
+        pltpu.with_memory_space_constraint(x, pltpu.MemorySpace.HBM)
+        for x in (query_block, cache_keys, stored_values)
     ]
-    split = call(
+    outs = [shape((outer, rows, width), bf16)] * INNER
+    outs += [shape((len(p), 2 * keys + 16, HEAD_SIZE), bf16) for k, p in groups]
+    split = pl.pallas_call(
         functools.partial(split_kernel, outer=outer, width=width, groups=groups, copies=copies),
-        [live_counts, query_block, cache_keys, stored_values], outs, scalars=1,
-    )
+        out_shape=tuple(outs),
+        in_specs=[sspec()] + [pl.BlockSpec(memory_space=pltpu.MemorySpace.HBM)] * 3,
+        out_specs=tuple(vspec() for _ in outs),
+        scratch_shapes=[pltpu.VMEM(x.shape, x.dtype) for x in inputs]
+        + [pltpu.SemaphoreType.DMA((3,))],
+        name="split",
+        compiler_params=pltpu.CompilerParams(vmem_limit_bytes=8 << 20),
+    )(live_counts, *inputs)
     q_out, kv_out = split[:INNER], split[INNER:]
     q_got = {k: swap(q_out[k], k) for k in (2, 3, 1)}
     kv_pair = swap(kv_out[1], 1)
@@ -267,22 +285,20 @@
     w_other = swap(w_send, 1)
 
     partial_of = {}
-    at = 0
-    for i, offsets in enumerate(phases):
-        size = len(offsets)
-        outs = call(
+    for near, kk in enumerate(order):
+        i = [kk in p for p in phases].index(True)
+        far = phases[i].index(kk)
+        (out,) = call(
             functools.partial(
-                attention_kernel, outer=outer, first=at, offsets=offsets, rows_all=rows_all,
-                keys=keys, heads=heads, width=width,
+                attention_kernel, outer=outer, begin=(near, near) + (far,) * (INNER - 2),
+                offsets=[kk], rows_all=rows_all, keys=keys, heads=heads, width=width,
             ),
             [first_position, *ys, kv_out[0], kv_pair, kv_far[i][2], kv_far[i][3]],
-            [shape((rows_all + 16, width), bf16)] * size,
+            [shape((rows_all + 16, width), bf16)],
             scratch=[pltpu.VMEM((rows_all, INNER * keys), f32), pltpu.VMEM((rows_all, width), f32)],
-            scalars=1, flops=4 * rows_all * INNER * keys * width * size, limit=20,
+            scalars=1, flops=4 * rows_all * INNER * keys * width, limit=16,
         )
-        at += size
-        for kk, out in zip(offsets, outs):
-            partial_of[kk] = swap(out, kk * INNER) if kk else out
+        partial_of[kk] = swap(out, kk * INNER) if kk else out
 
     (merged,) = call(
         functools.partial(merge_kernel, sources=outer, rows_all=rows_all, heads=heads, width=width),

time: 81.2 us -> 80.2 us (0.988); the launches traced: 80.1 us -> 80 us
  waiting for transfers between devices: 44.3 us -> 40.2 us
  starting transfers between devices: 24.5 us -> 27.1 us
  Pallas kernels: 7.84 us -> 9.59 us
    ppermute x26, waiting for transfers between devices: 44.3 us -> 40.2 us  [swap(): return lax.ppermute(x, 'seq', [(i, i ^ k) for i in range(devices)])]
    ppermute x26, starting transfers between devices: 24.5 us -> 27.1 us  [swap(): return lax.ppermute(x, 'seq', [(i, i ^ k) for i in range(devices)])]
    pallas_call x0 -> x1, Pallas kernels: none -> 2.21 us  [layer(): pl.pallas_call(functools.partial(split_kernel, outer=outer, width=width,...]
    unnamed x10 -> x4, local copies, waits for them, and re-layouts: 1.98 us -> 1.78 us
  transfers between devices with their start and end apart: 26 -> 26, of which waited for: 16 -> 16; matrix products, arithmetic and copies ran while one was open for 0% -> 0% of each run, Pallas kernels for 7% -> 10%
where the time goes in v6:
time: 80.2 us; the launch traced here: 80 us
  waiting for transfers between devices  40.2 us (50%)
  starting transfers between devices  27.1 us (34%)
  Pallas kernels  9.59 us (12%)
  local copies, waits for them, and re-layouts  1.78 us (2%)
  between operations  1.44 us (2%)
    ppermute x26, waiting for transfers between devices, swap(): return lax.ppermute(x, 'seq', [(i, i ^ k) for i in range(devices)])  40.2 us
    ppermute x26, starting transfers between devices, swap(): return lax.ppermute(x, 'seq', [(i, i ^ k) for i in range(devices)])  27.1 us
    pallas_call x12, Pallas kernels, call(): pl.pallas_call(kernel, out_shape=tuple(outs), in_specs=in_specs, out_spec...  7.38 us
    pallas_call x1, Pallas kernels, layer(): pl.pallas_call(functools.partial(split_kernel, outer=outer, width=width,...  2.21 us
    unnamed x4, local copies, waits for them, and re-layouts  1.78 us
  transfers between devices with their start and end apart: 26, of which 16 were waited for; matrix products, arithmetic and copies ran while one was open for 0% of the time, Pallas kernels for 10%

profile of v6, /device:TPU:0, one launch (start us, length us, event | category | flops | bytes accessed | tf_op | source)
XLA Modules:
  0.0 80.0 jit_solution(18325312916846972555)
XLA Ops:
  0.0 1.8 %copy-done = bf16[256,5376]{1,0:T(8,128)(2,1)S(1)} copy-done((bf16[256,5376]{1,0:T(8,128)(2,1)S(1)}, bf16[256,5376]{1,0:T(8,128)(2,1)}, u32[]{:S(2)}) %copy-start) | copy-done | bytes 2752536
  3.1 2.2 %split.1 = (bf16[4,16,256]{2,1,0:T(8,128)(2,1)S(1)}, bf16[4,16,256]{2,1,0:T(8,128)(2,1)S(1)}, bf16[4,16,256]{2,1,0:T(8,128)(2,1)S(1)}, bf16[4,16,256]{2,1,0:T(8,...) custom-call(s32[1]{0:T(128)S(6)} %copy.7.live_ref, ...), custom_call_target="tpu_custom_call" | custom-call | tf_op jit(solution)/shard_map/split/pallas_call | solution.py:261
  5.4 3.0 %collective-permute-start.1 = (bf16[4,16,256]{2,1,0:T(8,128)(2,1)S(1)}, bf16[4,16,256]{2,1,0:T(8,128)(2,1)S(1)}, u32[]{:S(2)}, u32[]{:S(2)}) collective-permute-start(bf16[4,16,256]{2,1,0:T(8,128)(2,1)S(1)} %get-tuple-element.29), channel_id=1, source_target_pairs={{0,2},{1,3},{2,0},{3,1},{4,6},{5,7},{6,4},{7,5},{8,10},{9,11},{10,... | collective-permute-start | bytes 98312 | tf_op jit(solution)/shard_map/ppermute | solution.py:250
  8.5 1.8 %collective-permute-done.1 = bf16[4,16,256]{2,1,0:T(8,128)(2,1)S(1)} collective-permute-done((bf16[4,16,256]{2,1,0:T(8,128)(2,1)S(1)}, bf16[4,16,256]{2,1,0:T(8,128)(2,1)S(1)}, u32[]{:S(2)}, u32[]{:S(2)}) %collective-permute-start.1) | collective-permute-done | bytes 32800 | tf_op jit(solution)/shard_map/ppermute | solution.py:250
  10.3 1.8 %collective-permute-done.2 = bf16[4,16,256]{2,1,0:T(8,128)(2,1)S(1)} collective-permute-done((bf16[4,16,256]{2,1,0:T(8,128)(2,1)S(1)}, bf16[4,16,256]{2,1,0:T(8,128)(2,1)S(1)}, u32[]{:S(2)}, u32[]{:S(2)}) %collective-permute-start.2) | collective-permute-done | bytes 32800 | tf_op jit(solution)/shard_map/ppermute | solution.py:250
  12.1 1.6 %collective-permute-start.3 = (bf16[4,4,16,256]{3,2,1,0:T(8,128)(2,1)S(1)}, bf16[4,4,16,256]{3,2,1,0:T(8,128)(2,1)S(1)}, u32[]{:S(2)}, u32[]{:S(2)}) collective-permute-start(bf16[4,4,16,256]{3,2,1,0:T(8,128)(2,1)S(1)} %pad_maximum_fusion.refs_0_), channel_id=1, source_target_pairs={{0,4},{1,5},{2,6},{3,7},{4,0},{5,1},{6,2},{7,3},{8,12},{9,13},{10,... | collective-permute-start | bytes 393224 | tf_op jit(solution)/shard_map/ppermute | solution.py:250
  13.7 2.6 %collective-permute-start.4 = (bf16[4,4,16,256]{3,2,1,0:T(8,128)(2,1)S(1)}, bf16[4,4,16,256]{3,2,1,0:T(8,128)(2,1)S(1)}, u32[]{:S(2)}, u32[]{:S(2)}) collective-permute-start(bf16[4,4,16,256]{3,2,1,0:T(8,128)(2,1)S(1)} %pad_maximum_fusion.refs_0_), channel_id=1, source_target_pairs={{0,8},{1,9},{2,10},{3,11},{4,12},{5,13},{6,14},{7,15},{8,0},{9,1},... | collective-permute-start | bytes 393224 | tf_op jit(solution)/shard_map/ppermute | solution.py:250
  16.3 1.3 %collective-permute-done.3.refs_1_ = bf16[4,4,16,256]{3,2,1,0:T(8,128)(2,1)S(1)} collective-permute-done((bf16[4,4,16,256]{3,2,1,0:T(8,128)(2,1)S(1)}, bf16[4,4,16,256]{3,2,1,0:T(8,128)(2,1)S(1)}, u32[]{:S(2)}, u32[]{:S(2)}) %collective-permute-start.3) | collective-permute-done | bytes 131104 | tf_op jit(solution)/shard_map/ppermute | solution.py:250
  18.1 5.4 %collective-permute-done.4.refs_2_ = bf16[4,4,16,256]{3,2,1,0:T(8,128)(2,1)S(1)} collective-permute-done((bf16[4,4,16,256]{3,2,1,0:T(8,128)(2,1)S(1)}, bf16[4,4,16,256]{3,2,1,0:T(8,128)(2,1)S(1)}, u32[]{:S(2)}, u32[]{:S(2)}) %collective-permute-start.4) | collective-permute-done | bytes 131104 | tf_op jit(solution)/shard_map/ppermute | solution.py:250
  23.5 2.5 %collective-permute-start.5 = (bf16[4,4,16,256]{3,2,1,0:T(8,128)(2,1)S(1)}, bf16[4,4,16,256]{3,2,1,0:T(8,128)(2,1)S(1)}, u32[]{:S(2)}, u32[]{:S(2)}) collective-permute-start(bf16[4,4,16,256]{3,2,1,0:T(8,128)(2,1)S(1)} %pad_maximum_fusion.refs_0_), channel_id=1, source_target_pairs={{0,12},{1,13},{2,14},{3,15},{4,8},{5,9},{6,10},{7,11},{8,4},{9,5},... | collective-permute-start | bytes 393224 | tf_op jit(solution)/shard_map/ppermute | solution.py:250
  26.0 4.5 %collective-permute-done.5.refs_3_ = bf16[4,4,16,256]{3,2,1,0:T(8,128)(2,1)S(1)} collective-permute-done((bf16[4,4,16,256]{3,2,1,0:T(8,128)(2,1)S(1)}, bf16[4,4,16,256]{3,2,1,0:T(8,128)(2,1)S(1)}, u32[]{:S(2)}, u32[]{:S(2)}) %collective-permute-start.5) | collective-permute-done | bytes 131104 | tf_op jit(solution)/shard_map/ppermute | solution.py:250
  30.5 1.6 %collective-permute-start.12 = (bf16[1,528,128]{2,1,0:T(8,128)(2,1)S(1)}, bf16[1,528,128]{2,1,0:T(8,128)(2,1)S(1)}, u32[]{:S(2)}, u32[]{:S(2)}) collective-permute-start(bf16[1,528,128]{2,1,0:T(8,128)(2,1)S(1)} %get-tuple-element.37), channel_id=1, source_target_pairs={{0,2},{1,3},{2,0},{3,1},{4,6},{5,7},{6,4},{7,5},{8,10},{9,11},{10,... | collective-permute-start | bytes 405512 | tf_op jit(solution)/shard_map/ppermute | solution.py:250
  33.3 1.5 %collective-permute-start.8 = (bf16[1,528,128]{2,1,0:T(8,128)(2,1)S(1)}, bf16[1,528,128]{2,1,0:T(8,128)(2,1)S(1)}, u32[]{:S(2)}, u32[]{:S(2)}) collective-permute-start(bf16[1,528,128]{2,1,0:T(8,128)(2,1)S(1)} %get-tuple-element.34), channel_id=1, source_target_pairs={{0,3},{1,2},{2,1},{3,0},{4,7},{5,6},{6,5},{7,4},{8,11},{9,10},{10,... | collective-permute-start | bytes 405512 | tf_op jit(solution)/shard_map/ppermute | solution.py:250
  36.1 2.4 %collective-permute-start.15 = (bf16[272,256]{1,0:T(8,128)(2,1)S(1)}, bf16[272,256]{1,0:T(8,128)(2,1)S(1)}, u32[]{:S(2)}, u32[]{:S(2)}) collective-permute-start(bf16[272,256]{1,0:T(8,128)(2,1)S(1)} %shard_map.67), channel_id=1, source_target_pairs={{0,12},{1,13},{2,14},{3,15},{4,8},{5,9},{6,10},{7,11},{8,4},{9,5},... | collective-permute-start | bytes 417800 | tf_op jit(solution)/shard_map/ppermute | solution.py:250
  41.8 2.7 %collective-permute-start.11 = (bf16[272,256]{1,0:T(8,128)(2,1)S(1)}, bf16[272,256]{1,0:T(8,128)(2,1)S(1)}, u32[]{:S(2)}, u32[]{:S(2)}) collective-permute-start(bf16[272,256]{1,0:T(8,128)(2,1)S(1)} %shard_map.65), channel_id=1, source_target_pairs={{0,4},{1,5},{2,6},{3,7},{4,0},{5,1},{6,2},{7,3},{8,12},{9,13},{10,... | collective-permute-start | bytes 417800 | tf_op jit(solution)/shard_map/ppermute | solution.py:250
  45.8 5.3 %collective-permute-done.14.refs_2_ = bf16[272,256]{1,0:T(8,128)(2,1)S(1)} collective-permute-done((bf16[272,256]{1,0:T(8,128)(2,1)S(1)}, bf16[272,256]{1,0:T(8,128)(2,1)S(1)}, u32[]{:S(2)}, u32[]{:S(2)}) %collective-permute-start.14) | collective-permute-done | bytes 139296 | tf_op jit(solution)/shard_map/ppermute | solution.py:250
  51.6 1.3 %collective-permute-done.16.other_ref = bf16[256,256]{1,0:T(8,128)(2,1)S(1)} collective-permute-done((bf16[256,256]{1,0:T(8,128)(2,1)S(1)}, bf16[256,256]{1,0:T(8,128)(2,1)S(1)}, u32[]{:S(2)}, u32[]{:S(2)}) %collective-permute-start.16) | collective-permute-done | bytes 131104 | tf_op jit(solution)/shard_map/ppermute | solution.py:250
  54.0 2.6 %collective-permute-start.23 = (bf16[32,2688]{1,0:T(8,128)(2,1)S(1)}, bf16[32,2688]{1,0:T(8,128)(2,1)S(1)}, u32[]{:S(2)}, u32[]{:S(2)}) collective-permute-start(bf16[32,2688]{1,0:T(8,128)(2,1)S(1)} %get-tuple-element.46), channel_id=1, source_target_pairs={{0,2},{1,3},{2,0},{3,1},{4,6},{5,7},{6,4},{7,5},{8,10},{9,11},{10,... | collective-permute-start | bytes 516104 | tf_op jit(solution)/shard_map/ppermute | solution.py:250
  56.6 1.9 %collective-permute-start.19 = (bf16[32,2688]{1,0:T(8,128)(2,1)S(1)}, bf16[32,2688]{1,0:T(8,128)(2,1)S(1)}, u32[]{:S(2)}, u32[]{:S(2)}) collective-permute-start(bf16[32,2688]{1,0:T(8,128)(2,1)S(1)} %get-tuple-element.42), channel_id=1, source_target_pairs={{0,2},{1,3},{2,0},{3,1},{4,6},{5,7},{6,4},{7,5},{8,10},{9,11},{10,... | collective-permute-start | bytes 516104 | tf_op jit(solution)/shard_map/ppermute | solution.py:250
  58.6 3.1 %collective-permute-done.23.got_ref = bf16[32,2688]{1,0:T(8,128)(2,1)S(1)} collective-permute-done((bf16[32,2688]{1,0:T(8,128)(2,1)S(1)}, bf16[32,2688]{1,0:T(8,128)(2,1)S(1)}, u32[]{:S(2)}, u32[]{:S(2)}) %collective-permute-start.23) | collective-permute-done | bytes 172064 | tf_op jit(solution)/shard_map/ppermute | solution.py:250
  62.0 3.4 %collective-permute-done.21.got_ref = bf16[32,2688]{1,0:T(8,128)(2,1)S(1)} collective-permute-done((bf16[32,2688]{1,0:T(8,128)(2,1)S(1)}, bf16[32,2688]{1,0:T(8,128)(2,1)S(1)}, u32[]{:S(2)}, u32[]{:S(2)}) %collective-permute-start.21) | collective-permute-done | bytes 172064 | tf_op jit(solution)/shard_map/ppermute | solution.py:250
  65.5 3.6 %collective-permute-done.19.got_ref = bf16[32,2688]{1,0:T(8,128)(2,1)S(1)} collective-permute-done((bf16[32,2688]{1,0:T(8,128)(2,1)S(1)}, bf16[32,2688]{1,0:T(8,128)(2,1)S(1)}, u32[]{:S(2)}, u32[]{:S(2)}) %collective-permute-start.19) | collective-permute-done | bytes 172064 | tf_op jit(solution)/shard_map/ppermute | solution.py:250
  69.2 2.1 %collective-permute-start.20 = (bf16[32,2688]{1,0:T(8,128)(2,1)S(1)}, bf16[32,2688]{1,0:T(8,128)(2,1)S(1)}, u32[]{:S(2)}, u32[]{:S(2)}) collective-permute-start(bf16[32,2688]{1,0:T(8,128)(2,1)S(1)} %shard_map.71), channel_id=1, source_target_pairs={{0,12},{1,13},{2,14},{3,15},{4,8},{5,9},{6,10},{7,11},{8,4},{9,5},... | collective-permute-start | bytes 516104 | tf_op jit(solution)/shard_map/ppermute | solution.py:250
  72.3 5.6 %collective-permute-done.22.refs_1_ = bf16[32,2688]{1,0:T(8,128)(2,1)S(1)} collective-permute-done((bf16[32,2688]{1,0:T(8,128)(2,1)S(1)}, bf16[32,2688]{1,0:T(8,128)(2,1)S(1)}, u32[]{:S(2)}, u32[]{:S(2)}) %collective-permute-start.22) | collective-permute-done | bytes 172064 | tf_op jit(solution)/shard_map/ppermute | solution.py:250
  (46 shorter events, 13.0 us)
Async XLA Ops:
  1.9 51.1 %collective-permute-start.17 = (bf16[256,2688]{1,0:T(8,128)(2,1)S(1)}, bf16[256,2688]{1,0:T(8,128)(2,1)S(1)}, u32[]{:S(2)}, u32[]{:S(2)}) collective-permute-start(bf16[256,2688]{1,0:T(8,128)(2,1)S(1)} %shard_map.69), channel_id=1, source_target_pairs={{0,1},{1,0},{2,3},{3,2},{4,5},{5,4},{6,7},{7,6},{8,9},{9,8},{10,11... | collective-permute-start | bytes 4128776 | tf_op jit(solution)/shard_map/ppermute | solution.py:250
  5.3 3.2 %collective-permute-start = (bf16[4,16,256]{2,1,0:T(8,128)(2,1)S(1)}, bf16[4,16,256]{2,1,0:T(8,128)(2,1)S(1)}, u32[]{:S(2)}, u32[]{:S(2)}) collective-permute-start(bf16[4,16,256]{2,1,0:T(8,128)(2,1)S(1)} %get-tuple-element.28), channel_id=1, source_target_pairs={{0,1},{1,0},{2,3},{3,2},{4,5},{5,4},{6,7},{7,6},{8,9},{9,8},{10,11... | collective-permute-start | bytes 98312 | tf_op jit(solution)/shard_map/ppermute | solution.py:250
  5.4 4.9 %collective-permute-start.1 = (bf16[4,16,256]{2,1,0:T(8,128)(2,1)S(1)}, bf16[4,16,256]{2,1,0:T(8,128)(2,1)S(1)}, u32[]{:S(2)}, u32[]{:S(2)}) collective-permute-start(bf16[4,16,256]{2,1,0:T(8,128)(2,1)S(1)} %get-tuple-element.29), channel_id=1, source_target_pairs={{0,2},{1,3},{2,0},{3,1},{4,6},{5,7},{6,4},{7,5},{8,10},{9,11},{10,... | collective-permute-start | bytes 98312 | tf_op jit(solution)/shard_map/ppermute | solution.py:250
  8.4 3.7 %collective-permute-start.2 = (bf16[4,16,256]{2,1,0:T(8,128)(2,1)S(1)}, bf16[4,16,256]{2,1,0:T(8,128)(2,1)S(1)}, u32[]{:S(2)}, u32[]{:S(2)}) collective-permute-start(bf16[4,16,256]{2,1,0:T(8,128)(2,1)S(1)} %get-tuple-element.30), channel_id=1, source_target_pairs={{0,3},{1,2},{2,1},{3,0},{4,7},{5,6},{6,5},{7,4},{8,11},{9,10},{10,... | collective-permute-start | bytes 98312 | tf_op jit(solution)/shard_map/ppermute | solution.py:250
  8.4 24.9 %collective-permute-start.6 = (bf16[4,528,128]{2,1,0:T(8,128)(2,1)S(1)}, bf16[4,528,128]{2,1,0:T(8,128)(2,1)S(1)}, u32[]{:S(2)}, u32[]{:S(2)}) collective-permute-start(bf16[4,528,128]{2,1,0:T(8,128)(2,1)S(1)} %get-tuple-element.32), channel_id=1, source_target_pairs={{0,1},{1,0},{2,3},{3,2},{4,5},{5,4},{6,7},{7,6},{8,9},{9,8},{10,11... | collective-permute-start | bytes 1622024 | tf_op jit(solution)/shard_map/ppermute | solution.py:250
  12.1 5.6 %collective-permute-start.3 = (bf16[4,4,16,256]{3,2,1,0:T(8,128)(2,1)S(1)}, bf16[4,4,16,256]{3,2,1,0:T(8,128)(2,1)S(1)}, u32[]{:S(2)}, u32[]{:S(2)}) collective-permute-start(bf16[4,4,16,256]{3,2,1,0:T(8,128)(2,1)S(1)} %pad_maximum_fusion.refs_0_), channel_id=1, source_target_pairs={{0,4},{1,5},{2,6},{3,7},{4,0},{5,1},{6,2},{7,3},{8,12},{9,13},{10,... | collective-permute-start | bytes 393224 | tf_op jit(solution)/shard_map/ppermute | solution.py:250
  13.7 18.4 %collective-permute-start.10 = (bf16[2,528,128]{2,1,0:T(8,128)(2,1)S(1)}, bf16[2,528,128]{2,1,0:T(8,128)(2,1)S(1)}, u32[]{:S(2)}, u32[]{:S(2)}) collective-permute-start(bf16[2,528,128]{2,1,0:T(8,128)(2,1)S(1)} %get-tuple-element.36), channel_id=1, source_target_pairs={{0,3},{1,2},{2,1},{3,0},{4,7},{5,6},{6,5},{7,4},{8,11},{9,10},{10,... | collective-permute-start | bytes 811016 | tf_op jit(solution)/shard_map/ppermute | solution.py:250
  13.7 9.7 %collective-permute-start.4 = (bf16[4,4,16,256]{3,2,1,0:T(8,128)(2,1)S(1)}, bf16[4,4,16,256]{3,2,1,0:T(8,128)(2,1)S(1)}, u32[]{:S(2)}, u32[]{:S(2)}) collective-permute-start(bf16[4,4,16,256]{3,2,1,0:T(8,128)(2,1)S(1)} %pad_maximum_fusion.refs_0_), channel_id=1, source_target_pairs={{0,8},{1,9},{2,10},{3,11},{4,12},{5,13},{6,14},{7,15},{8,0},{9,1},... | collective-permute-start | bytes 393224 | tf_op jit(solution)/shard_map/ppermute | solution.py:250
  17.6 14.5 %collective-permute-start.9 = (bf16[2,528,128]{2,1,0:T(8,128)(2,1)S(1)}, bf16[2,528,128]{2,1,0:T(8,128)(2,1)S(1)}, u32[]{:S(2)}, u32[]{:S(2)}) collective-permute-start(bf16[2,528,128]{2,1,0:T(8,128)(2,1)S(1)} %get-tuple-element.35), channel_id=1, source_target_pairs={{0,2},{1,3},{2,0},{3,1},{4,6},{5,7},{6,4},{7,5},{8,10},{9,11},{10,... | collective-permute-start | bytes 811016 | tf_op jit(solution)/shard_map/ppermute | solution.py:250
  23.5 7.1 %collective-permute-start.5 = (bf16[4,4,16,256]{3,2,1,0:T(8,128)(2,1)S(1)}, bf16[4,4,16,256]{3,2,1,0:T(8,128)(2,1)S(1)}, u32[]{:S(2)}, u32[]{:S(2)}) collective-permute-start(bf16[4,4,16,256]{3,2,1,0:T(8,128)(2,1)S(1)} %pad_maximum_fusion.refs_0_), channel_id=1, source_target_pairs={{0,12},{1,13},{2,14},{3,15},{4,8},{5,9},{6,10},{7,11},{8,4},{9,5},... | collective-permute-start | bytes 393224 | tf_op jit(solution)/shard_map/ppermute | solution.py:250
  30.5 5.6 %collective-permute-start.12 = (bf16[1,528,128]{2,1,0:T(8,128)(2,1)S(1)}, bf16[1,528,128]{2,1,0:T(8,128)(2,1)S(1)}, u32[]{:S(2)}, u32[]{:S(2)}) collective-permute-start(bf16[1,528,128]{2,1,0:T(8,128)(2,1)S(1)} %get-tuple-element.37), channel_id=1, source_target_pairs={{0,2},{1,3},{2,0},{3,1},{4,6},{5,7},{6,4},{7,5},{8,10},{9,11},{10,... | collective-permute-start | bytes 405512 | tf_op jit(solution)/shard_map/ppermute | solution.py:250
  32.1 6.9 %collective-permute-start.13 = (bf16[1,528,128]{2,1,0:T(8,128)(2,1)S(1)}, bf16[1,528,128]{2,1,0:T(8,128)(2,1)S(1)}, u32[]{:S(2)}, u32[]{:S(2)}) collective-permute-start(bf16[1,528,128]{2,1,0:T(8,128)(2,1)S(1)} %get-tuple-element.38), channel_id=1, source_target_pairs={{0,3},{1,2},{2,1},{3,0},{4,7},{5,6},{6,5},{7,4},{8,11},{9,10},{10,... | collective-permute-start | bytes 405512 | tf_op jit(solution)/shard_map/ppermute | solution.py:250
  32.1 9.6 %collective-permute-start.7 = (bf16[1,528,128]{2,1,0:T(8,128)(2,1)S(1)}, bf16[1,528,128]{2,1,0:T(8,128)(2,1)S(1)}, u32[]{:S(2)}, u32[]{:S(2)}) collective-permute-start(bf16[1,528,128]{2,1,0:T(8,128)(2,1)S(1)} %get-tuple-element.33), channel_id=1, source_target_pairs={{0,2},{1,3},{2,0},{3,1},{4,6},{5,7},{6,4},{7,5},{8,10},{9,11},{10,... | collective-permute-start | bytes 405512 | tf_op jit(solution)/shard_map/ppermute | solution.py:250
  33.3 11.2 %collective-permute-start.8 = (bf16[1,528,128]{2,1,0:T(8,128)(2,1)S(1)}, bf16[1,528,128]{2,1,0:T(8,128)(2,1)S(1)}, u32[]{:S(2)}, u32[]{:S(2)}) collective-permute-start(bf16[1,528,128]{2,1,0:T(8,128)(2,1)S(1)} %get-tuple-element.34), channel_id=1, source_target_pairs={{0,3},{1,2},{2,1},{3,0},{4,7},{5,6},{6,5},{7,4},{8,11},{9,10},{10,... | collective-permute-start | bytes 405512 | tf_op jit(solution)/shard_map/ppermute | solution.py:250
  36.1 9.7 %collective-permute-start.15 = (bf16[272,256]{1,0:T(8,128)(2,1)S(1)}, bf16[272,256]{1,0:T(8,128)(2,1)S(1)}, u32[]{:S(2)}, u32[]{:S(2)}) collective-permute-start(bf16[272,256]{1,0:T(8,128)(2,1)S(1)} %shard_map.67), channel_id=1, source_target_pairs={{0,12},{1,13},{2,14},{3,15},{4,8},{5,9},{6,10},{7,11},{8,4},{9,5},... | collective-permute-start | bytes 417800 | tf_op jit(solution)/shard_map/ppermute | solution.py:250
  40.2 10.8 %collective-permute-start.14 = (bf16[272,256]{1,0:T(8,128)(2,1)S(1)}, bf16[272,256]{1,0:T(8,128)(2,1)S(1)}, u32[]{:S(2)}, u32[]{:S(2)}) collective-permute-start(bf16[272,256]{1,0:T(8,128)(2,1)S(1)} %shard_map.66), channel_id=1, source_target_pairs={{0,8},{1,9},{2,10},{3,11},{4,12},{5,13},{6,14},{7,15},{8,0},{9,1},... | collective-permute-start | bytes 417800 | tf_op jit(solution)/shard_map/ppermute | solution.py:250
  41.8 9.3 %collective-permute-start.11 = (bf16[272,256]{1,0:T(8,128)(2,1)S(1)}, bf16[272,256]{1,0:T(8,128)(2,1)S(1)}, u32[]{:S(2)}, u32[]{:S(2)}) collective-permute-start(bf16[272,256]{1,0:T(8,128)(2,1)S(1)} %shard_map.65), channel_id=1, source_target_pairs={{0,4},{1,5},{2,6},{3,7},{4,0},{5,1},{6,2},{7,3},{8,12},{9,13},{10,... | collective-permute-start | bytes 417800 | tf_op jit(solution)/shard_map/ppermute | solution.py:250
  54.0 7.8 %collective-permute-start.23 = (bf16[32,2688]{1,0:T(8,128)(2,1)S(1)}, bf16[32,2688]{1,0:T(8,128)(2,1)S(1)}, u32[]{:S(2)}, u32[]{:S(2)}) collective-permute-start(bf16[32,2688]{1,0:T(8,128)(2,1)S(1)} %get-tuple-element.46), channel_id=1, source_target_pairs={{0,2},{1,3},{2,0},{3,1},{4,6},{5,7},{6,4},{7,5},{8,10},{9,11},{10,... | collective-permute-start | bytes 516104 | tf_op jit(solution)/shard_map/ppermute | solution.py:250
  56.5 8.9 %collective-permute-start.21 = (bf16[32,2688]{1,0:T(8,128)(2,1)S(1)}, bf16[32,2688]{1,0:T(8,128)(2,1)S(1)}, u32[]{:S(2)}, u32[]{:S(2)}) collective-permute-start(bf16[32,2688]{1,0:T(8,128)(2,1)S(1)} %get-tuple-element.44), channel_id=1, source_target_pairs={{0,2},{1,3},{2,0},{3,1},{4,6},{5,7},{6,4},{7,5},{8,10},{9,11},{10,... | collective-permute-start | bytes 516104 | tf_op jit(solution)/shard_map/ppermute | solution.py:250
  56.6 12.5 %collective-permute-start.19 = (bf16[32,2688]{1,0:T(8,128)(2,1)S(1)}, bf16[32,2688]{1,0:T(8,128)(2,1)S(1)}, u32[]{:S(2)}, u32[]{:S(2)}) collective-permute-start(bf16[32,2688]{1,0:T(8,128)(2,1)S(1)} %get-tuple-element.42), channel_id=1, source_target_pairs={{0,2},{1,3},{2,0},{3,1},{4,6},{5,7},{6,4},{7,5},{8,10},{9,11},{10,... | collective-permute-start | bytes 516104 | tf_op jit(solution)/shard_map/ppermute | solution.py:250
  58.5 13.7 %collective-permute-start.18 = (bf16[32,2688]{1,0:T(8,128)(2,1)S(1)}, bf16[32,2688]{1,0:T(8,128)(2,1)S(1)}, u32[]{:S(2)}, u32[]{:S(2)}) collective-permute-start(bf16[32,2688]{1,0:T(8,128)(2,1)S(1)} %get-tuple-element.40), channel_id=1, source_target_pairs={{0,2},{1,3},{2,0},{3,1},{4,6},{5,7},{6,4},{7,5},{8,10},{9,11},{10,... | collective-permute-start | bytes 516104 | tf_op jit(solution)/shard_map/ppermute | solution.py:250
  61.8 10.5 %collective-permute-start.24 = (bf16[32,2688]{1,0:T(8,128)(2,1)S(1)}, bf16[32,2688]{1,0:T(8,128)(2,1)S(1)}, u32[]{:S(2)}, u32[]{:S(2)}) collective-permute-start(bf16[32,2688]{1,0:T(8,128)(2,1)S(1)} %shard_map.73), channel_id=1, source_target_pairs={{0,8},{1,9},{2,10},{3,11},{4,12},{5,13},{6,14},{7,15},{8,0},{9,1},... | collective-permute-start | bytes 516104 | tf_op jit(solution)/shard_map/ppermute | solution.py:250
  65.5 12.4 %collective-permute-start.22 = (bf16[32,2688]{1,0:T(8,128)(2,1)S(1)}, bf16[32,2688]{1,0:T(8,128)(2,1)S(1)}, u32[]{:S(2)}, u32[]{:S(2)}) collective-permute-start(bf16[32,2688]{1,0:T(8,128)(2,1)S(1)} %shard_map.72), channel_id=1, source_target_pairs={{0,4},{1,5},{2,6},{3,7},{4,0},{5,1},{6,2},{7,3},{8,12},{9,13},{10,... | collective-permute-start | bytes 516104 | tf_op jit(solution)/shard_map/ppermute | solution.py:250
  69.2 8.7 %collective-permute-start.20 = (bf16[32,2688]{1,0:T(8,128)(2,1)S(1)}, bf16[32,2688]{1,0:T(8,128)(2,1)S(1)}, u32[]{:S(2)}, u32[]{:S(2)}) collective-permute-start(bf16[32,2688]{1,0:T(8,128)(2,1)S(1)} %shard_map.71), channel_id=1, source_target_pairs={{0,12},{1,13},{2,14},{3,15},{4,8},{5,9},{6,10},{7,11},{8,4},{9,5},... | collective-permute-start | bytes 516104 | tf_op jit(solution)/shard_map/ppermute | solution.py:250
  (4 other events, 17.1 us)

commit v7 on v6

--- a/solution.py
+++ b/solution.py
@@ -12,7 +12,7 @@
 KEY_VALUE_HEADS = 16
 HEAD_SIZE = 128
 INNER = 4
-CHUNKS = 3
+EARLY_PART = 20
 
 score_scale = 168.0 ** (-0.5)
 masked_value = -1e30
@@ -179,46 +179,71 @@
         out[:, cols] = acc.astype(bf16)
 
 
-def project_kernel(mine_ref, other_ref, w_mine_ref, w_other_ref, *out_refs, groups, rows, blocks):
+def project_kernel(
+    mine_ref, other_ref, w_mine_ref, w_other_ref, *out_refs, order, outer, rows, early, blocks
+):
     _, z, r = place()
     y = lax.shift_right_logical(r, 1)
     half = w_other_ref.shape[1]
-    cols = half // blocks
-
-    def gather(ref, side):
+    sends, keeps, earlies = out_refs[:outer], out_refs[outer:2 * outer], out_refs[2 * outer:]
+
+    def gather(ref, first, size):
         found = []
-        for group in groups:
-            for kk in group:
-                at = (lax.bitwise_xor(z, kk) * INNER + side * 2) * rows
-                found.append(ref[pl.ds(pl.multiple_of(at, 2 * rows), 2 * rows), :])
-        return jnp.concatenate(found, axis=0)
-
-    mine = jnp.concatenate([gather(mine_ref, 1 - y), gather(mine_ref, y)], axis=0)
-    other = jnp.concatenate([gather(other_ref, 1 - y), gather(other_ref, y)], axis=0)
+        for kk in order:
+            at = (lax.bitwise_xor(z, kk) * INNER + first) * rows
+            found.append(ref[pl.ds(pl.multiple_of(at, size), size), :])
+        return found
+
+    def terms(mine, other, begin, cols):
+        col = pl.multiple_of(lax.bitwise_and(r, 1) * half + begin, 128)
+        term = jnp.dot(mine, w_mine_ref[:, pl.ds(col, cols)], preferred_element_type=f32)
+        return term + jnp.dot(
+            other, w_other_ref[:, begin:begin + cols], preferred_element_type=f32
+        )
+
+    def store(term, outs, here):
+        for i, out in enumerate(outs):
+            size = out.shape[0]
+            out[:, here] = term[i * size:(i + 1) * size].astype(out.dtype)
+
+    span = 2 * rows
+    lines = [
+        jnp.concatenate(gather(ref, 2 * (1 - y), span) + gather(ref, 2 * y, span), axis=0)
+        for ref in (mine_ref, other_ref)
+    ]
+    cols = (half - early) // blocks
     for j in range(blocks):
-        here = slice(j * cols, (j + 1) * cols)
-        col = pl.multiple_of(lax.bitwise_and(r, 1) * half + j * cols, 128)
-        term = jnp.dot(mine, w_mine_ref[:, pl.ds(col, cols)], preferred_element_type=f32)
-        term = term + jnp.dot(other, w_other_ref[:, here], preferred_element_type=f32)
-        at = 0
-        for group, out in zip(groups + groups, out_refs):
-            size = 2 * rows * len(group)
-            out[:, here] = term[at:at + size].astype(out.dtype)
-            at += size
+        term = terms(*lines, early + j * cols, cols)
+        store(term, sends + keeps, slice(j * cols, (j + 1) * cols))
+    lines = [
+        jnp.concatenate(gather(ref, 0, INNER * rows), axis=0) for ref in (mine_ref, other_ref)
+    ]
+    store(terms(*lines, 0, early), earlies, slice(0, early))
 
 
 def first_sum_kernel(keep_ref, got_ref, out_ref):
     out_ref[...] = (keep_ref[...] + got_ref[...].astype(f32)).astype(out_ref.dtype)
 
 
-def last_sum_kernel(keep_ref, got_ref, *refs, rows):
+def early_sum_kernel(*refs, span):
+    *parts, send_ref, keep_ref, total_ref = refs
+    _, _, r = place()
+    y = lax.shift_right_logical(r, 1)
+    total_ref[...] = functools.reduce(jnp.add, [part[...].astype(f32) for part in parts])
+    send_ref[...] = total_ref[pl.ds(pl.multiple_of((1 - y) * span, span), span), :].astype(bf16)
+    keep_ref[...] = total_ref[pl.ds(pl.multiple_of(y * span, span), span), :]
+
+
+def last_sum_kernel(early_keep_ref, early_got_ref, keep_ref, got_ref, *refs, rows):
     *parts, mine_ref, other_ref, total_ref = refs
     _, _, r = place()
     c = lax.bitwise_and(r, 1)
+    early = early_keep_ref.shape[1]
+    total_ref[:, :early] = early_keep_ref[...] + early_got_ref[...].astype(f32)
     total = keep_ref[...] + got_ref[...].astype(f32)
     for part in parts:
         total = total + part[...].astype(f32)
-    total_ref[...] = total
+    total_ref[:, early:] = total
     mine_ref[...] = total_ref[pl.ds(pl.multiple_of(c * rows, rows), rows), :].astype(bf16)
     other_ref[...] = total_ref[pl.ds(pl.multiple_of((1 - c) * rows, rows), rows), :].astype(bf16)
 
@@ -243,7 +268,9 @@
     model = out_weight.shape[1]
     half = model // 2
     assert heads * copies == QUERY_HEADS // KEY_VALUE_HEADS and keys <= 256
-    blocks = CHUNKS if half % (CHUNKS * 128) == 0 else 1
+    tiles = half // 128
+    early = 128 * (tiles * EARLY_PART // 100)
+    blocks = 2 if (half - early) % 256 == 0 else 1
     shape = jax.ShapeDtypeStruct
 
     def swap(x, k):
@@ -308,22 +335,31 @@
     other = swap(merged, 1)
 
     span = 2 * rows
-    term_groups = [[kk] for kk in order]
+    main = half - early
     terms = call(
-        functools.partial(project_kernel, groups=term_groups, rows=rows, blocks=blocks),
+        functools.partial(
+            project_kernel, order=order, outer=outer, rows=rows, early=early, blocks=blocks
+        ),
         [merged, other, out_weight, w_other],
-        [shape((span * len(g), half), bf16) for g in term_groups]
-        + [shape((span * len(g), half), f32) for g in term_groups],
+        [shape((span, main), bf16)] * outer + [shape((span, main), f32)] * outer
+        + [shape((2 * span, early), bf16)] * (outer - 1) + [shape((2 * span, early), f32)],
         flops=4 * rows_all * width * half, limit=20,
     )
-    sends, keeps = terms[:outer], terms[outer:]
+    sends, keeps, earlies = terms[:outer], terms[outer:2 * outer], terms[2 * outer:]
     gots = [swap(x, 2) for x in sends]
+    early_gots = [swap(x, kk * INNER) for kk, x in zip(order[:-1], earlies)]
     parts = []
     for i, kk in enumerate(order[:-1]):
-        (part,) = call(first_sum_kernel, [keeps[i], gots[i]], [shape((span, half), bf16)])
+        (part,) = call(first_sum_kernel, [keeps[i], gots[i]], [shape((span, main), bf16)])
         parts.append(swap(part, kk * INNER))
+    early_send, early_keep = call(
+        functools.partial(early_sum_kernel, span=span),
+        [earlies[-1]] + early_gots, [shape((span, early), bf16), shape((span, early), f32)],
+        scratch=[pltpu.VMEM((2 * span, early), f32)],
+    )
     mine, theirs = call(
-        functools.partial(last_sum_kernel, rows=rows), [keeps[-1], gots[-1]] + parts,
+        functools.partial(last_sum_kernel, rows=rows),
+        [early_keep, swap(early_send, 2), keeps[-1], gots[-1]] + parts,
         [shape((rows, half), bf16)] * 2, scratch=[pltpu.VMEM((span, half), f32)],
     )
     (joined,) = call(join_kernel, [mine, swap(theirs, 1)], [shape((rows, model), bf16)])

time: 80.2 us -> 86.7 us (1.081)
  starting transfers between devices: 27.1 us -> 33.2 us
    ppermute x26 -> x30, starting transfers between devices: 27.1 us -> 33.2 us  [swap(): return lax.ppermute(x, 'seq', [(i, i ^ k) for i in range(devices)])]
    ppermute x26 -> x30, waiting for transfers between devices: 40.2 us -> 40.4 us  [swap(): return lax.ppermute(x, 'seq', [(i, i ^ k) for i in range(devices)])]
    pallas_call x12 -> x13, Pallas kernels: 7.38 us -> 7.33 us  [call(): pl.pallas_call(kernel, out_shape=tuple(outs), in_specs=in_specs, out_spec...]
  transfers between devices with their start and end apart: 26 -> 30, of which waited for: 16 -> 16; matrix products, arithmetic and copies ran while one was open for 0% -> 0% of each run, Pallas kernels for 10% -> 9%
where the time goes in v7:
time: 86.7 us; the launch traced here: 86.5 us
  waiting for transfers between devices  40.4 us (47%)
  starting transfers between devices  33.2 us (38%)
  Pallas kernels  9.54 us (11%)
  local copies, waits for them, and re-layouts  1.78 us (2%)
  between operations  1.45 us (2%)
    ppermute x30, waiting for transfers between devices, swap(): return lax.ppermute(x, 'seq', [(i, i ^ k) for i in range(devices)])  40.4 us
    ppermute x30, starting transfers between devices, swap(): return lax.ppermute(x, 'seq', [(i, i ^ k) for i in range(devices)])  33.2 us
    pallas_call x13, Pallas kernels, call(): pl.pallas_call(kernel, out_shape=tuple(outs), in_specs=in_specs, out_spec...  7.33 us
    pallas_call x1, Pallas kernels, layer(): pl.pallas_call(functools.partial(split_kernel, outer=outer, width=width,...  2.21 us
    unnamed x4, local copies, waits for them, and re-layouts  1.78 us
  transfers between devices with their start and end apart: 30, of which 16 were waited for; matrix products, arithmetic and copies ran while one was open for 0% of the time, Pallas kernels for 9%

profile of v7, /device:TPU:0, one launch (start us, length us, event | category | flops | bytes accessed | tf_op | source)
XLA Modules:
  0.0 86.5 jit_solution(9351626002457529889)
XLA Ops:
  0.0 1.8 %copy-done = bf16[256,5376]{1,0:T(8,128)(2,1)S(1)} copy-done((bf16[256,5376]{1,0:T(8,128)(2,1)S(1)}, bf16[256,5376]{1,0:T(8,128)(2,1)}, u32[]{:S(2)}) %copy-start) | copy-done | bytes 2752536
  3.1 2.2 %split.1 = (bf16[4,16,256]{2,1,0:T(8,128)(2,1)S(1)}, bf16[4,16,256]{2,1,0:T(8,128)(2,1)S(1)}, bf16[4,16,256]{2,1,0:T(8,128)(2,1)S(1)}, bf16[4,16,256]{2,1,0:T(8,...) custom-call(s32[1]{0:T(128)S(6)} %copy.7.live_ref, ...), custom_call_target="tpu_custom_call" | custom-call | tf_op jit(solution)/shard_map/split/pallas_call | solution.py:288
  5.4 3.0 %collective-permute-start.1 = (bf16[4,16,256]{2,1,0:T(8,128)(2,1)S(1)}, bf16[4,16,256]{2,1,0:T(8,128)(2,1)S(1)}, u32[]{:S(2)}, u32[]{:S(2)}) collective-permute-start(bf16[4,16,256]{2,1,0:T(8,128)(2,1)S(1)} %get-tuple-element.35), channel_id=1, source_target_pairs={{0,2},{1,3},{2,0},{3,1},{4,6},{5,7},{6,4},{7,5},{8,10},{9,11},{10,... | collective-permute-start | bytes 98312 | tf_op jit(solution)/shard_map/ppermute | solution.py:277
  8.5 1.8 %collective-permute-done.1 = bf16[4,16,256]{2,1,0:T(8,128)(2,1)S(1)} collective-permute-done((bf16[4,16,256]{2,1,0:T(8,128)(2,1)S(1)}, bf16[4,16,256]{2,1,0:T(8,128)(2,1)S(1)}, u32[]{:S(2)}, u32[]{:S(2)}) %collective-permute-start.1) | collective-permute-done | bytes 32800 | tf_op jit(solution)/shard_map/ppermute | solution.py:277
  10.3 1.8 %collective-permute-done.2 = bf16[4,16,256]{2,1,0:T(8,128)(2,1)S(1)} collective-permute-done((bf16[4,16,256]{2,1,0:T(8,128)(2,1)S(1)}, bf16[4,16,256]{2,1,0:T(8,128)(2,1)S(1)}, u32[]{:S(2)}, u32[]{:S(2)}) %collective-permute-start.2) | collective-permute-done | bytes 32800 | tf_op jit(solution)/shard_map/ppermute | solution.py:277
  12.1 1.6 %collective-permute-start.3 = (bf16[4,4,16,256]{3,2,1,0:T(8,128)(2,1)S(1)}, bf16[4,4,16,256]{3,2,1,0:T(8,128)(2,1)S(1)}, u32[]{:S(2)}, u32[]{:S(2)}) collective-permute-start(bf16[4,4,16,256]{3,2,1,0:T(8,128)(2,1)S(1)} %pad_maximum_fusion.refs_0_), channel_id=1, source_target_pairs={{0,4},{1,5},{2,6},{3,7},{4,0},{5,1},{6,2},{7,3},{8,12},{9,13},{10,... | collective-permute-start | bytes 393224 | tf_op jit(solution)/shard_map/ppermute | solution.py:277
  13.7 2.6 %collective-permute-start.4 = (bf16[4,4,16,256]{3,2,1,0:T(8,128)(2,1)S(1)}, bf16[4,4,16,256]{3,2,1,0:T(8,128)(2,1)S(1)}, u32[]{:S(2)}, u32[]{:S(2)}) collective-permute-start(bf16[4,4,16,256]{3,2,1,0:T(8,128)(2,1)S(1)} %pad_maximum_fusion.refs_0_), channel_id=1, source_target_pairs={{0,8},{1,9},{2,10},{3,11},{4,12},{5,13},{6,14},{7,15},{8,0},{9,1},... | collective-permute-start | bytes 393224 | tf_op jit(solution)/shard_map/ppermute | solution.py:277
  18.1 5.4 %collective-permute-done.4.refs_2_ = bf16[4,4,16,256]{3,2,1,0:T(8,128)(2,1)S(1)} collective-permute-done((bf16[4,4,16,256]{3,2,1,0:T(8,128)(2,1)S(1)}, bf16[4,4,16,256]{3,2,1,0:T(8,128)(2,1)S(1)}, u32[]{:S(2)}, u32[]{:S(2)}) %collective-permute-start.4) | collective-permute-done | bytes 131104 | tf_op jit(solution)/shard_map/ppermute | solution.py:277
  23.5 2.5 %collective-permute-start.5 = (bf16[4,4,16,256]{3,2,1,0:T(8,128)(2,1)S(1)}, bf16[4,4,16,256]{3,2,1,0:T(8,128)(2,1)S(1)}, u32[]{:S(2)}, u32[]{:S(2)}) collective-permute-start(bf16[4,4,16,256]{3,2,1,0:T(8,128)(2,1)S(1)} %pad_maximum_fusion.refs_0_), channel_id=1, source_target_pairs={{0,12},{1,13},{2,14},{3,15},{4,8},{5,9},{6,10},{7,11},{8,4},{9,5},... | collective-permute-start | bytes 393224 | tf_op jit(solution)/shard_map/ppermute | solution.py:277
  26.0 4.5 %collective-permute-done.5.refs_3_ = bf16[4,4,16,256]{3,2,1,0:T(8,128)(2,1)S(1)} collective-permute-done((bf16[4,4,16,256]{3,2,1,0:T(8,128)(2,1)S(1)}, bf16[4,4,16,256]{3,2,1,0:T(8,128)(2,1)S(1)}, u32[]{:S(2)}, u32[]{:S(2)}) %collective-permute-start.5) | collective-permute-done | bytes 131104 | tf_op jit(solution)/shard_map/ppermute | solution.py:277
  30.5 1.6 %collective-permute-start.12 = (bf16[1,528,128]{2,1,0:T(8,128)(2,1)S(1)}, bf16[1,528,128]{2,1,0:T(8,128)(2,1)S(1)}, u32[]{:S(2)}, u32[]{:S(2)}) collective-permute-start(bf16[1,528,128]{2,1,0:T(8,128)(2,1)S(1)} %get-tuple-element.43), channel_id=1, source_target_pairs={{0,2},{1,3},{2,0},{3,1},{4,6},{5,7},{6,4},{7,5},{8,10},{9,11},{10,... | collective-permute-start | bytes 405512 | tf_op jit(solution)/shard_map/ppermute | solution.py:277
  33.3 1.5 %collective-permute-start.8 = (bf16[1,528,128]{2,1,0:T(8,128)(2,1)S(1)}, bf16[1,528,128]{2,1,0:T(8,128)(2,1)S(1)}, u32[]{:S(2)}, u32[]{:S(2)}) collective-permute-start(bf16[1,528,128]{2,1,0:T(8,128)(2,1)S(1)} %get-tuple-element.40), channel_id=1, source_target_pairs={{0,3},{1,2},{2,1},{3,0},{4,7},{5,6},{6,5},{7,4},{8,11},{9,10},{10,... | collective-permute-start | bytes 405512 | tf_op jit(solution)/shard_map/ppermute | solution.py:277
  36.1 2.4 %collective-permute-start.15 = (bf16[272,256]{1,0:T(8,128)(2,1)S(1)}, bf16[272,256]{1,0:T(8,128)(2,1)S(1)}, u32[]{:S(2)}, u32[]{:S(2)}) collective-permute-start(bf16[272,256]{1,0:T(8,128)(2,1)S(1)} %shard_map.67), channel_id=1, source_target_pairs={{0,12},{1,13},{2,14},{3,15},{4,8},{5,9},{6,10},{7,11},{8,4},{9,5},... | collective-permute-start | bytes 417800 | tf_op jit(solution)/shard_map/ppermute | solution.py:277
  41.8 2.7 %collective-permute-start.11 = (bf16[272,256]{1,0:T(8,128)(2,1)S(1)}, bf16[272,256]{1,0:T(8,128)(2,1)S(1)}, u32[]{:S(2)}, u32[]{:S(2)}) collective-permute-start(bf16[272,256]{1,0:T(8,128)(2,1)S(1)} %shard_map.65), channel_id=1, source_target_pairs={{0,4},{1,5},{2,6},{3,7},{4,0},{5,1},{6,2},{7,3},{8,12},{9,13},{10,... | collective-permute-start | bytes 417800 | tf_op jit(solution)/shard_map/ppermute | solution.py:277
  45.8 5.3 %collective-permute-done.14.refs_2_ = bf16[272,256]{1,0:T(8,128)(2,1)S(1)} collective-permute-done((bf16[272,256]{1,0:T(8,128)(2,1)S(1)}, bf16[272,256]{1,0:T(8,128)(2,1)S(1)}, u32[]{:S(2)}, u32[]{:S(2)}) %collective-permute-start.14) | collective-permute-done | bytes 139296 | tf_op jit(solution)/shard_map/ppermute | solution.py:277
  53.9 2.6 %collective-permute-start.27 = (bf16[32,2176]{1,0:T(8,128)(2,1)S(1)}, bf16[32,2176]{1,0:T(8,128)(2,1)S(1)}, u32[]{:S(2)}, u32[]{:S(2)}) collective-permute-start(bf16[32,2176]{1,0:T(8,128)(2,1)S(1)} %get-tuple-element.58), channel_id=1, source_target_pairs={{0,2},{1,3},{2,0},{3,1},{4,6},{5,7},{6,4},{7,5},{8,10},{9,11},{10,... | collective-permute-start | bytes 417800 | tf_op jit(solution)/shard_map/ppermute | solution.py:277
  56.5 1.9 %collective-permute-start.23 = (bf16[32,2176]{1,0:T(8,128)(2,1)S(1)}, bf16[32,2176]{1,0:T(8,128)(2,1)S(1)}, u32[]{:S(2)}, u32[]{:S(2)}) collective-permute-start(bf16[32,2176]{1,0:T(8,128)(2,1)S(1)} %get-tuple-element.54), channel_id=1, source_target_pairs={{0,2},{1,3},{2,0},{3,1},{4,6},{5,7},{6,4},{7,5},{8,10},{9,11},{10,... | collective-permute-start | bytes 417800 | tf_op jit(solution)/shard_map/ppermute | solution.py:277
  58.5 1.5 %collective-permute-start.18 = (bf16[64,512]{1,0:T(8,128)(2,1)S(1)}, bf16[64,512]{1,0:T(8,128)(2,1)S(1)}, u32[]{:S(2)}, u32[]{:S(2)}) collective-permute-start(bf16[64,512]{1,0:T(8,128)(2,1)S(1)} %get-tuple-element.46), channel_id=1, source_target_pairs={{0,12},{1,13},{2,14},{3,15},{4,8},{5,9},{6,10},{7,11},{8,4},{9,5},... | collective-permute-start | bytes 196616 | tf_op jit(solution)/shard_map/ppermute | solution.py:277
  61.0 2.0 %collective-permute-start.22 = (bf16[32,2176]{1,0:T(8,128)(2,1)S(1)}, bf16[32,2176]{1,0:T(8,128)(2,1)S(1)}, u32[]{:S(2)}, u32[]{:S(2)}) collective-permute-start(bf16[32,2176]{1,0:T(8,128)(2,1)S(1)} %get-tuple-element.52), channel_id=1, source_target_pairs={{0,2},{1,3},{2,0},{3,1},{4,6},{5,7},{6,4},{7,5},{8,10},{9,11},{10,... | collective-permute-start | bytes 417800 | tf_op jit(solution)/shard_map/ppermute | solution.py:277
  64.1 2.8 %collective-permute-done.23.got_ref = bf16[32,2176]{1,0:T(8,128)(2,1)S(1)} collective-permute-done((bf16[32,2176]{1,0:T(8,128)(2,1)S(1)}, bf16[32,2176]{1,0:T(8,128)(2,1)S(1)}, u32[]{:S(2)}, u32[]{:S(2)}) %collective-permute-start.23) | collective-permute-done | bytes 139296 | tf_op jit(solution)/shard_map/ppermute | solution.py:277
  67.0 2.1 %collective-permute-start.24 = (bf16[32,2176]{1,0:T(8,128)(2,1)S(1)}, bf16[32,2176]{1,0:T(8,128)(2,1)S(1)}, u32[]{:S(2)}, u32[]{:S(2)}) collective-permute-start(bf16[32,2176]{1,0:T(8,128)(2,1)S(1)} %shard_map.72), channel_id=1, source_target_pairs={{0,12},{1,13},{2,14},{3,15},{4,8},{5,9},{6,10},{7,11},{8,4},{9,5},... | collective-permute-start | bytes 417800 | tf_op jit(solution)/shard_map/ppermute | solution.py:277
  70.5 9.7 %collective-permute-done.20.refs_3_ = bf16[64,512]{1,0:T(8,128)(2,1)S(1)} collective-permute-done((bf16[64,512]{1,0:T(8,128)(2,1)S(1)}, bf16[64,512]{1,0:T(8,128)(2,1)S(1)}, u32[]{:S(2)}, u32[]{:S(2)}) %collective-permute-start.20) | collective-permute-done | bytes 65568 | tf_op jit(solution)/shard_map/ppermute | solution.py:277
  80.3 1.5 %collective-permute-start.21 = (bf16[32,512]{1,0:T(8,128)(2,1)S(1)}, bf16[32,512]{1,0:T(8,128)(2,1)S(1)}, u32[]{:S(2)}, u32[]{:S(2)}) collective-permute-start(bf16[32,512]{1,0:T(8,128)(2,1)S(1)} %get-tuple-element.50), channel_id=1, source_target_pairs={{0,2},{1,3},{2,0},{3,1},{4,6},{5,7},{6,4},{7,5},{8,10},{9,11},{10,... | collective-permute-start | bytes 98312 | tf_op jit(solution)/shard_map/ppermute | solution.py:277
  81.8 2.5 %collective-permute-done.21.early_got_ref = bf16[32,512]{1,0:T(8,128)(2,1)S(1)} collective-permute-done((bf16[32,512]{1,0:T(8,128)(2,1)S(1)}, bf16[32,512]{1,0:T(8,128)(2,1)S(1)}, u32[]{:S(2)}, u32[]{:S(2)}) %collective-permute-start.21) | collective-permute-done | bytes 32800 | tf_op jit(solution)/shard_map/ppermute | solution.py:277
  (55 shorter events, 17.7 us)
Async XLA Ops:
  1.9 51.1 %collective-permute-start.17 = (bf16[256,2688]{1,0:T(8,128)(2,1)S(1)}, bf16[256,2688]{1,0:T(8,128)(2,1)S(1)}, u32[]{:S(2)}, u32[]{:S(2)}) collective-permute-start(bf16[256,2688]{1,0:T(8,128)(2,1)S(1)} %shard_map.69), channel_id=1, source_target_pairs={{0,1},{1,0},{2,3},{3,2},{4,5},{5,4},{6,7},{7,6},{8,9},{9,8},{10,11... | collective-permute-start | bytes 4128776 | tf_op jit(solution)/shard_map/ppermute | solution.py:277
  8.4 24.9 %collective-permute-start.6 = (bf16[4,528,128]{2,1,0:T(8,128)(2,1)S(1)}, bf16[4,528,128]{2,1,0:T(8,128)(2,1)S(1)}, u32[]{:S(2)}, u32[]{:S(2)}) collective-permute-start(bf16[4,528,128]{2,1,0:T(8,128)(2,1)S(1)} %get-tuple-element.38), channel_id=1, source_target_pairs={{0,1},{1,0},{2,3},{3,2},{4,5},{5,4},{6,7},{7,6},{8,9},{9,8},{10,11... | collective-permute-start | bytes 1622024 | tf_op jit(solution)/shard_map/ppermute | solution.py:277
  12.1 5.6 %collective-permute-start.3 = (bf16[4,4,16,256]{3,2,1,0:T(8,128)(2,1)S(1)}, bf16[4,4,16,256]{3,2,1,0:T(8,128)(2,1)S(1)}, u32[]{:S(2)}, u32[]{:S(2)}) collective-permute-start(bf16[4,4,16,256]{3,2,1,0:T(8,128)(2,1)S(1)} %pad_maximum_fusion.refs_0_), channel_id=1, source_target_pairs={{0,4},{1,5},{2,6},{3,7},{4,0},{5,1},{6,2},{7,3},{8,12},{9,13},{10,... | collective-permute-start | bytes 393224 | tf_op jit(solution)/shard_map/ppermute | solution.py:277
  13.7 18.4 %collective-permute-start.10 = (bf16[2,528,128]{2,1,0:T(8,128)(2,1)S(1)}, bf16[2,528,128]{2,1,0:T(8,128)(2,1)S(1)}, u32[]{:S(2)}, u32[]{:S(2)}) collective-permute-start(bf16[2,528,128]{2,1,0:T(8,128)(2,1)S(1)} %get-tuple-element.42), channel_id=1, source_target_pairs={{0,3},{1,2},{2,1},{3,0},{4,7},{5,6},{6,5},{7,4},{8,11},{9,10},{10,... | collective-permute-start | bytes 811016 | tf_op jit(solution)/shard_map/ppermute | solution.py:277
  13.7 9.7 %collective-permute-start.4 = (bf16[4,4,16,256]{3,2,1,0:T(8,128)(2,1)S(1)}, bf16[4,4,16,256]{3,2,1,0:T(8,128)(2,1)S(1)}, u32[]{:S(2)}, u32[]{:S(2)}) collective-permute-start(bf16[4,4,16,256]{3,2,1,0:T(8,128)(2,1)S(1)} %pad_maximum_fusion.refs_0_), channel_id=1, source_target_pairs={{0,8},{1,9},{2,10},{3,11},{4,12},{5,13},{6,14},{7,15},{8,0},{9,1},... | collective-permute-start | bytes 393224 | tf_op jit(solution)/shard_map/ppermute | solution.py:277
  17.6 14.5 %collective-permute-start.9 = (bf16[2,528,128]{2,1,0:T(8,128)(2,1)S(1)}, bf16[2,528,128]{2,1,0:T(8,128)(2,1)S(1)}, u32[]{:S(2)}, u32[]{:S(2)}) collective-permute-start(bf16[2,528,128]{2,1,0:T(8,128)(2,1)S(1)} %get-tuple-element.41), channel_id=1, source_target_pairs={{0,2},{1,3},{2,0},{3,1},{4,6},{5,7},{6,4},{7,5},{8,10},{9,11},{10,... | collective-permute-start | bytes 811016 | tf_op jit(solution)/shard_map/ppermute | solution.py:277
  23.5 7.1 %collective-permute-start.5 = (bf16[4,4,16,256]{3,2,1,0:T(8,128)(2,1)S(1)}, bf16[4,4,16,256]{3,2,1,0:T(8,128)(2,1)S(1)}, u32[]{:S(2)}, u32[]{:S(2)}) collective-permute-start(bf16[4,4,16,256]{3,2,1,0:T(8,128)(2,1)S(1)} %pad_maximum_fusion.refs_0_), channel_id=1, source_target_pairs={{0,12},{1,13},{2,14},{3,15},{4,8},{5,9},{6,10},{7,11},{8,4},{9,5},... | collective-permute-start | bytes 393224 | tf_op jit(solution)/shard_map/ppermute | solution.py:277
  30.5 5.6 %collective-permute-start.12 = (bf16[1,528,128]{2,1,0:T(8,128)(2,1)S(1)}, bf16[1,528,128]{2,1,0:T(8,128)(2,1)S(1)}, u32[]{:S(2)}, u32[]{:S(2)}) collective-permute-start(bf16[1,528,128]{2,1,0:T(8,128)(2,1)S(1)} %get-tuple-element.43), channel_id=1, source_target_pairs={{0,2},{1,3},{2,0},{3,1},{4,6},{5,7},{6,4},{7,5},{8,10},{9,11},{10,... | collective-permute-start | bytes 405512 | tf_op jit(solution)/shard_map/ppermute | solution.py:277
  32.1 6.9 %collective-permute-start.13 = (bf16[1,528,128]{2,1,0:T(8,128)(2,1)S(1)}, bf16[1,528,128]{2,1,0:T(8,128)(2,1)S(1)}, u32[]{:S(2)}, u32[]{:S(2)}) collective-permute-start(bf16[1,528,128]{2,1,0:T(8,128)(2,1)S(1)} %get-tuple-element.44), channel_id=1, source_target_pairs={{0,3},{1,2},{2,1},{3,0},{4,7},{5,6},{6,5},{7,4},{8,11},{9,10},{10,... | collective-permute-start | bytes 405512 | tf_op jit(solution)/shard_map/ppermute | solution.py:277
  32.1 9.6 %collective-permute-start.7 = (bf16[1,528,128]{2,1,0:T(8,128)(2,1)S(1)}, bf16[1,528,128]{2,1,0:T(8,128)(2,1)S(1)}, u32[]{:S(2)}, u32[]{:S(2)}) collective-permute-start(bf16[1,528,128]{2,1,0:T(8,128)(2,1)S(1)} %get-tuple-element.39), channel_id=1, source_target_pairs={{0,2},{1,3},{2,0},{3,1},{4,6},{5,7},{6,4},{7,5},{8,10},{9,11},{10,... | collective-permute-start | bytes 405512 | tf_op jit(solution)/shard_map/ppermute | solution.py:277
  33.3 11.2 %collective-permute-start.8 = (bf16[1,528,128]{2,1,0:T(8,128)(2,1)S(1)}, bf16[1,528,128]{2,1,0:T(8,128)(2,1)S(1)}, u32[]{:S(2)}, u32[]{:S(2)}) collective-permute-start(bf16[1,528,128]{2,1,0:T(8,128)(2,1)S(1)} %get-tuple-element.40), channel_id=1, source_target_pairs={{0,3},{1,2},{2,1},{3,0},{4,7},{5,6},{6,5},{7,4},{8,11},{9,10},{10,... | collective-permute-start | bytes 405512 | tf_op jit(solution)/shard_map/ppermute | solution.py:277
  36.1 9.7 %collective-permute-start.15 = (bf16[272,256]{1,0:T(8,128)(2,1)S(1)}, bf16[272,256]{1,0:T(8,128)(2,1)S(1)}, u32[]{:S(2)}, u32[]{:S(2)}) collective-permute-start(bf16[272,256]{1,0:T(8,128)(2,1)S(1)} %shard_map.67), channel_id=1, source_target_pairs={{0,12},{1,13},{2,14},{3,15},{4,8},{5,9},{6,10},{7,11},{8,4},{9,5},... | collective-permute-start | bytes 417800 | tf_op jit(solution)/shard_map/ppermute | solution.py:277
  40.2 10.8 %collective-permute-start.14 = (bf16[272,256]{1,0:T(8,128)(2,1)S(1)}, bf16[272,256]{1,0:T(8,128)(2,1)S(1)}, u32[]{:S(2)}, u32[]{:S(2)}) collective-permute-start(bf16[272,256]{1,0:T(8,128)(2,1)S(1)} %shard_map.66), channel_id=1, source_target_pairs={{0,8},{1,9},{2,10},{3,11},{4,12},{5,13},{6,14},{7,15},{8,0},{9,1},... | collective-permute-start | bytes 417800 | tf_op jit(solution)/shard_map/ppermute | solution.py:277
  41.8 9.3 %collective-permute-start.11 = (bf16[272,256]{1,0:T(8,128)(2,1)S(1)}, bf16[272,256]{1,0:T(8,128)(2,1)S(1)}, u32[]{:S(2)}, u32[]{:S(2)}) collective-permute-start(bf16[272,256]{1,0:T(8,128)(2,1)S(1)} %shard_map.65), channel_id=1, source_target_pairs={{0,4},{1,5},{2,6},{3,7},{4,0},{5,1},{6,2},{7,3},{8,12},{9,13},{10,... | collective-permute-start | bytes 417800 | tf_op jit(solution)/shard_map/ppermute | solution.py:277
  53.9 7.1 %collective-permute-start.27 = (bf16[32,2176]{1,0:T(8,128)(2,1)S(1)}, bf16[32,2176]{1,0:T(8,128)(2,1)S(1)}, u32[]{:S(2)}, u32[]{:S(2)}) collective-permute-start(bf16[32,2176]{1,0:T(8,128)(2,1)S(1)} %get-tuple-element.58), channel_id=1, source_target_pairs={{0,2},{1,3},{2,0},{3,1},{4,6},{5,7},{6,4},{7,5},{8,10},{9,11},{10,... | collective-permute-start | bytes 417800 | tf_op jit(solution)/shard_map/ppermute | solution.py:277
  56.4 7.5 %collective-permute-start.25 = (bf16[32,2176]{1,0:T(8,128)(2,1)S(1)}, bf16[32,2176]{1,0:T(8,128)(2,1)S(1)}, u32[]{:S(2)}, u32[]{:S(2)}) collective-permute-start(bf16[32,2176]{1,0:T(8,128)(2,1)S(1)} %get-tuple-element.56), channel_id=1, source_target_pairs={{0,2},{1,3},{2,0},{3,1},{4,6},{5,7},{6,4},{7,5},{8,10},{9,11},{10,... | collective-permute-start | bytes 417800 | tf_op jit(solution)/shard_map/ppermute | solution.py:277
  56.5 10.4 %collective-permute-start.23 = (bf16[32,2176]{1,0:T(8,128)(2,1)S(1)}, bf16[32,2176]{1,0:T(8,128)(2,1)S(1)}, u32[]{:S(2)}, u32[]{:S(2)}) collective-permute-start(bf16[32,2176]{1,0:T(8,128)(2,1)S(1)} %get-tuple-element.54), channel_id=1, source_target_pairs={{0,2},{1,3},{2,0},{3,1},{4,6},{5,7},{6,4},{7,5},{8,10},{9,11},{10,... | collective-permute-start | bytes 417800 | tf_op jit(solution)/shard_map/ppermute | solution.py:277
  58.5 8.5 %collective-permute-start.18 = (bf16[64,512]{1,0:T(8,128)(2,1)S(1)}, bf16[64,512]{1,0:T(8,128)(2,1)S(1)}, u32[]{:S(2)}, u32[]{:S(2)}) collective-permute-start(bf16[64,512]{1,0:T(8,128)(2,1)S(1)} %get-tuple-element.46), channel_id=1, source_target_pairs={{0,12},{1,13},{2,14},{3,15},{4,8},{5,9},{6,10},{7,11},{8,4},{9,5},... | collective-permute-start | bytes 196616 | tf_op jit(solution)/shard_map/ppermute | solution.py:277
  60.0 9.2 %collective-permute-start.19 = (bf16[64,512]{1,0:T(8,128)(2,1)S(1)}, bf16[64,512]{1,0:T(8,128)(2,1)S(1)}, u32[]{:S(2)}, u32[]{:S(2)}) collective-permute-start(bf16[64,512]{1,0:T(8,128)(2,1)S(1)} %get-tuple-element.47), channel_id=1, source_target_pairs={{0,4},{1,5},{2,6},{3,7},{4,0},{5,1},{6,2},{7,3},{8,12},{9,13},{10,... | collective-permute-start | bytes 196616 | tf_op jit(solution)/shard_map/ppermute | solution.py:277
  61.0 23.3 %collective-permute-start.22 = (bf16[32,2176]{1,0:T(8,128)(2,1)S(1)}, bf16[32,2176]{1,0:T(8,128)(2,1)S(1)}, u32[]{:S(2)}, u32[]{:S(2)}) collective-permute-start(bf16[32,2176]{1,0:T(8,128)(2,1)S(1)} %get-tuple-element.52), channel_id=1, source_target_pairs={{0,2},{1,3},{2,0},{3,1},{4,6},{5,7},{6,4},{7,5},{8,10},{9,11},{10,... | collective-permute-start | bytes 417800 | tf_op jit(solution)/shard_map/ppermute | solution.py:277
  64.0 20.3 %collective-permute-start.28 = (bf16[32,2176]{1,0:T(8,128)(2,1)S(1)}, bf16[32,2176]{1,0:T(8,128)(2,1)S(1)}, u32[]{:S(2)}, u32[]{:S(2)}) collective-permute-start(bf16[32,2176]{1,0:T(8,128)(2,1)S(1)} %shard_map.74), channel_id=1, source_target_pairs={{0,8},{1,9},{2,10},{3,11},{4,12},{5,13},{6,14},{7,15},{8,0},{9,1},... | collective-permute-start | bytes 417800 | tf_op jit(solution)/shard_map/ppermute | solution.py:277
  66.9 17.4 %collective-permute-start.26 = (bf16[32,2176]{1,0:T(8,128)(2,1)S(1)}, bf16[32,2176]{1,0:T(8,128)(2,1)S(1)}, u32[]{:S(2)}, u32[]{:S(2)}) collective-permute-start(bf16[32,2176]{1,0:T(8,128)(2,1)S(1)} %shard_map.73), channel_id=1, source_target_pairs={{0,4},{1,5},{2,6},{3,7},{4,0},{5,1},{6,2},{7,3},{8,12},{9,13},{10,... | collective-permute-start | bytes 417800 | tf_op jit(solution)/shard_map/ppermute | solution.py:277
  67.0 17.3 %collective-permute-start.24 = (bf16[32,2176]{1,0:T(8,128)(2,1)S(1)}, bf16[32,2176]{1,0:T(8,128)(2,1)S(1)}, u32[]{:S(2)}, u32[]{:S(2)}) collective-permute-start(bf16[32,2176]{1,0:T(8,128)(2,1)S(1)} %shard_map.72), channel_id=1, source_target_pairs={{0,12},{1,13},{2,14},{3,15},{4,8},{5,9},{6,10},{7,11},{8,4},{9,5},... | collective-permute-start | bytes 417800 | tf_op jit(solution)/shard_map/ppermute | solution.py:277
  69.1 11.1 %collective-permute-start.20 = (bf16[64,512]{1,0:T(8,128)(2,1)S(1)}, bf16[64,512]{1,0:T(8,128)(2,1)S(1)}, u32[]{:S(2)}, u32[]{:S(2)}) collective-permute-start(bf16[64,512]{1,0:T(8,128)(2,1)S(1)} %get-tuple-element.48), channel_id=1, source_target_pairs={{0,8},{1,9},{2,10},{3,11},{4,12},{5,13},{6,14},{7,15},{8,0},{9,1},... | collective-permute-start | bytes 196616 | tf_op jit(solution)/shard_map/ppermute | solution.py:277
  (8 other events, 32.9 us)

commit v8 on v7

--- a/solution.py
+++ b/solution.py
@@ -12,7 +12,7 @@
 KEY_VALUE_HEADS = 16
 HEAD_SIZE = 128
 INNER = 4
-EARLY_PART = 20
+EARLY_PART = 24
 
 score_scale = 168.0 ** (-0.5)
 masked_value = -1e30
@@ -186,39 +186,42 @@
     y = lax.shift_right_logical(r, 1)
     half = w_other_ref.shape[1]
     sends, keeps, earlies = out_refs[:outer], out_refs[outer:2 * outer], out_refs[2 * outer:]
-
-    def gather(ref, first, size):
+    span = 2 * rows
+    far = [kk for kk in order if kk >= outer // 2]
+
+    def gather(picks):
         found = []
-        for kk in order:
-            at = (lax.bitwise_xor(z, kk) * INNER + first) * rows
-            found.append(ref[pl.ds(pl.multiple_of(at, size), size), :])
+        for ref in (mine_ref, other_ref):
+            lines = []
+            for kk, first, size in picks:
+                at = (lax.bitwise_xor(z, kk) * INNER + first) * rows
+                lines.append(ref[pl.ds(pl.multiple_of(at, size), size), :])
+            found.append(jnp.concatenate(lines, axis=0))
         return found
 
-    def terms(mine, other, begin, cols):
+    def terms(lines, begin, cols):
         col = pl.multiple_of(lax.bitwise_and(r, 1) * half + begin, 128)
-        term = jnp.dot(mine, w_mine_ref[:, pl.ds(col, cols)], preferred_element_type=f32)
+        term = jnp.dot(lines[0], w_mine_ref[:, pl.ds(col, cols)], preferred_element_type=f32)
         return term + jnp.dot(
-            other, w_other_ref[:, begin:begin + cols], preferred_element_type=f32
+            lines[1], w_other_ref[:, begin:begin + cols], preferred_element_type=f32
         )
 
-    def store(term, outs, here):
-        for i, out in enumerate(outs):
-            size = out.shape[0]
-            out[:, here] = term[i * size:(i + 1) * size].astype(out.dtype)
-
-    span = 2 * rows
-    lines = [
-        jnp.concatenate(gather(ref, 2 * (1 - y), span) + gather(ref, 2 * y, span), axis=0)
-        for ref in (mine_ref, other_ref)
-    ]
+    sides = [(2 * (1 - y), sends), (2 * y, keeps)]
+    lines = gather([(kk, first, span) for first, outs in sides for kk in order])
     cols = (half - early) // blocks
     for j in range(blocks):
-        term = terms(*lines, early + j * cols, cols)
-        store(term, sends + keeps, slice(j * cols, (j + 1) * cols))
-    lines = [
-        jnp.concatenate(gather(ref, 0, INNER * rows), axis=0) for ref in (mine_ref, other_ref)
-    ]
-    store(terms(*lines, 0, early), earlies, slice(0, early))
+        term = terms(lines, early + j * cols, cols)
+        for i, out in enumerate(sends + keeps):
+            at = j * cols + out.shape[1] - (half - early)
+            out[:, at:at + cols] = term[i * span:(i + 1) * span].astype(out.dtype)
+    near = [(kk, first, outs[i]) for first, outs in sides for i, kk in enumerate(order)
+            if kk not in far]
+    picks = [(kk, 0, 2 * span) for kk in far] + [(kk, first, span) for kk, first, out in near]
+    term = terms(gather(picks), 0, early)
+    at = 0
+    for out in list(earlies) + [out for kk, first, out in near]:
+        out[:, 0:early] = term[at:at + out.shape[0]].astype(out.dtype)
+        at += out.shape[0]
 
 
 def first_sum_kernel(keep_ref, got_ref, out_ref):
@@ -239,10 +242,16 @@
     _, _, r = place()
     c = lax.bitwise_and(r, 1)
     early = early_keep_ref.shape[1]
-    total_ref[:, :early] = early_keep_ref[...] + early_got_ref[...].astype(f32)
+    half = keep_ref.shape[1]
     total = keep_ref[...] + got_ref[...].astype(f32)
     for part in parts:
-        total = total + part[...].astype(f32)
+        if part.shape[1] == half:
+            total = total + part[...].astype(f32)
+    total_ref[:, :early] = total[:, :early] + early_keep_ref[...] + early_got_ref[...].astype(f32)
+    total = total[:, early:]
+    for part in parts:
+        if part.shape[1] != half:
+            total = total + part[...].astype(f32)
     total_ref[:, early:] = total
     mine_ref[...] = total_ref[pl.ds(pl.multiple_of(c * rows, rows), rows), :].astype(bf16)
     other_ref[...] = total_ref[pl.ds(pl.multiple_of((1 - c) * rows, rows), rows), :].astype(bf16)
@@ -270,7 +279,7 @@
     assert heads * copies == QUERY_HEADS // KEY_VALUE_HEADS and keys <= 256
     tiles = half // 128
     early = 128 * (tiles * EARLY_PART // 100)
-    blocks = 2 if (half - early) % 256 == 0 else 1
+    blocks = next(b for b in (2, 3, 1) if (half - early) % (128 * b) == 0)
     shape = jax.ShapeDtypeStruct
 
     def swap(x, k):
@@ -335,26 +344,30 @@
     other = swap(merged, 1)
 
     span = 2 * rows
-    main = half - early
+    far = [kk for kk in order if kk >= outer // 2]
+    widths = [half - early if kk in far else half for kk in order]
     terms = call(
         functools.partial(
             project_kernel, order=order, outer=outer, rows=rows, early=early, blocks=blocks
         ),
         [merged, other, out_weight, w_other],
-        [shape((span, main), bf16)] * outer + [shape((span, main), f32)] * outer
-        + [shape((2 * span, early), bf16)] * (outer - 1) + [shape((2 * span, early), f32)],
+        [shape((span, w), bf16) for w in widths] + [shape((span, w), f32) for w in widths]
+        + [shape((2 * span, early), bf16)] * len(far),
         flops=4 * rows_all * width * half, limit=20,
     )
     sends, keeps, earlies = terms[:outer], terms[outer:2 * outer], terms[2 * outer:]
     gots = [swap(x, 2) for x in sends]
-    early_gots = [swap(x, kk * INNER) for kk, x in zip(order[:-1], earlies)]
+    early_gots = [swap(x, kk * INNER) for kk, x in zip(far, earlies)]
     parts = []
     for i, kk in enumerate(order[:-1]):
-        (part,) = call(first_sum_kernel, [keeps[i], gots[i]], [shape((span, main), bf16)])
+        (part,) = call(
+            first_sum_kernel, [keeps[i], gots[i]],
+            [shape((span, widths[i]), bf16)],
+        )
         parts.append(swap(part, kk * INNER))
     early_send, early_keep = call(
         functools.partial(early_sum_kernel, span=span),
-        [earlies[-1]] + early_gots, [shape((span, early), bf16), shape((span, early), f32)],
+        early_gots, [shape((span, early), bf16), shape((span, early), f32)],
         scratch=[pltpu.VMEM((2 * span, early), f32)],
     )
     mine, theirs = call(

time: 86.7 us -> 87.9 us (1.014)
  waiting for transfers between devices: 40.4 us -> 44.4 us
  starting transfers between devices: 33.2 us -> 30.5 us
    ppermute x30 -> x29, waiting for transfers between devices: 40.4 us -> 44.4 us  [swap(): return lax.ppermute(x, 'seq', [(i, i ^ k) for i in range(devices)])]
    ppermute x30 -> x29, starting transfers between devices: 33.2 us -> 30.5 us  [swap(): return lax.ppermute(x, 'seq', [(i, i ^ k) for i in range(devices)])]
  transfers between devices with their start and end apart: 30 -> 29, of which waited for: 16 -> 16; matrix products, arithmetic and copies ran while one was open for 0% -> 0% of each run, Pallas kernels for 9% -> 9%
where the time goes in v8:
time: 87.9 us; the launch traced here: 87.7 us
  waiting for transfers between devices  44.4 us (51%)
  starting transfers between devices  30.5 us (35%)
  Pallas kernels  9.55 us (11%)
  local copies, waits for them, and re-layouts  1.78 us (2%)
  between operations  1.45 us (2%)
    ppermute x29, waiting for transfers between devices, swap(): return lax.ppermute(x, 'seq', [(i, i ^ k) for i in range(devices)])  44.4 us
    ppermute x29, starting transfers between devices, swap(): return lax.ppermute(x, 'seq', [(i, i ^ k) for i in range(devices)])  30.5 us
    pallas_call x13, Pallas kernels, call(): pl.pallas_call(kernel, out_shape=tuple(outs), in_specs=in_specs, out_spec...  7.34 us
    pallas_call x1, Pallas kernels, layer(): pl.pallas_call(functools.partial(split_kernel, outer=outer, width=width,...  2.21 us
    unnamed x4, local copies, waits for them, and re-layouts  1.78 us
  transfers between devices with their start and end apart: 29, of which 16 were waited for; matrix products, arithmetic and copies ran while one was open for 0% of the time, Pallas kernels for 9%

profile of v8, /device:TPU:0, one launch (start us, length us, event | category | flops | bytes accessed | tf_op | source)
XLA Modules:
  0.0 87.7 jit_solution(5318646562846633892)
XLA Ops:
  0.0 1.8 %copy-done = bf16[256,5376]{1,0:T(8,128)(2,1)S(1)} copy-done((bf16[256,5376]{1,0:T(8,128)(2,1)S(1)}, bf16[256,5376]{1,0:T(8,128)(2,1)}, u32[]{:S(2)}) %copy-start) | copy-done | bytes 2752536
  3.1 2.2 %split.1 = (bf16[4,16,256]{2,1,0:T(8,128)(2,1)S(1)}, bf16[4,16,256]{2,1,0:T(8,128)(2,1)S(1)}, bf16[4,16,256]{2,1,0:T(8,128)(2,1)S(1)}, bf16[4,16,256]{2,1,0:T(8,...) custom-call(s32[1]{0:T(128)S(6)} %copy.7.live_ref, ...), custom_call_target="tpu_custom_call" | custom-call | tf_op jit(solution)/shard_map/split/pallas_call | solution.py:297
  5.4 3.0 %collective-permute-start.1 = (bf16[4,16,256]{2,1,0:T(8,128)(2,1)S(1)}, bf16[4,16,256]{2,1,0:T(8,128)(2,1)S(1)}, u32[]{:S(2)}, u32[]{:S(2)}) collective-permute-start(bf16[4,16,256]{2,1,0:T(8,128)(2,1)S(1)} %get-tuple-element.33), channel_id=1, source_target_pairs={{0,2},{1,3},{2,0},{3,1},{4,6},{5,7},{6,4},{7,5},{8,10},{9,11},{10,... | collective-permute-start | bytes 98312 | tf_op jit(solution)/shard_map/ppermute | solution.py:286
  8.5 1.8 %collective-permute-done.1 = bf16[4,16,256]{2,1,0:T(8,128)(2,1)S(1)} collective-permute-done((bf16[4,16,256]{2,1,0:T(8,128)(2,1)S(1)}, bf16[4,16,256]{2,1,0:T(8,128)(2,1)S(1)}, u32[]{:S(2)}, u32[]{:S(2)}) %collective-permute-start.1) | collective-permute-done | bytes 32800 | tf_op jit(solution)/shard_map/ppermute | solution.py:286
  10.3 1.8 %collective-permute-done.2 = bf16[4,16,256]{2,1,0:T(8,128)(2,1)S(1)} collective-permute-done((bf16[4,16,256]{2,1,0:T(8,128)(2,1)S(1)}, bf16[4,16,256]{2,1,0:T(8,128)(2,1)S(1)}, u32[]{:S(2)}, u32[]{:S(2)}) %collective-permute-start.2) | collective-permute-done | bytes 32800 | tf_op jit(solution)/shard_map/ppermute | solution.py:286
  12.1 1.6 %collective-permute-start.3 = (bf16[4,4,16,256]{3,2,1,0:T(8,128)(2,1)S(1)}, bf16[4,4,16,256]{3,2,1,0:T(8,128)(2,1)S(1)}, u32[]{:S(2)}, u32[]{:S(2)}) collective-permute-start(bf16[4,4,16,256]{3,2,1,0:T(8,128)(2,1)S(1)} %pad_maximum_fusion.refs_0_), channel_id=1, source_target_pairs={{0,4},{1,5},{2,6},{3,7},{4,0},{5,1},{6,2},{7,3},{8,12},{9,13},{10,... | collective-permute-start | bytes 393224 | tf_op jit(solution)/shard_map/ppermute | solution.py:286
  13.7 2.6 %collective-permute-start.4 = (bf16[4,4,16,256]{3,2,1,0:T(8,128)(2,1)S(1)}, bf16[4,4,16,256]{3,2,1,0:T(8,128)(2,1)S(1)}, u32[]{:S(2)}, u32[]{:S(2)}) collective-permute-start(bf16[4,4,16,256]{3,2,1,0:T(8,128)(2,1)S(1)} %pad_maximum_fusion.refs_0_), channel_id=1, source_target_pairs={{0,8},{1,9},{2,10},{3,11},{4,12},{5,13},{6,14},{7,15},{8,0},{9,1},... | collective-permute-start | bytes 393224 | tf_op jit(solution)/shard_map/ppermute | solution.py:286
  18.1 5.4 %collective-permute-done.4.refs_2_ = bf16[4,4,16,256]{3,2,1,0:T(8,128)(2,1)S(1)} collective-permute-done((bf16[4,4,16,256]{3,2,1,0:T(8,128)(2,1)S(1)}, bf16[4,4,16,256]{3,2,1,0:T(8,128)(2,1)S(1)}, u32[]{:S(2)}, u32[]{:S(2)}) %collective-permute-start.4) | collective-permute-done | bytes 131104 | tf_op jit(solution)/shard_map/ppermute | solution.py:286
  23.5 2.5 %collective-permute-start.5 = (bf16[4,4,16,256]{3,2,1,0:T(8,128)(2,1)S(1)}, bf16[4,4,16,256]{3,2,1,0:T(8,128)(2,1)S(1)}, u32[]{:S(2)}, u32[]{:S(2)}) collective-permute-start(bf16[4,4,16,256]{3,2,1,0:T(8,128)(2,1)S(1)} %pad_maximum_fusion.refs_0_), channel_id=1, source_target_pairs={{0,12},{1,13},{2,14},{3,15},{4,8},{5,9},{6,10},{7,11},{8,4},{9,5},... | collective-permute-start | bytes 393224 | tf_op jit(solution)/shard_map/ppermute | solution.py:286
  26.0 4.5 %collective-permute-done.5.refs_3_ = bf16[4,4,16,256]{3,2,1,0:T(8,128)(2,1)S(1)} collective-permute-done((bf16[4,4,16,256]{3,2,1,0:T(8,128)(2,1)S(1)}, bf16[4,4,16,256]{3,2,1,0:T(8,128)(2,1)S(1)}, u32[]{:S(2)}, u32[]{:S(2)}) %collective-permute-start.5) | collective-permute-done | bytes 131104 | tf_op jit(solution)/shard_map/ppermute | solution.py:286
  30.5 1.6 %collective-permute-start.12 = (bf16[1,528,128]{2,1,0:T(8,128)(2,1)S(1)}, bf16[1,528,128]{2,1,0:T(8,128)(2,1)S(1)}, u32[]{:S(2)}, u32[]{:S(2)}) collective-permute-start(bf16[1,528,128]{2,1,0:T(8,128)(2,1)S(1)} %get-tuple-element.41), channel_id=1, source_target_pairs={{0,2},{1,3},{2,0},{3,1},{4,6},{5,7},{6,4},{7,5},{8,10},{9,11},{10,... | collective-permute-start | bytes 405512 | tf_op jit(solution)/shard_map/ppermute | solution.py:286
  33.3 1.5 %collective-permute-start.8 = (bf16[1,528,128]{2,1,0:T(8,128)(2,1)S(1)}, bf16[1,528,128]{2,1,0:T(8,128)(2,1)S(1)}, u32[]{:S(2)}, u32[]{:S(2)}) collective-permute-start(bf16[1,528,128]{2,1,0:T(8,128)(2,1)S(1)} %get-tuple-element.38), channel_id=1, source_target_pairs={{0,3},{1,2},{2,1},{3,0},{4,7},{5,6},{6,5},{7,4},{8,11},{9,10},{10,... | collective-permute-start | bytes 405512 | tf_op jit(solution)/shard_map/ppermute | solution.py:286
  36.1 2.4 %collective-permute-start.15 = (bf16[272,256]{1,0:T(8,128)(2,1)S(1)}, bf16[272,256]{1,0:T(8,128)(2,1)S(1)}, u32[]{:S(2)}, u32[]{:S(2)}) collective-permute-start(bf16[272,256]{1,0:T(8,128)(2,1)S(1)} %shard_map.67), channel_id=1, source_target_pairs={{0,12},{1,13},{2,14},{3,15},{4,8},{5,9},{6,10},{7,11},{8,4},{9,5},... | collective-permute-start | bytes 417800 | tf_op jit(solution)/shard_map/ppermute | solution.py:286
  41.8 2.7 %collective-permute-start.11 = (bf16[272,256]{1,0:T(8,128)(2,1)S(1)}, bf16[272,256]{1,0:T(8,128)(2,1)S(1)}, u32[]{:S(2)}, u32[]{:S(2)}) collective-permute-start(bf16[272,256]{1,0:T(8,128)(2,1)S(1)} %shard_map.65), channel_id=1, source_target_pairs={{0,4},{1,5},{2,6},{3,7},{4,0},{5,1},{6,2},{7,3},{8,12},{9,13},{10,... | collective-permute-start | bytes 417800 | tf_op jit(solution)/shard_map/ppermute | solution.py:286
  45.8 5.3 %collective-permute-done.14.refs_2_ = bf16[272,256]{1,0:T(8,128)(2,1)S(1)} collective-permute-done((bf16[272,256]{1,0:T(8,128)(2,1)S(1)}, bf16[272,256]{1,0:T(8,128)(2,1)S(1)}, u32[]{:S(2)}, u32[]{:S(2)}) %collective-permute-start.14) | collective-permute-done | bytes 139296 | tf_op jit(solution)/shard_map/ppermute | solution.py:286
  53.9 2.6 %collective-permute-start.24 = (bf16[32,2688]{1,0:T(8,128)(2,1)S(1)}, bf16[32,2688]{1,0:T(8,128)(2,1)S(1)}, u32[]{:S(2)}, u32[]{:S(2)}) collective-permute-start(bf16[32,2688]{1,0:T(8,128)(2,1)S(1)} %get-tuple-element.52), channel_id=1, source_target_pairs={{0,2},{1,3},{2,0},{3,1},{4,6},{5,7},{6,4},{7,5},{8,10},{9,11},{10,... | collective-permute-start | bytes 516104 | tf_op jit(solution)/shard_map/ppermute | solution.py:286
  56.5 1.9 %collective-permute-start.22 = (bf16[32,2048]{1,0:T(8,128)(2,1)S(1)}, bf16[32,2048]{1,0:T(8,128)(2,1)S(1)}, u32[]{:S(2)}, u32[]{:S(2)}) collective-permute-start(bf16[32,2048]{1,0:T(8,128)(2,1)S(1)} %get-tuple-element.50), channel_id=1, source_target_pairs={{0,2},{1,3},{2,0},{3,1},{4,6},{5,7},{6,4},{7,5},{8,10},{9,11},{10,... | collective-permute-start | bytes 393224 | tf_op jit(solution)/shard_map/ppermute | solution.py:286
  58.5 1.5 %collective-permute-start.18 = (bf16[64,640]{1,0:T(8,128)(2,1)S(1)}, bf16[64,640]{1,0:T(8,128)(2,1)S(1)}, u32[]{:S(2)}, u32[]{:S(2)}) collective-permute-start(bf16[64,640]{1,0:T(8,128)(2,1)S(1)} %get-tuple-element.43), channel_id=1, source_target_pairs={{0,12},{1,13},{2,14},{3,15},{4,8},{5,9},{6,10},{7,11},{8,4},{9,5},... | collective-permute-start | bytes 245768 | tf_op jit(solution)/shard_map/ppermute | solution.py:286
  61.8 2.7 %collective-permute-done.26.got_ref = bf16[32,2048]{1,0:T(8,128)(2,1)S(1)} collective-permute-done((bf16[32,2048]{1,0:T(8,128)(2,1)S(1)}, bf16[32,2048]{1,0:T(8,128)(2,1)S(1)}, u32[]{:S(2)}, u32[]{:S(2)}) %collective-permute-start.26) | collective-permute-done | bytes 131104 | tf_op jit(solution)/shard_map/ppermute | solution.py:286
  64.7 2.6 %collective-permute-done.22.got_ref = bf16[32,2048]{1,0:T(8,128)(2,1)S(1)} collective-permute-done((bf16[32,2048]{1,0:T(8,128)(2,1)S(1)}, bf16[32,2048]{1,0:T(8,128)(2,1)S(1)}, u32[]{:S(2)}, u32[]{:S(2)}) %collective-permute-start.22) | collective-permute-done | bytes 131104 | tf_op jit(solution)/shard_map/ppermute | solution.py:286
  67.3 2.1 %collective-permute-start.23 = (bf16[32,2048]{1,0:T(8,128)(2,1)S(1)}, bf16[32,2048]{1,0:T(8,128)(2,1)S(1)}, u32[]{:S(2)}, u32[]{:S(2)}) collective-permute-start(bf16[32,2048]{1,0:T(8,128)(2,1)S(1)} %shard_map.72), channel_id=1, source_target_pairs={{0,12},{1,13},{2,14},{3,15},{4,8},{5,9},{6,10},{7,11},{8,4},{9,5},... | collective-permute-start | bytes 393224 | tf_op jit(solution)/shard_map/ppermute | solution.py:286
  69.5 11.9 %collective-permute-done.19.refs_1_ = bf16[64,640]{1,0:T(8,128)(2,1)S(1)} collective-permute-done((bf16[64,640]{1,0:T(8,128)(2,1)S(1)}, bf16[64,640]{1,0:T(8,128)(2,1)S(1)}, u32[]{:S(2)}, u32[]{:S(2)}) %collective-permute-start.19) | collective-permute-done | bytes 81952 | tf_op jit(solution)/shard_map/ppermute | solution.py:286
  81.4 1.5 %collective-permute-start.20 = (bf16[32,640]{1,0:T(8,128)(2,1)S(1)}, bf16[32,640]{1,0:T(8,128)(2,1)S(1)}, u32[]{:S(2)}, u32[]{:S(2)}) collective-permute-start(bf16[32,640]{1,0:T(8,128)(2,1)S(1)} %get-tuple-element.46), channel_id=1, source_target_pairs={{0,2},{1,3},{2,0},{3,1},{4,6},{5,7},{6,4},{7,5},{8,10},{9,11},{10,... | collective-permute-start | bytes 122888 | tf_op jit(solution)/shard_map/ppermute | solution.py:286
  82.9 2.6 %collective-permute-done.20.early_got_ref = bf16[32,640]{1,0:T(8,128)(2,1)S(1)} collective-permute-done((bf16[32,640]{1,0:T(8,128)(2,1)S(1)}, bf16[32,640]{1,0:T(8,128)(2,1)S(1)}, u32[]{:S(2)}, u32[]{:S(2)}) %collective-permute-start.20) | collective-permute-done | bytes 40992 | tf_op jit(solution)/shard_map/ppermute | solution.py:286
  (53 shorter events, 16.2 us)
Async XLA Ops:
  1.9 51.1 %collective-permute-start.17 = (bf16[256,2688]{1,0:T(8,128)(2,1)S(1)}, bf16[256,2688]{1,0:T(8,128)(2,1)S(1)}, u32[]{:S(2)}, u32[]{:S(2)}) collective-permute-start(bf16[256,2688]{1,0:T(8,128)(2,1)S(1)} %shard_map.69), channel_id=1, source_target_pairs={{0,1},{1,0},{2,3},{3,2},{4,5},{5,4},{6,7},{7,6},{8,9},{9,8},{10,11... | collective-permute-start | bytes 4128776 | tf_op jit(solution)/shard_map/ppermute | solution.py:286
  5.4 4.9 %collective-permute-start.1 = (bf16[4,16,256]{2,1,0:T(8,128)(2,1)S(1)}, bf16[4,16,256]{2,1,0:T(8,128)(2,1)S(1)}, u32[]{:S(2)}, u32[]{:S(2)}) collective-permute-start(bf16[4,16,256]{2,1,0:T(8,128)(2,1)S(1)} %get-tuple-element.33), channel_id=1, source_target_pairs={{0,2},{1,3},{2,0},{3,1},{4,6},{5,7},{6,4},{7,5},{8,10},{9,11},{10,... | collective-permute-start | bytes 98312 | tf_op jit(solution)/shard_map/ppermute | solution.py:286
  8.4 24.9 %collective-permute-start.6 = (bf16[4,528,128]{2,1,0:T(8,128)(2,1)S(1)}, bf16[4,528,128]{2,1,0:T(8,128)(2,1)S(1)}, u32[]{:S(2)}, u32[]{:S(2)}) collective-permute-start(bf16[4,528,128]{2,1,0:T(8,128)(2,1)S(1)} %get-tuple-element.36), channel_id=1, source_target_pairs={{0,1},{1,0},{2,3},{3,2},{4,5},{5,4},{6,7},{7,6},{8,9},{9,8},{10,11... | collective-permute-start | bytes 1622024 | tf_op jit(solution)/shard_map/ppermute | solution.py:286
  12.1 5.6 %collective-permute-start.3 = (bf16[4,4,16,256]{3,2,1,0:T(8,128)(2,1)S(1)}, bf16[4,4,16,256]{3,2,1,0:T(8,128)(2,1)S(1)}, u32[]{:S(2)}, u32[]{:S(2)}) collective-permute-start(bf16[4,4,16,256]{3,2,1,0:T(8,128)(2,1)S(1)} %pad_maximum_fusion.refs_0_), channel_id=1, source_target_pairs={{0,4},{1,5},{2,6},{3,7},{4,0},{5,1},{6,2},{7,3},{8,12},{9,13},{10,... | collective-permute-start | bytes 393224 | tf_op jit(solution)/shard_map/ppermute | solution.py:286
  13.7 18.4 %collective-permute-start.10 = (bf16[2,528,128]{2,1,0:T(8,128)(2,1)S(1)}, bf16[2,528,128]{2,1,0:T(8,128)(2,1)S(1)}, u32[]{:S(2)}, u32[]{:S(2)}) collective-permute-start(bf16[2,528,128]{2,1,0:T(8,128)(2,1)S(1)} %get-tuple-element.40), channel_id=1, source_target_pairs={{0,3},{1,2},{2,1},{3,0},{4,7},{5,6},{6,5},{7,4},{8,11},{9,10},{10,... | collective-permute-start | bytes 811016 | tf_op jit(solution)/shard_map/ppermute | solution.py:286
  13.7 9.7 %collective-permute-start.4 = (bf16[4,4,16,256]{3,2,1,0:T(8,128)(2,1)S(1)}, bf16[4,4,16,256]{3,2,1,0:T(8,128)(2,1)S(1)}, u32[]{:S(2)}, u32[]{:S(2)}) collective-permute-start(bf16[4,4,16,256]{3,2,1,0:T(8,128)(2,1)S(1)} %pad_maximum_fusion.refs_0_), channel_id=1, source_target_pairs={{0,8},{1,9},{2,10},{3,11},{4,12},{5,13},{6,14},{7,15},{8,0},{9,1},... | collective-permute-start | bytes 393224 | tf_op jit(solution)/shard_map/ppermute | solution.py:286
  17.6 14.5 %collective-permute-start.9 = (bf16[2,528,128]{2,1,0:T(8,128)(2,1)S(1)}, bf16[2,528,128]{2,1,0:T(8,128)(2,1)S(1)}, u32[]{:S(2)}, u32[]{:S(2)}) collective-permute-start(bf16[2,528,128]{2,1,0:T(8,128)(2,1)S(1)} %get-tuple-element.39), channel_id=1, source_target_pairs={{0,2},{1,3},{2,0},{3,1},{4,6},{5,7},{6,4},{7,5},{8,10},{9,11},{10,... | collective-permute-start | bytes 811016 | tf_op jit(solution)/shard_map/ppermute | solution.py:286
  23.5 7.1 %collective-permute-start.5 = (bf16[4,4,16,256]{3,2,1,0:T(8,128)(2,1)S(1)}, bf16[4,4,16,256]{3,2,1,0:T(8,128)(2,1)S(1)}, u32[]{:S(2)}, u32[]{:S(2)}) collective-permute-start(bf16[4,4,16,256]{3,2,1,0:T(8,128)(2,1)S(1)} %pad_maximum_fusion.refs_0_), channel_id=1, source_target_pairs={{0,12},{1,13},{2,14},{3,15},{4,8},{5,9},{6,10},{7,11},{8,4},{9,5},... | collective-permute-start | bytes 393224 | tf_op jit(solution)/shard_map/ppermute | solution.py:286
  30.5 5.6 %collective-permute-start.12 = (bf16[1,528,128]{2,1,0:T(8,128)(2,1)S(1)}, bf16[1,528,128]{2,1,0:T(8,128)(2,1)S(1)}, u32[]{:S(2)}, u32[]{:S(2)}) collective-permute-start(bf16[1,528,128]{2,1,0:T(8,128)(2,1)S(1)} %get-tuple-element.41), channel_id=1, source_target_pairs={{0,2},{1,3},{2,0},{3,1},{4,6},{5,7},{6,4},{7,5},{8,10},{9,11},{10,... | collective-permute-start | bytes 405512 | tf_op jit(solution)/shard_map/ppermute | solution.py:286
  32.1 6.9 %collective-permute-start.13 = (bf16[1,528,128]{2,1,0:T(8,128)(2,1)S(1)}, bf16[1,528,128]{2,1,0:T(8,128)(2,1)S(1)}, u32[]{:S(2)}, u32[]{:S(2)}) collective-permute-start(bf16[1,528,128]{2,1,0:T(8,128)(2,1)S(1)} %get-tuple-element.42), channel_id=1, source_target_pairs={{0,3},{1,2},{2,1},{3,0},{4,7},{5,6},{6,5},{7,4},{8,11},{9,10},{10,... | collective-permute-start | bytes 405512 | tf_op jit(solution)/shard_map/ppermute | solution.py:286
  32.1 9.6 %collective-permute-start.7 = (bf16[1,528,128]{2,1,0:T(8,128)(2,1)S(1)}, bf16[1,528,128]{2,1,0:T(8,128)(2,1)S(1)}, u32[]{:S(2)}, u32[]{:S(2)}) collective-permute-start(bf16[1,528,128]{2,1,0:T(8,128)(2,1)S(1)} %get-tuple-element.37), channel_id=1, source_target_pairs={{0,2},{1,3},{2,0},{3,1},{4,6},{5,7},{6,4},{7,5},{8,10},{9,11},{10,... | collective-permute-start | bytes 405512 | tf_op jit(solution)/shard_map/ppermute | solution.py:286
  33.3 11.2 %collective-permute-start.8 = (bf16[1,528,128]{2,1,0:T(8,128)(2,1)S(1)}, bf16[1,528,128]{2,1,0:T(8,128)(2,1)S(1)}, u32[]{:S(2)}, u32[]{:S(2)}) collective-permute-start(bf16[1,528,128]{2,1,0:T(8,128)(2,1)S(1)} %get-tuple-element.38), channel_id=1, source_target_pairs={{0,3},{1,2},{2,1},{3,0},{4,7},{5,6},{6,5},{7,4},{8,11},{9,10},{10,... | collective-permute-start | bytes 405512 | tf_op jit(solution)/shard_map/ppermute | solution.py:286
  36.1 9.7 %collective-permute-start.15 = (bf16[272,256]{1,0:T(8,128)(2,1)S(1)}, bf16[272,256]{1,0:T(8,128)(2,1)S(1)}, u32[]{:S(2)}, u32[]{:S(2)}) collective-permute-start(bf16[272,256]{1,0:T(8,128)(2,1)S(1)} %shard_map.67), channel_id=1, source_target_pairs={{0,12},{1,13},{2,14},{3,15},{4,8},{5,9},{6,10},{7,11},{8,4},{9,5},... | collective-permute-start | bytes 417800 | tf_op jit(solution)/shard_map/ppermute | solution.py:286
  40.2 10.8 %collective-permute-start.14 = (bf16[272,256]{1,0:T(8,128)(2,1)S(1)}, bf16[272,256]{1,0:T(8,128)(2,1)S(1)}, u32[]{:S(2)}, u32[]{:S(2)}) collective-permute-start(bf16[272,256]{1,0:T(8,128)(2,1)S(1)} %shard_map.66), channel_id=1, source_target_pairs={{0,8},{1,9},{2,10},{3,11},{4,12},{5,13},{6,14},{7,15},{8,0},{9,1},... | collective-permute-start | bytes 417800 | tf_op jit(solution)/shard_map/ppermute | solution.py:286
  41.8 9.3 %collective-permute-start.11 = (bf16[272,256]{1,0:T(8,128)(2,1)S(1)}, bf16[272,256]{1,0:T(8,128)(2,1)S(1)}, u32[]{:S(2)}, u32[]{:S(2)}) collective-permute-start(bf16[272,256]{1,0:T(8,128)(2,1)S(1)} %shard_map.65), channel_id=1, source_target_pairs={{0,4},{1,5},{2,6},{3,7},{4,0},{5,1},{6,2},{7,3},{8,12},{9,13},{10,... | collective-permute-start | bytes 417800 | tf_op jit(solution)/shard_map/ppermute | solution.py:286
  53.9 7.8 %collective-permute-start.24 = (bf16[32,2688]{1,0:T(8,128)(2,1)S(1)}, bf16[32,2688]{1,0:T(8,128)(2,1)S(1)}, u32[]{:S(2)}, u32[]{:S(2)}) collective-permute-start(bf16[32,2688]{1,0:T(8,128)(2,1)S(1)} %get-tuple-element.52), channel_id=1, source_target_pairs={{0,2},{1,3},{2,0},{3,1},{4,6},{5,7},{6,4},{7,5},{8,10},{9,11},{10,... | collective-permute-start | bytes 516104 | tf_op jit(solution)/shard_map/ppermute | solution.py:286
  56.4 8.0 %collective-permute-start.26 = (bf16[32,2048]{1,0:T(8,128)(2,1)S(1)}, bf16[32,2048]{1,0:T(8,128)(2,1)S(1)}, u32[]{:S(2)}, u32[]{:S(2)}) collective-permute-start(bf16[32,2048]{1,0:T(8,128)(2,1)S(1)} %get-tuple-element.54), channel_id=1, source_target_pairs={{0,2},{1,3},{2,0},{3,1},{4,6},{5,7},{6,4},{7,5},{8,10},{9,11},{10,... | collective-permute-start | bytes 393224 | tf_op jit(solution)/shard_map/ppermute | solution.py:286
  56.5 10.8 %collective-permute-start.22 = (bf16[32,2048]{1,0:T(8,128)(2,1)S(1)}, bf16[32,2048]{1,0:T(8,128)(2,1)S(1)}, u32[]{:S(2)}, u32[]{:S(2)}) collective-permute-start(bf16[32,2048]{1,0:T(8,128)(2,1)S(1)} %get-tuple-element.50), channel_id=1, source_target_pairs={{0,2},{1,3},{2,0},{3,1},{4,6},{5,7},{6,4},{7,5},{8,10},{9,11},{10,... | collective-permute-start | bytes 393224 | tf_op jit(solution)/shard_map/ppermute | solution.py:286
  58.5 11.0 %collective-permute-start.18 = (bf16[64,640]{1,0:T(8,128)(2,1)S(1)}, bf16[64,640]{1,0:T(8,128)(2,1)S(1)}, u32[]{:S(2)}, u32[]{:S(2)}) collective-permute-start(bf16[64,640]{1,0:T(8,128)(2,1)S(1)} %get-tuple-element.43), channel_id=1, source_target_pairs={{0,12},{1,13},{2,14},{3,15},{4,8},{5,9},{6,10},{7,11},{8,4},{9,5},... | collective-permute-start | bytes 245768 | tf_op jit(solution)/shard_map/ppermute | solution.py:286
  60.0 25.5 %collective-permute-start.21 = (bf16[32,2688]{1,0:T(8,128)(2,1)S(1)}, bf16[32,2688]{1,0:T(8,128)(2,1)S(1)}, u32[]{:S(2)}, u32[]{:S(2)}) collective-permute-start(bf16[32,2688]{1,0:T(8,128)(2,1)S(1)} %get-tuple-element.48), channel_id=1, source_target_pairs={{0,2},{1,3},{2,0},{3,1},{4,6},{5,7},{6,4},{7,5},{8,10},{9,11},{10,... | collective-permute-start | bytes 516104 | tf_op jit(solution)/shard_map/ppermute | solution.py:286
  61.7 23.8 %collective-permute-start.25 = (bf16[32,2688]{1,0:T(8,128)(2,1)S(1)}, bf16[32,2688]{1,0:T(8,128)(2,1)S(1)}, u32[]{:S(2)}, u32[]{:S(2)}) collective-permute-start(bf16[32,2688]{1,0:T(8,128)(2,1)S(1)} %shard_map.73), channel_id=1, source_target_pairs={{0,4},{1,5},{2,6},{3,7},{4,0},{5,1},{6,2},{7,3},{8,12},{9,13},{10,... | collective-permute-start | bytes 516104 | tf_op jit(solution)/shard_map/ppermute | solution.py:286
  64.5 21.0 %collective-permute-start.27 = (bf16[32,2048]{1,0:T(8,128)(2,1)S(1)}, bf16[32,2048]{1,0:T(8,128)(2,1)S(1)}, u32[]{:S(2)}, u32[]{:S(2)}) collective-permute-start(bf16[32,2048]{1,0:T(8,128)(2,1)S(1)} %shard_map.74), channel_id=1, source_target_pairs={{0,8},{1,9},{2,10},{3,11},{4,12},{5,13},{6,14},{7,15},{8,0},{9,1},... | collective-permute-start | bytes 393224 | tf_op jit(solution)/shard_map/ppermute | solution.py:286
  67.3 18.2 %collective-permute-start.23 = (bf16[32,2048]{1,0:T(8,128)(2,1)S(1)}, bf16[32,2048]{1,0:T(8,128)(2,1)S(1)}, u32[]{:S(2)}, u32[]{:S(2)}) collective-permute-start(bf16[32,2048]{1,0:T(8,128)(2,1)S(1)} %shard_map.72), channel_id=1, source_target_pairs={{0,12},{1,13},{2,14},{3,15},{4,8},{5,9},{6,10},{7,11},{8,4},{9,5},... | collective-permute-start | bytes 393224 | tf_op jit(solution)/shard_map/ppermute | solution.py:286
  69.5 11.9 %collective-permute-start.19 = (bf16[64,640]{1,0:T(8,128)(2,1)S(1)}, bf16[64,640]{1,0:T(8,128)(2,1)S(1)}, u32[]{:S(2)}, u32[]{:S(2)}) collective-permute-start(bf16[64,640]{1,0:T(8,128)(2,1)S(1)} %get-tuple-element.44), channel_id=1, source_target_pairs={{0,8},{1,9},{2,10},{3,11},{4,12},{5,13},{6,14},{7,15},{8,0},{9,1},... | collective-permute-start | bytes 245768 | tf_op jit(solution)/shard_map/ppermute | solution.py:286
  (7 other events, 28.1 us)

commit v9 on v8

--- a/solution.py
+++ b/solution.py
@@ -65,7 +65,7 @@
     ]
     for load in loads:
         load.start()
-    live = jnp.full((16, HEAD_SIZE), live_ref[0], jnp.int32).astype(f32).astype(bf16)
+    live = jnp.full((8, HEAD_SIZE), live_ref[0], jnp.int32).astype(f32).astype(bf16)
     loads[0].wait()
     for k, out in enumerate(q_outs):
         for zz in range(outer):
@@ -79,7 +79,7 @@
             col = pl.multiple_of((head // copies) * HEAD_SIZE, HEAD_SIZE)
             out[i, 0:keys, :] = k_ref[:, pl.ds(col, HEAD_SIZE)]
             out[i, keys:2 * keys, :] = v_ref[:, pl.ds(col, HEAD_SIZE)]
-            out[i, 2 * keys:2 * keys + 16, :] = live
+            out[i, 2 * keys:2 * keys + 8, :] = live
 
 
 def split_weight_kernel(w_ref, out_ref):
@@ -146,20 +146,20 @@
                 stats = jnp.where(column == p * heads + h, piece, stats)
         turned = stats.T
         pieces = rows_all // width
-        per = 16 // pieces
+        per = 8 // pieces
         block = [turned[0:per, j * width:(j + 1) * width] for j in range(pieces)]
         block = block[0] if pieces == 1 else jnp.concatenate(block, axis=0)
-        outs[i][rows_all:rows_all + 16, :] = block.astype(bf16)
+        outs[i][rows_all:rows_all + 8, :] = block.astype(bf16)
 
 
 def merge_kernel(*refs, sources, rows_all, heads, width):
     parts = refs[:sources]
     out, turn_ref = refs[sources:]
     pieces = rows_all // width
-    per = 16 // pieces
+    per = 8 // pieces
     logs = []
     for part in parts:
-        block = part[rows_all:rows_all + 16, :].astype(f32)
+        block = part[rows_all:rows_all + 8, :].astype(f32)
         block = [block[j * per:(j + 1) * per] for j in range(pieces)]
         block = block[0] if pieces == 1 else jnp.concatenate(block, axis=1)
         logs.append(block[0:heads] + (block[heads:2 * heads] + block[2 * heads:3 * heads]))
@@ -293,7 +293,7 @@
         for x in (query_block, cache_keys, stored_values)
     ]
     outs = [shape((outer, rows, width), bf16)] * INNER
-    outs += [shape((len(p), 2 * keys + 16, HEAD_SIZE), bf16) for k, p in groups]
+    outs += [shape((len(p), 2 * keys + 8, HEAD_SIZE), bf16) for k, p in groups]
     split = pl.pallas_call(
         functools.partial(split_kernel, outer=outer, width=width, groups=groups, copies=copies),
         out_shape=tuple(outs),
@@ -330,7 +330,7 @@
                 offsets=[kk], rows_all=rows_all, keys=keys, heads=heads, width=width,
             ),
             [first_position, *ys, kv_out[0], kv_pair, kv_far[i][2], kv_far[i][3]],
-            [shape((rows_all + 16, width), bf16)],
+            [shape((rows_all + 8, width), bf16)],
             scratch=[pltpu.VMEM((rows_all, INNER * keys), f32), pltpu.VMEM((rows_all, width), f32)],
             scalars=1, flops=4 * rows_all * INNER * keys * width, limit=16,
         )

time: 87.9 us -> 87.6 us (level)
  no operation moved by 1% of the time
where the time goes in v9:
time: 87.6 us; the launch traced here: 87.4 us
  waiting for transfers between devices  44.1 us (50%)
  starting transfers between devices  30.5 us (35%)
  Pallas kernels  9.56 us (11%)
  local copies, waits for them, and re-layouts  1.78 us (2%)
  between operations  1.45 us (2%)
    ppermute x29, waiting for transfers between devices, swap(): return lax.ppermute(x, 'seq', [(i, i ^ k) for i in range(devices)])  44.1 us
    ppermute x29, starting transfers between devices, swap(): return lax.ppermute(x, 'seq', [(i, i ^ k) for i in range(devices)])  30.5 us
    pallas_call x13, Pallas kernels, call(): pl.pallas_call(kernel, out_shape=tuple(outs), in_specs=in_specs, out_spec...  7.36 us
    pallas_call x1, Pallas kernels, layer(): pl.pallas_call(functools.partial(split_kernel, outer=outer, width=width,...  2.21 us
    unnamed x4, local copies, waits for them, and re-layouts  1.78 us
  transfers between devices with their start and end apart: 29, of which 16 were waited for; matrix products, arithmetic and copies ran while one was open for 0% of the time, Pallas kernels for 9%

profile of v9, /device:TPU:0, one launch (start us, length us, event | category | flops | bytes accessed | tf_op | source)
XLA Modules:
  0.0 87.4 jit_solution(5220121869561098913)
XLA Ops:
  0.0 1.8 %copy-done = bf16[256,5376]{1,0:T(8,128)(2,1)S(1)} copy-done((bf16[256,5376]{1,0:T(8,128)(2,1)S(1)}, bf16[256,5376]{1,0:T(8,128)(2,1)}, u32[]{:S(2)}) %copy-start) | copy-done | bytes 2752536
  3.1 2.2 %split.1 = (bf16[4,16,256]{2,1,0:T(8,128)(2,1)S(1)}, bf16[4,16,256]{2,1,0:T(8,128)(2,1)S(1)}, bf16[4,16,256]{2,1,0:T(8,128)(2,1)S(1)}, bf16[4,16,256]{2,1,0:T(8,...) custom-call(s32[1]{0:T(128)S(6)} %copy.7.live_ref, ...), custom_call_target="tpu_custom_call" | custom-call | tf_op jit(solution)/shard_map/split/pallas_call | solution.py:297
  5.4 3.0 %collective-permute-start.1 = (bf16[4,16,256]{2,1,0:T(8,128)(2,1)S(1)}, bf16[4,16,256]{2,1,0:T(8,128)(2,1)S(1)}, u32[]{:S(2)}, u32[]{:S(2)}) collective-permute-start(bf16[4,16,256]{2,1,0:T(8,128)(2,1)S(1)} %get-tuple-element.33), channel_id=1, source_target_pairs={{0,2},{1,3},{2,0},{3,1},{4,6},{5,7},{6,4},{7,5},{8,10},{9,11},{10,... | collective-permute-start | bytes 98312 | tf_op jit(solution)/shard_map/ppermute | solution.py:286
  8.5 1.8 %collective-permute-done.1 = bf16[4,16,256]{2,1,0:T(8,128)(2,1)S(1)} collective-permute-done((bf16[4,16,256]{2,1,0:T(8,128)(2,1)S(1)}, bf16[4,16,256]{2,1,0:T(8,128)(2,1)S(1)}, u32[]{:S(2)}, u32[]{:S(2)}) %collective-permute-start.1) | collective-permute-done | bytes 32800 | tf_op jit(solution)/shard_map/ppermute | solution.py:286
  10.3 1.8 %collective-permute-done.2 = bf16[4,16,256]{2,1,0:T(8,128)(2,1)S(1)} collective-permute-done((bf16[4,16,256]{2,1,0:T(8,128)(2,1)S(1)}, bf16[4,16,256]{2,1,0:T(8,128)(2,1)S(1)}, u32[]{:S(2)}, u32[]{:S(2)}) %collective-permute-start.2) | collective-permute-done | bytes 32800 | tf_op jit(solution)/shard_map/ppermute | solution.py:286
  12.1 1.6 %collective-permute-start.3 = (bf16[4,4,16,256]{3,2,1,0:T(8,128)(2,1)S(1)}, bf16[4,4,16,256]{3,2,1,0:T(8,128)(2,1)S(1)}, u32[]{:S(2)}, u32[]{:S(2)}) collective-permute-start(bf16[4,4,16,256]{3,2,1,0:T(8,128)(2,1)S(1)} %pad_maximum_fusion.refs_0_), channel_id=1, source_target_pairs={{0,4},{1,5},{2,6},{3,7},{4,0},{5,1},{6,2},{7,3},{8,12},{9,13},{10,... | collective-permute-start | bytes 393224 | tf_op jit(solution)/shard_map/ppermute | solution.py:286
  13.7 2.6 %collective-permute-start.4 = (bf16[4,4,16,256]{3,2,1,0:T(8,128)(2,1)S(1)}, bf16[4,4,16,256]{3,2,1,0:T(8,128)(2,1)S(1)}, u32[]{:S(2)}, u32[]{:S(2)}) collective-permute-start(bf16[4,4,16,256]{3,2,1,0:T(8,128)(2,1)S(1)} %pad_maximum_fusion.refs_0_), channel_id=1, source_target_pairs={{0,8},{1,9},{2,10},{3,11},{4,12},{5,13},{6,14},{7,15},{8,0},{9,1},... | collective-permute-start | bytes 393224 | tf_op jit(solution)/shard_map/ppermute | solution.py:286
  18.1 5.4 %collective-permute-done.4.refs_2_ = bf16[4,4,16,256]{3,2,1,0:T(8,128)(2,1)S(1)} collective-permute-done((bf16[4,4,16,256]{3,2,1,0:T(8,128)(2,1)S(1)}, bf16[4,4,16,256]{3,2,1,0:T(8,128)(2,1)S(1)}, u32[]{:S(2)}, u32[]{:S(2)}) %collective-permute-start.4) | collective-permute-done | bytes 131104 | tf_op jit(solution)/shard_map/ppermute | solution.py:286
  23.5 2.5 %collective-permute-start.5 = (bf16[4,4,16,256]{3,2,1,0:T(8,128)(2,1)S(1)}, bf16[4,4,16,256]{3,2,1,0:T(8,128)(2,1)S(1)}, u32[]{:S(2)}, u32[]{:S(2)}) collective-permute-start(bf16[4,4,16,256]{3,2,1,0:T(8,128)(2,1)S(1)} %pad_maximum_fusion.refs_0_), channel_id=1, source_target_pairs={{0,12},{1,13},{2,14},{3,15},{4,8},{5,9},{6,10},{7,11},{8,4},{9,5},... | collective-permute-start | bytes 393224 | tf_op jit(solution)/shard_map/ppermute | solution.py:286
  26.0 4.5 %collective-permute-done.5.refs_3_ = bf16[4,4,16,256]{3,2,1,0:T(8,128)(2,1)S(1)} collective-permute-done((bf16[4,4,16,256]{3,2,1,0:T(8,128)(2,1)S(1)}, bf16[4,4,16,256]{3,2,1,0:T(8,128)(2,1)S(1)}, u32[]{:S(2)}, u32[]{:S(2)}) %collective-permute-start.5) | collective-permute-done | bytes 131104 | tf_op jit(solution)/shard_map/ppermute | solution.py:286
  30.5 1.6 %collective-permute-start.12 = (bf16[1,520,128]{2,1,0:T(8,128)(2,1)S(1)}, bf16[1,520,128]{2,1,0:T(8,128)(2,1)S(1)}, u32[]{:S(2)}, u32[]{:S(2)}) collective-permute-start(bf16[1,520,128]{2,1,0:T(8,128)(2,1)S(1)} %get-tuple-element.41), channel_id=1, source_target_pairs={{0,2},{1,3},{2,0},{3,1},{4,6},{5,7},{6,4},{7,5},{8,10},{9,11},{10,... | collective-permute-start | bytes 399368 | tf_op jit(solution)/shard_map/ppermute | solution.py:286
  33.3 1.5 %collective-permute-start.8 = (bf16[1,520,128]{2,1,0:T(8,128)(2,1)S(1)}, bf16[1,520,128]{2,1,0:T(8,128)(2,1)S(1)}, u32[]{:S(2)}, u32[]{:S(2)}) collective-permute-start(bf16[1,520,128]{2,1,0:T(8,128)(2,1)S(1)} %get-tuple-element.38), channel_id=1, source_target_pairs={{0,3},{1,2},{2,1},{3,0},{4,7},{5,6},{6,5},{7,4},{8,11},{9,10},{10,... | collective-permute-start | bytes 399368 | tf_op jit(solution)/shard_map/ppermute | solution.py:286
  36.1 2.4 %collective-permute-start.15 = (bf16[264,256]{1,0:T(8,128)(2,1)S(1)}, bf16[264,256]{1,0:T(8,128)(2,1)S(1)}, u32[]{:S(2)}, u32[]{:S(2)}) collective-permute-start(bf16[264,256]{1,0:T(8,128)(2,1)S(1)} %shard_map.67), channel_id=1, source_target_pairs={{0,12},{1,13},{2,14},{3,15},{4,8},{5,9},{6,10},{7,11},{8,4},{9,5},... | collective-permute-start | bytes 405512 | tf_op jit(solution)/shard_map/ppermute | solution.py:286
  41.7 2.8 %collective-permute-start.11 = (bf16[264,256]{1,0:T(8,128)(2,1)S(1)}, bf16[264,256]{1,0:T(8,128)(2,1)S(1)}, u32[]{:S(2)}, u32[]{:S(2)}) collective-permute-start(bf16[264,256]{1,0:T(8,128)(2,1)S(1)} %shard_map.65), channel_id=1, source_target_pairs={{0,4},{1,5},{2,6},{3,7},{4,0},{5,1},{6,2},{7,3},{8,12},{9,13},{10,... | collective-permute-start | bytes 405512 | tf_op jit(solution)/shard_map/ppermute | solution.py:286
  45.7 5.0 %collective-permute-done.14.refs_2_ = bf16[264,256]{1,0:T(8,128)(2,1)S(1)} collective-permute-done((bf16[264,256]{1,0:T(8,128)(2,1)S(1)}, bf16[264,256]{1,0:T(8,128)(2,1)S(1)}, u32[]{:S(2)}, u32[]{:S(2)}) %collective-permute-start.14) | collective-permute-done | bytes 135200 | tf_op jit(solution)/shard_map/ppermute | solution.py:286
  53.5 2.7 %collective-permute-start.24 = (bf16[32,2688]{1,0:T(8,128)(2,1)S(1)}, bf16[32,2688]{1,0:T(8,128)(2,1)S(1)}, u32[]{:S(2)}, u32[]{:S(2)}) collective-permute-start(bf16[32,2688]{1,0:T(8,128)(2,1)S(1)} %get-tuple-element.52), channel_id=1, source_target_pairs={{0,2},{1,3},{2,0},{3,1},{4,6},{5,7},{6,4},{7,5},{8,10},{9,11},{10,... | collective-permute-start | bytes 516104 | tf_op jit(solution)/shard_map/ppermute | solution.py:286
  56.3 1.9 %collective-permute-start.22 = (bf16[32,2048]{1,0:T(8,128)(2,1)S(1)}, bf16[32,2048]{1,0:T(8,128)(2,1)S(1)}, u32[]{:S(2)}, u32[]{:S(2)}) collective-permute-start(bf16[32,2048]{1,0:T(8,128)(2,1)S(1)} %get-tuple-element.50), channel_id=1, source_target_pairs={{0,2},{1,3},{2,0},{3,1},{4,6},{5,7},{6,4},{7,5},{8,10},{9,11},{10,... | collective-permute-start | bytes 393224 | tf_op jit(solution)/shard_map/ppermute | solution.py:286
  58.2 1.5 %collective-permute-start.18 = (bf16[64,640]{1,0:T(8,128)(2,1)S(1)}, bf16[64,640]{1,0:T(8,128)(2,1)S(1)}, u32[]{:S(2)}, u32[]{:S(2)}) collective-permute-start(bf16[64,640]{1,0:T(8,128)(2,1)S(1)} %get-tuple-element.43), channel_id=1, source_target_pairs={{0,12},{1,13},{2,14},{3,15},{4,8},{5,9},{6,10},{7,11},{8,4},{9,5},... | collective-permute-start | bytes 245768 | tf_op jit(solution)/shard_map/ppermute | solution.py:286
  61.5 2.7 %collective-permute-done.26.got_ref = bf16[32,2048]{1,0:T(8,128)(2,1)S(1)} collective-permute-done((bf16[32,2048]{1,0:T(8,128)(2,1)S(1)}, bf16[32,2048]{1,0:T(8,128)(2,1)S(1)}, u32[]{:S(2)}, u32[]{:S(2)}) %collective-permute-start.26) | collective-permute-done | bytes 131104 | tf_op jit(solution)/shard_map/ppermute | solution.py:286
  64.4 2.7 %collective-permute-done.22.got_ref = bf16[32,2048]{1,0:T(8,128)(2,1)S(1)} collective-permute-done((bf16[32,2048]{1,0:T(8,128)(2,1)S(1)}, bf16[32,2048]{1,0:T(8,128)(2,1)S(1)}, u32[]{:S(2)}, u32[]{:S(2)}) %collective-permute-start.22) | collective-permute-done | bytes 131104 | tf_op jit(solution)/shard_map/ppermute | solution.py:286
  67.1 2.0 %collective-permute-start.23 = (bf16[32,2048]{1,0:T(8,128)(2,1)S(1)}, bf16[32,2048]{1,0:T(8,128)(2,1)S(1)}, u32[]{:S(2)}, u32[]{:S(2)}) collective-permute-start(bf16[32,2048]{1,0:T(8,128)(2,1)S(1)} %shard_map.72), channel_id=1, source_target_pairs={{0,12},{1,13},{2,14},{3,15},{4,8},{5,9},{6,10},{7,11},{8,4},{9,5},... | collective-permute-start | bytes 393224 | tf_op jit(solution)/shard_map/ppermute | solution.py:286
  69.1 12.0 %collective-permute-done.19.refs_1_ = bf16[64,640]{1,0:T(8,128)(2,1)S(1)} collective-permute-done((bf16[64,640]{1,0:T(8,128)(2,1)S(1)}, bf16[64,640]{1,0:T(8,128)(2,1)S(1)}, u32[]{:S(2)}, u32[]{:S(2)}) %collective-permute-start.19) | collective-permute-done | bytes 81952 | tf_op jit(solution)/shard_map/ppermute | solution.py:286
  81.1 1.5 %collective-permute-start.20 = (bf16[32,640]{1,0:T(8,128)(2,1)S(1)}, bf16[32,640]{1,0:T(8,128)(2,1)S(1)}, u32[]{:S(2)}, u32[]{:S(2)}) collective-permute-start(bf16[32,640]{1,0:T(8,128)(2,1)S(1)} %get-tuple-element.46), channel_id=1, source_target_pairs={{0,2},{1,3},{2,0},{3,1},{4,6},{5,7},{6,4},{7,5},{8,10},{9,11},{10,... | collective-permute-start | bytes 122888 | tf_op jit(solution)/shard_map/ppermute | solution.py:286
  82.6 2.5 %collective-permute-done.20.early_got_ref = bf16[32,640]{1,0:T(8,128)(2,1)S(1)} collective-permute-done((bf16[32,640]{1,0:T(8,128)(2,1)S(1)}, bf16[32,640]{1,0:T(8,128)(2,1)S(1)}, u32[]{:S(2)}, u32[]{:S(2)}) %collective-permute-start.20) | collective-permute-done | bytes 40992 | tf_op jit(solution)/shard_map/ppermute | solution.py:286
  (53 shorter events, 15.9 us)
Async XLA Ops:
  1.9 50.7 %collective-permute-start.17 = (bf16[256,2688]{1,0:T(8,128)(2,1)S(1)}, bf16[256,2688]{1,0:T(8,128)(2,1)S(1)}, u32[]{:S(2)}, u32[]{:S(2)}) collective-permute-start(bf16[256,2688]{1,0:T(8,128)(2,1)S(1)} %shard_map.69), channel_id=1, source_target_pairs={{0,1},{1,0},{2,3},{3,2},{4,5},{5,4},{6,7},{7,6},{8,9},{9,8},{10,11... | collective-permute-start | bytes 4128776 | tf_op jit(solution)/shard_map/ppermute | solution.py:286
  5.4 4.9 %collective-permute-start.1 = (bf16[4,16,256]{2,1,0:T(8,128)(2,1)S(1)}, bf16[4,16,256]{2,1,0:T(8,128)(2,1)S(1)}, u32[]{:S(2)}, u32[]{:S(2)}) collective-permute-start(bf16[4,16,256]{2,1,0:T(8,128)(2,1)S(1)} %get-tuple-element.33), channel_id=1, source_target_pairs={{0,2},{1,3},{2,0},{3,1},{4,6},{5,7},{6,4},{7,5},{8,10},{9,11},{10,... | collective-permute-start | bytes 98312 | tf_op jit(solution)/shard_map/ppermute | solution.py:286
  8.4 24.9 %collective-permute-start.6 = (bf16[4,520,128]{2,1,0:T(8,128)(2,1)S(1)}, bf16[4,520,128]{2,1,0:T(8,128)(2,1)S(1)}, u32[]{:S(2)}, u32[]{:S(2)}) collective-permute-start(bf16[4,520,128]{2,1,0:T(8,128)(2,1)S(1)} %get-tuple-element.36), channel_id=1, source_target_pairs={{0,1},{1,0},{2,3},{3,2},{4,5},{5,4},{6,7},{7,6},{8,9},{9,8},{10,11... | collective-permute-start | bytes 1597448 | tf_op jit(solution)/shard_map/ppermute | solution.py:286
  12.1 5.6 %collective-permute-start.3 = (bf16[4,4,16,256]{3,2,1,0:T(8,128)(2,1)S(1)}, bf16[4,4,16,256]{3,2,1,0:T(8,128)(2,1)S(1)}, u32[]{:S(2)}, u32[]{:S(2)}) collective-permute-start(bf16[4,4,16,256]{3,2,1,0:T(8,128)(2,1)S(1)} %pad_maximum_fusion.refs_0_), channel_id=1, source_target_pairs={{0,4},{1,5},{2,6},{3,7},{4,0},{5,1},{6,2},{7,3},{8,12},{9,13},{10,... | collective-permute-start | bytes 393224 | tf_op jit(solution)/shard_map/ppermute | solution.py:286
  13.7 18.4 %collective-permute-start.10 = (bf16[2,520,128]{2,1,0:T(8,128)(2,1)S(1)}, bf16[2,520,128]{2,1,0:T(8,128)(2,1)S(1)}, u32[]{:S(2)}, u32[]{:S(2)}) collective-permute-start(bf16[2,520,128]{2,1,0:T(8,128)(2,1)S(1)} %get-tuple-element.40), channel_id=1, source_target_pairs={{0,3},{1,2},{2,1},{3,0},{4,7},{5,6},{6,5},{7,4},{8,11},{9,10},{10,... | collective-permute-start | bytes 798728 | tf_op jit(solution)/shard_map/ppermute | solution.py:286
  13.7 9.7 %collective-permute-start.4 = (bf16[4,4,16,256]{3,2,1,0:T(8,128)(2,1)S(1)}, bf16[4,4,16,256]{3,2,1,0:T(8,128)(2,1)S(1)}, u32[]{:S(2)}, u32[]{:S(2)}) collective-permute-start(bf16[4,4,16,256]{3,2,1,0:T(8,128)(2,1)S(1)} %pad_maximum_fusion.refs_0_), channel_id=1, source_target_pairs={{0,8},{1,9},{2,10},{3,11},{4,12},{5,13},{6,14},{7,15},{8,0},{9,1},... | collective-permute-start | bytes 393224 | tf_op jit(solution)/shard_map/ppermute | solution.py:286
  17.6 14.5 %collective-permute-start.9 = (bf16[2,520,128]{2,1,0:T(8,128)(2,1)S(1)}, bf16[2,520,128]{2,1,0:T(8,128)(2,1)S(1)}, u32[]{:S(2)}, u32[]{:S(2)}) collective-permute-start(bf16[2,520,128]{2,1,0:T(8,128)(2,1)S(1)} %get-tuple-element.39), channel_id=1, source_target_pairs={{0,2},{1,3},{2,0},{3,1},{4,6},{5,7},{6,4},{7,5},{8,10},{9,11},{10,... | collective-permute-start | bytes 798728 | tf_op jit(solution)/shard_map/ppermute | solution.py:286
  23.5 7.1 %collective-permute-start.5 = (bf16[4,4,16,256]{3,2,1,0:T(8,128)(2,1)S(1)}, bf16[4,4,16,256]{3,2,1,0:T(8,128)(2,1)S(1)}, u32[]{:S(2)}, u32[]{:S(2)}) collective-permute-start(bf16[4,4,16,256]{3,2,1,0:T(8,128)(2,1)S(1)} %pad_maximum_fusion.refs_0_), channel_id=1, source_target_pairs={{0,12},{1,13},{2,14},{3,15},{4,8},{5,9},{6,10},{7,11},{8,4},{9,5},... | collective-permute-start | bytes 393224 | tf_op jit(solution)/shard_map/ppermute | solution.py:286
  30.5 5.5 %collective-permute-start.12 = (bf16[1,520,128]{2,1,0:T(8,128)(2,1)S(1)}, bf16[1,520,128]{2,1,0:T(8,128)(2,1)S(1)}, u32[]{:S(2)}, u32[]{:S(2)}) collective-permute-start(bf16[1,520,128]{2,1,0:T(8,128)(2,1)S(1)} %get-tuple-element.41), channel_id=1, source_target_pairs={{0,2},{1,3},{2,0},{3,1},{4,6},{5,7},{6,4},{7,5},{8,10},{9,11},{10,... | collective-permute-start | bytes 399368 | tf_op jit(solution)/shard_map/ppermute | solution.py:286
  32.1 6.8 %collective-permute-start.13 = (bf16[1,520,128]{2,1,0:T(8,128)(2,1)S(1)}, bf16[1,520,128]{2,1,0:T(8,128)(2,1)S(1)}, u32[]{:S(2)}, u32[]{:S(2)}) collective-permute-start(bf16[1,520,128]{2,1,0:T(8,128)(2,1)S(1)} %get-tuple-element.42), channel_id=1, source_target_pairs={{0,3},{1,2},{2,1},{3,0},{4,7},{5,6},{6,5},{7,4},{8,11},{9,10},{10,... | collective-permute-start | bytes 399368 | tf_op jit(solution)/shard_map/ppermute | solution.py:286
  32.1 9.5 %collective-permute-start.7 = (bf16[1,520,128]{2,1,0:T(8,128)(2,1)S(1)}, bf16[1,520,128]{2,1,0:T(8,128)(2,1)S(1)}, u32[]{:S(2)}, u32[]{:S(2)}) collective-permute-start(bf16[1,520,128]{2,1,0:T(8,128)(2,1)S(1)} %get-tuple-element.37), channel_id=1, source_target_pairs={{0,2},{1,3},{2,0},{3,1},{4,6},{5,7},{6,4},{7,5},{8,10},{9,11},{10,... | collective-permute-start | bytes 399368 | tf_op jit(solution)/shard_map/ppermute | solution.py:286
  33.3 11.1 %collective-permute-start.8 = (bf16[1,520,128]{2,1,0:T(8,128)(2,1)S(1)}, bf16[1,520,128]{2,1,0:T(8,128)(2,1)S(1)}, u32[]{:S(2)}, u32[]{:S(2)}) collective-permute-start(bf16[1,520,128]{2,1,0:T(8,128)(2,1)S(1)} %get-tuple-element.38), channel_id=1, source_target_pairs={{0,3},{1,2},{2,1},{3,0},{4,7},{5,6},{6,5},{7,4},{8,11},{9,10},{10,... | collective-permute-start | bytes 399368 | tf_op jit(solution)/shard_map/ppermute | solution.py:286
  36.1 9.6 %collective-permute-start.15 = (bf16[264,256]{1,0:T(8,128)(2,1)S(1)}, bf16[264,256]{1,0:T(8,128)(2,1)S(1)}, u32[]{:S(2)}, u32[]{:S(2)}) collective-permute-start(bf16[264,256]{1,0:T(8,128)(2,1)S(1)} %shard_map.67), channel_id=1, source_target_pairs={{0,12},{1,13},{2,14},{3,15},{4,8},{5,9},{6,10},{7,11},{8,4},{9,5},... | collective-permute-start | bytes 405512 | tf_op jit(solution)/shard_map/ppermute | solution.py:286
  40.1 10.6 %collective-permute-start.14 = (bf16[264,256]{1,0:T(8,128)(2,1)S(1)}, bf16[264,256]{1,0:T(8,128)(2,1)S(1)}, u32[]{:S(2)}, u32[]{:S(2)}) collective-permute-start(bf16[264,256]{1,0:T(8,128)(2,1)S(1)} %shard_map.66), channel_id=1, source_target_pairs={{0,8},{1,9},{2,10},{3,11},{4,12},{5,13},{6,14},{7,15},{8,0},{9,1},... | collective-permute-start | bytes 405512 | tf_op jit(solution)/shard_map/ppermute | solution.py:286
  41.7 9.1 %collective-permute-start.11 = (bf16[264,256]{1,0:T(8,128)(2,1)S(1)}, bf16[264,256]{1,0:T(8,128)(2,1)S(1)}, u32[]{:S(2)}, u32[]{:S(2)}) collective-permute-start(bf16[264,256]{1,0:T(8,128)(2,1)S(1)} %shard_map.65), channel_id=1, source_target_pairs={{0,4},{1,5},{2,6},{3,7},{4,0},{5,1},{6,2},{7,3},{8,12},{9,13},{10,... | collective-permute-start | bytes 405512 | tf_op jit(solution)/shard_map/ppermute | solution.py:286
  53.5 7.9 %collective-permute-start.24 = (bf16[32,2688]{1,0:T(8,128)(2,1)S(1)}, bf16[32,2688]{1,0:T(8,128)(2,1)S(1)}, u32[]{:S(2)}, u32[]{:S(2)}) collective-permute-start(bf16[32,2688]{1,0:T(8,128)(2,1)S(1)} %get-tuple-element.52), channel_id=1, source_target_pairs={{0,2},{1,3},{2,0},{3,1},{4,6},{5,7},{6,4},{7,5},{8,10},{9,11},{10,... | collective-permute-start | bytes 516104 | tf_op jit(solution)/shard_map/ppermute | solution.py:286
  56.2 8.0 %collective-permute-start.26 = (bf16[32,2048]{1,0:T(8,128)(2,1)S(1)}, bf16[32,2048]{1,0:T(8,128)(2,1)S(1)}, u32[]{:S(2)}, u32[]{:S(2)}) collective-permute-start(bf16[32,2048]{1,0:T(8,128)(2,1)S(1)} %get-tuple-element.54), channel_id=1, source_target_pairs={{0,2},{1,3},{2,0},{3,1},{4,6},{5,7},{6,4},{7,5},{8,10},{9,11},{10,... | collective-permute-start | bytes 393224 | tf_op jit(solution)/shard_map/ppermute | solution.py:286
  56.3 10.8 %collective-permute-start.22 = (bf16[32,2048]{1,0:T(8,128)(2,1)S(1)}, bf16[32,2048]{1,0:T(8,128)(2,1)S(1)}, u32[]{:S(2)}, u32[]{:S(2)}) collective-permute-start(bf16[32,2048]{1,0:T(8,128)(2,1)S(1)} %get-tuple-element.50), channel_id=1, source_target_pairs={{0,2},{1,3},{2,0},{3,1},{4,6},{5,7},{6,4},{7,5},{8,10},{9,11},{10,... | collective-permute-start | bytes 393224 | tf_op jit(solution)/shard_map/ppermute | solution.py:286
  58.2 10.9 %collective-permute-start.18 = (bf16[64,640]{1,0:T(8,128)(2,1)S(1)}, bf16[64,640]{1,0:T(8,128)(2,1)S(1)}, u32[]{:S(2)}, u32[]{:S(2)}) collective-permute-start(bf16[64,640]{1,0:T(8,128)(2,1)S(1)} %get-tuple-element.43), channel_id=1, source_target_pairs={{0,12},{1,13},{2,14},{3,15},{4,8},{5,9},{6,10},{7,11},{8,4},{9,5},... | collective-permute-start | bytes 245768 | tf_op jit(solution)/shard_map/ppermute | solution.py:286
  59.7 25.5 %collective-permute-start.21 = (bf16[32,2688]{1,0:T(8,128)(2,1)S(1)}, bf16[32,2688]{1,0:T(8,128)(2,1)S(1)}, u32[]{:S(2)}, u32[]{:S(2)}) collective-permute-start(bf16[32,2688]{1,0:T(8,128)(2,1)S(1)} %get-tuple-element.48), channel_id=1, source_target_pairs={{0,2},{1,3},{2,0},{3,1},{4,6},{5,7},{6,4},{7,5},{8,10},{9,11},{10,... | collective-permute-start | bytes 516104 | tf_op jit(solution)/shard_map/ppermute | solution.py:286
  61.5 23.7 %collective-permute-start.25 = (bf16[32,2688]{1,0:T(8,128)(2,1)S(1)}, bf16[32,2688]{1,0:T(8,128)(2,1)S(1)}, u32[]{:S(2)}, u32[]{:S(2)}) collective-permute-start(bf16[32,2688]{1,0:T(8,128)(2,1)S(1)} %shard_map.73), channel_id=1, source_target_pairs={{0,4},{1,5},{2,6},{3,7},{4,0},{5,1},{6,2},{7,3},{8,12},{9,13},{10,... | collective-permute-start | bytes 516104 | tf_op jit(solution)/shard_map/ppermute | solution.py:286
  64.3 20.9 %collective-permute-start.27 = (bf16[32,2048]{1,0:T(8,128)(2,1)S(1)}, bf16[32,2048]{1,0:T(8,128)(2,1)S(1)}, u32[]{:S(2)}, u32[]{:S(2)}) collective-permute-start(bf16[32,2048]{1,0:T(8,128)(2,1)S(1)} %shard_map.74), channel_id=1, source_target_pairs={{0,8},{1,9},{2,10},{3,11},{4,12},{5,13},{6,14},{7,15},{8,0},{9,1},... | collective-permute-start | bytes 393224 | tf_op jit(solution)/shard_map/ppermute | solution.py:286
  67.1 18.1 %collective-permute-start.23 = (bf16[32,2048]{1,0:T(8,128)(2,1)S(1)}, bf16[32,2048]{1,0:T(8,128)(2,1)S(1)}, u32[]{:S(2)}, u32[]{:S(2)}) collective-permute-start(bf16[32,2048]{1,0:T(8,128)(2,1)S(1)} %shard_map.72), channel_id=1, source_target_pairs={{0,12},{1,13},{2,14},{3,15},{4,8},{5,9},{6,10},{7,11},{8,4},{9,5},... | collective-permute-start | bytes 393224 | tf_op jit(solution)/shard_map/ppermute | solution.py:286
  69.1 12.0 %collective-permute-start.19 = (bf16[64,640]{1,0:T(8,128)(2,1)S(1)}, bf16[64,640]{1,0:T(8,128)(2,1)S(1)}, u32[]{:S(2)}, u32[]{:S(2)}) collective-permute-start(bf16[64,640]{1,0:T(8,128)(2,1)S(1)} %get-tuple-element.44), channel_id=1, source_target_pairs={{0,8},{1,9},{2,10},{3,11},{4,12},{5,13},{6,14},{7,15},{8,0},{9,1},... | collective-permute-start | bytes 245768 | tf_op jit(solution)/shard_map/ppermute | solution.py:286
  (7 other events, 27.8 us)
